TPU v7x, 512 devices: a whole 4x4x16 slice. The times are simulated.
512 devices in a mesh: band: 128 (over y, z, core), pair: 4 (over x).
Axes of the slice: x: 4, y: 4, z: 16, core: 2. Of those that a mesh axis runs over, the one named last changes fastest.
Arguments:
- orbitals: bfloat16 [512, 262144], P(('band', 'pair')), may hold values from -64 to 64
- partners: int32 [512, 3], P(('band', 'pair')), may hold values from -1 to 511, as said below
Outputs:
- gradient: float32 [512, 262144], P(None, ('band', 'pair'))
Inputs may be any that keep to these rules, and one draw needn't show every extreme that they name: `partners`: slot k of orbital i holds either -1 or i XOR (4 * 2**k); j is listed by i exactly when i is listed by j.
All inputs are finite; a program needn't handle non-finite values.
Results may differ from a plain program's by a relative error of at most 0.0008.
The roundings to bfloat16 on the way count: a program that leaves them out, or rounds other values in their place, can miss the bound.
Values may be sent and summed in bfloat16 or wider, within the bound.
No kernel may reach another device: no remote copies, remote signals or barrier semaphores. Data moves between devices by JAX's collectives and lax.ppermute only.
A program may use at most 64 MiB of HBM per device.

v0:
```python
import math

import jax
import jax.numpy as jnp
from jax import lax
from jax.sharding import Mesh
from jax.sharding import PartitionSpec as P

NG = 64
PARTNERS = 3
NG3 = 262144
BAND = ("band_0", "band_1", "band_2")
BAND_PAIR = ("band_0", "band_1", "band_2", "pair")


screening = 0.05


def partner(value, axis, distance):
    mask = 2**distance
    pairs = [(source, source ^ mask) for source in range(lax.axis_size(axis))]
    return lax.ppermute(value, axis, pairs)


def in_blocks(array, dim, length):
    before, after = (array.shape[:dim], array.shape[dim + 1 :])
    return jnp.moveaxis(array.reshape(*before, length, -1, *after), dim, 0)


def in_order(tiles, dim):
    tiles = jnp.moveaxis(tiles, 0, dim)
    dims = tiles.shape
    return tiles.reshape(*dims[:dim], dims[dim] * dims[dim + 1], *dims[dim + 2 :])


def exchange_both(array, axis, axes, splits, concats):
    sizes = [lax.axis_size(a) for a in axes]
    tiles = in_blocks(array, splits[0], sizes[0])
    tiles = jnp.moveaxis(in_blocks(tiles, splits[1] + 1, sizes[1]), 0, 1)
    inside = tiles.shape[2:]
    tiles = tiles.reshape(-1, *inside)
    tiles = lax.all_to_all(tiles, axis, split_axis=0, concat_axis=0, tiled=True)
    tiles = in_order(tiles.reshape(*sizes, *inside), concats[0] + 1)
    return in_order(tiles, concats[1])


def filled_up(lines, length):
    spare = -len(lines) % length
    return jnp.pad(lines, [(0, spare)] + [(0, 0)] * (lines.ndim - 1))


def copy_for_each(array, axis):
    copies = jnp.broadcast_to(array, (lax.axis_size(axis), *array.shape))
    return lax.all_to_all(copies, axis, split_axis=0, concat_axis=0, tiled=True)


def whole_of(array, axes, dim):
    far, near = axes
    leading = copy_for_each(array, far)
    tiles = jnp.swapaxes(copy_for_each(leading, near), 0, 1)
    return in_order(tiles.reshape(-1, *array.shape), dim)


def sum_at_owner(array, axis, dim):
    tiles = in_blocks(array, dim, lax.axis_size(axis))
    arrived = lax.all_to_all(tiles, axis, split_axis=0, concat_axis=0, tiled=True)
    return arrived.sum(axis=0)


def sum_in_two_steps(array, axes, dim):
    far, near = axes
    own = sum_at_owner(in_blocks(array, dim, lax.axis_size(far)), near, dim + 1)
    return jnp.sum(lax.all_to_all(own, far, 0, 0, tiled=True), axis=0)


def total_of(array, axes):
    lines = array.reshape(-1, array.shape[-1])
    padded = filled_up(lines, lax.axis_size(axes[0]) * lax.axis_size(axes[1]))
    whole = whole_of(sum_in_two_steps(padded, axes, 0), axes, 0)
    return lax.slice_in_dim(whole, 0, len(lines)).reshape(array.shape)


def sine_table(size):
    index = jnp.arange(size, dtype=jnp.int32) + 1
    product = index[:, None] * index[None, :] % (2 * (size + 1))
    angle = math.pi * product.astype(jnp.float32) / (size + 1)
    return jnp.sqrt(jnp.float32(2.0 / (size + 1))) * jnp.sin(angle)


def eigen_sum(size):
    steps = jnp.arange(size, dtype=jnp.float32) + 1.0
    lam = 2.0 - 2.0 * jnp.cos(math.pi * steps / (size + 1))
    total = lam[:, None, None] + lam[None, :, None] + lam[None, None, :] + screening
    return total.reshape(size, size * size)


def sine_transform(field, table, doubled):
    size = table.shape[0]
    highest = lax.Precision.HIGHEST
    field = jnp.dot(table, field, precision=highest)
    field = jnp.dot(field.reshape(-1, 2 * size), doubled, precision=highest)
    field = jnp.einsum("ky,xyz->xkz", table, field.reshape(size, size, size), precision=highest)
    return field.reshape(size, size * size)


def on_device(orbitals, partners):
    table = sine_table(NG)
    doubled = jnp.kron(jnp.eye(2, dtype=jnp.float32), table)
    denom = eigen_sum(NG)

    def solved(density):
        return sine_transform(sine_transform(density, table, doubled) / denom, table, doubled)

    def nothing(density):
        return jnp.zeros_like(density)

    own = orbitals.reshape(NG, NG * NG).astype(jnp.float32)
    live = partners[0] >= 0
    total = jnp.zeros((NG, NG * NG), jnp.float32)
    for slot in range(PARTNERS):
        arrived = partner(orbitals, BAND, slot)
        other = arrived.reshape(NG, NG * NG).astype(jnp.float32)
        density = own * other
        potential = lax.cond(live[slot], solved, nothing, density)
        term = lax.optimization_barrier((potential * other).astype(jnp.bfloat16))
        total = total + jnp.where(live[slot], term.astype(jnp.float32), 0.0)
    applied = total.astype(jnp.bfloat16)
    band_count = lax.axis_size(BAND)
    pair_count = lax.axis_size("pair")
    cells = NG3 // (band_count * pair_count)
    layout = (1, 1, band_count, pair_count, cells)
    first = orbitals.reshape(layout)
    second = applied.reshape(layout)
    phi_slab, applied_slab = (
        exchange_both(first, BAND_PAIR, (BAND, "pair"), (2, 3), (0, 1)),
        exchange_both(second, BAND_PAIR, (BAND, "pair"), (2, 3), (0, 1)),
    )
    count = band_count * pair_count
    phi_slab = phi_slab.reshape(count, cells)
    applied_slab = applied_slab.reshape(count, cells)
    partial_intersection = lax.dot_general(
        phi_slab, applied_slab, (((1,), (1,)), ((), ())), preferred_element_type=jnp.float32
    )
    intersection = total_of(
        partial_intersection * (1.0 / NG3), (("band_0", "band_1"), ("band_2", "pair"))
    )
    removed = lax.dot_general(
        intersection,
        phi_slab.astype(jnp.float32),
        (((0,), (0,)), ((), ())),
        precision=lax.Precision.HIGHEST,
    )
    return applied_slab.astype(jnp.float32) - removed


def solution(mesh):
    torus = Mesh(
        mesh.devices.reshape(4, 16, 2, mesh.shape["pair"]), ("band_0", "band_1", "band_2", "pair")
    )
    in_specs = (P(BAND_PAIR, None), P(BAND_PAIR, None))
    out_specs = P(None, BAND_PAIR)
    return jax.shard_map(
        on_device, mesh=torus, in_specs=in_specs, out_specs=out_specs, check_vma=False
    )
```

profile of v0, /device:TPU:1, one launch (start us, length us, event | category | flops | bytes accessed | tf_op | source)
XLA Modules:
  0.0 358.6 jit_solution(5692601228402164736)
XLA Ops:
  0.0 4.5 %collective-permute-start.1 = (bf16[1,262144]{1,0:T(2,128)(2,1)}, bf16[1,262144]{1,0:T(2,128)(2,1)}, u32[]{:S(2)}, u32[]{:S(2)}) collective-permute-start(bf16[1,262144]{1,0:T(2,128)(2,1)} %param.8), channel_id=1, source_target_pairs={{0,8},{4,12},{8,0},{12,4},{16,24},{20,28},{24,16},{28,20},{32,40},... | collective-permute-start | bytes 1572872 | tf_op jit(solution)/shard_map/ppermute | solution.py:22
  4.5 4.9 %collective-permute-start.2 = (bf16[1,262144]{1,0:T(2,128)(2,1)}, bf16[1,262144]{1,0:T(2,128)(2,1)}, u32[]{:S(2)}, u32[]{:S(2)}) collective-permute-start(bf16[1,262144]{1,0:T(2,128)(2,1)} %param.8), channel_id=1, source_target_pairs={{0,16},{4,20},{8,24},{12,28},{16,0},{20,4},{24,8},{28,12},{32,48},... | collective-permute-start | bytes 1572872 | tf_op jit(solution)/shard_map/ppermute | solution.py:22
  13.3 4.7 %reduce.20 = bf16[512,512]{1,0:T(8,128)(2,1)S(1)} reduce(bf16[512,1,1,1,1,512]{5,4,3,2,1,0:T(2,128)(2,1)} %bitcast.102, bf16[]{:T(256)} %broadcast.181), dimensions={1,2,3,4}, to_apply=%bitcast.24.reduce_sub_computation | reduce | bytes 1048578 | tf_op jit(solution)/shard_map/reshape;transpose;transpose;reshape;transpose;reshape;reshape | solution.py:41
  19.0 22.8 %all-to-all-start.1 = ((bf16[512,2,256]{2,1,0:T(2,128)(2,1)}), bf16[512,2,256]{2,1,0:T(2,128)(2,1)}, u32[]{:S(2)}, u32[]{:S(2)}) async-start(bf16[512,2,256]{2,1,0:T(2,128)(2,1)} %reshape.245), calls=%async_computation.1 | async-start | bytes 1048576 | tf_op jit(solution)/shard_map/all_to_all | solution.py:42
  41.9 9.7 %convert_reduce_fusion.3 = f32[262144]{0:T(1024)} fusion(bf16[1,262144]{1,0:T(2,128)(2,1)S(1)} %copy-done.1), kind=kLoop, calls=%fused_computation.33 | loop fusion | flops 262144 | bytes 1572864 | tf_op jit(solution)/shard_map/convert_element_type | solution.py:117
  59.6 9.7 %convert_reduce_fusion.1 = f32[262144]{0:T(1024)S(1)} fusion(bf16[1,262144]{1,0:T(2,128)(2,1)} %collective-permute-done.1), kind=kLoop, calls=%fused_computation.31 | loop fusion | flops 262144 | bytes 1572864 | tf_op jit(solution)/shard_map/convert_element_type | solution.py:122
  69.5 8.1 %conditional.4 = (f32[64,4096]{1,0:T(8,128)S(1)}) conditional(s32[]{:T(128)} %convert_element_type.125, () %tuple.25, (f32[64,4096]{1,0:T(8,128)S(1)}, f32[64,4096]{1,0:T(8,128)S(1)}, f32[64,64]{1,0:T(8,128)S(1)}, f32[128,128]{1,0:T(8,128)S(1)}, f32[64,64]{1,0:T(8,128)S(1)}, /*index=5*/f32[64,4096]{1,0:T(8,128)}, f32[64,64]{1,0:T(8,128)S(1)}, ...), branch_computations={%region_2.3_spmd, %region_3.4_spmd} | conditional | flops 1611137024 | bytes 31653896 | solution.py:124
  78.5 9.7 %convert_reduce_fusion = f32[262144]{0:T(1024)S(1)} fusion(bf16[1,262144]{1,0:T(2,128)(2,1)} %collective-permute-done.2), kind=kLoop, calls=%fused_computation.30 | loop fusion | flops 262144 | bytes 1572864 | tf_op jit(solution)/shard_map/convert_element_type | solution.py:122
  88.5 39.2 %conditional.5 = (f32[64,4096]{1,0:T(8,128)S(1)}) conditional(s32[]{:T(128)} %convert_element_type.130, () %tuple.27, (f32[64,4096]{1,0:T(8,128)S(1)}, f32[64,4096]{1,0:T(8,128)S(1)}, f32[64,64]{1,0:T(8,128)S(1)}, f32[128,128]{1,0:T(8,128)S(1)}, f32[64,64]{1,0:T(8,128)S(1)}, /*index=5*/f32[64,4096]{1,0:T(8,128)}, f32[64,64]{1,0:T(8,128)S(1)}, ...), branch_computations={%region_4.5_spmd, %region_5.6_spmd} | conditional | flops 1611137024 | bytes 31653896 | solution.py:124
  94.6 6.4 %convolution_bitcast_fusion.11 = f32[64,64,64]{1,2,0:T(8,128)} fusion(f32[64,64,64]{2,1,0:T(8,128)} %reshape.198, f32[64,64]{1,0:T(8,128)S(1)} %get-tuple-element.85), kind=kOutput, calls=%fused_computation.19 | convolution fusion | flops 201326592 | bytes 2113536 | tf_op jit(solution)/shard_map/cond/branch_1_fun/ky,xyz->xkz/dot_general | solution.py:102
  106.4 3.4 convolution_bitcast_fusion.8
  116.1 6.4 %convolution_bitcast_fusion.10 = f32[64,64,64]{1,2,0:T(8,128)} fusion(f32[64,64,64]{2,1,0:T(8,128)} %reshape.201, f32[64,64]{1,0:T(8,128)S(1)} %get-tuple-element.85), kind=kOutput, calls=%fused_computation.18 | convolution fusion | flops 201326592 | bytes 2113536 | tf_op jit(solution)/shard_map/cond/branch_1_fun/ky,xyz->xkz/dot_general | solution.py:102
  128.5 9.7 %convert_reduce_fusion.2 = f32[262144]{0:T(1024)S(1)} fusion(bf16[1,262144]{1,0:T(2,128)(2,1)} %collective-permute-done), kind=kLoop, calls=%fused_computation.32 | loop fusion | flops 262144 | bytes 1572864 | tf_op jit(solution)/shard_map/convert_element_type | solution.py:122
  138.5 35.8 %conditional.3 = (f32[64,4096]{1,0:T(8,128)S(1)}) conditional(s32[]{:T(128)} %convert_element_type.116, () %tuple.23, (f32[64,4096]{1,0:T(8,128)S(1)}, f32[64,4096]{1,0:T(8,128)S(1)}, f32[64,64]{1,0:T(8,128)S(1)}, f32[128,128]{1,0:T(8,128)S(1)}, f32[64,64]{1,0:T(8,128)S(1)}, /*index=5*/f32[64,4096]{1,0:T(8,128)}, f32[64,64]{1,0:T(8,128)S(1)}, ...), branch_computations={%region_0.1_spmd, %region_1.2_spmd} | conditional | flops 1611137024 | bytes 35848228 | solution.py:124
  144.6 6.4 %convolution_bitcast_fusion.3 = f32[64,64,64]{1,2,0:T(8,128)} fusion(f32[64,64,64]{2,1,0:T(8,128)} %reshape.186, f32[64,64]{1,0:T(8,128)S(1)} %get-tuple-element.55), kind=kOutput, calls=%fused_computation.3 | convolution fusion | flops 201326592 | bytes 2113536 | tf_op jit(solution)/shard_map/cond/branch_1_fun/ky,xyz->xkz/dot_general | solution.py:102
  162.5 6.4 %convolution_bitcast_fusion.2 = f32[64,64,64]{1,2,0:T(8,128)} fusion(f32[64,64,64]{2,1,0:T(8,128)} %reshape.189, f32[64,64]{1,0:T(8,128)S(1)} %get-tuple-element.55), kind=kOutput, calls=%fused_computation.2 | convolution fusion | flops 201326592 | bytes 2113536 | tf_op jit(solution)/shard_map/cond/branch_1_fun/ky,xyz->xkz/dot_general | solution.py:102
  178.6 3.8 %reduce.21 = bf16[512,512]{1,0:T(8,128)(2,1)S(1)} reduce(bf16[512,1,1,1,1,512]{5,4,3,2,1,0:T(2,128)(2,1)S(1)} %reshape_transpose_transpose_reshape_transpose_reshape_reshape.8, bf16[]{:T(256)} %broadcast.181), dimensions={1,2,3,4}, to_apply=%reshape_transpose_transpose_reshape_transpose_reshape_reshape.8.reduce_sub_co... | reduce | bytes 1048578 | tf_op jit(solution)/shard_map/reshape;transpose;transpose;reshape;transpose;reshape;reshape | solution.py:41
  183.3 52.8 %all-to-all-start = ((bf16[512,2,256]{2,1,0:T(2,128)(2,1)}), bf16[512,2,256]{2,1,0:T(2,128)(2,1)S(1)}, u32[]{:S(2)}, u32[]{:S(2)}) async-start(bf16[512,2,256]{2,1,0:T(2,128)(2,1)} %reshape.247), calls=%async_computation | async-start | bytes 1048576 | tf_op jit(solution)/shard_map/all_to_all | solution.py:42
  236.1 3.6 reshape.246
  243.2 29.0 %all-to-all-done = bf16[512,2,256]{2,1,0:T(2,128)(2,1)S(1)} async-done(((bf16[512,2,256]{2,1,0:T(2,128)(2,1)}), bf16[512,2,256]{2,1,0:T(2,128)(2,1)S(1)}, u32[]{:S(2)}, u32[]{:S(2)}) %all-to-all-start) | async-done | bytes 524320 | tf_op jit(solution)/shard_map/all_to_all | solution.py:42
  277.2 17.9 %all_to_all.33 = f32[8,64,1,512]{3,1,2,0:T(8,128)S(1)} all-to-all(f32[8,64,1,512]{3,1,2,0:T(8,128)S(1)} %bitcast.103), channel_id=1, replica_groups=mesh['band_0'=4,'band_1'=16,'band_2'=2,'pair'=4] {'band_2','pair'}, dimensions={0} | all-to-all | bytes 2097152 | tf_op jit(solution)/shard_map/all_to_all | solution.py:66
  295.2 18.7 %all_to_all.34 = f32[64,1,512]{2,1,0:T(1,128)S(1)} all-to-all(f32[64,1,512]{2,1,0:T(1,128)S(1)} %reduce_sum.21), channel_id=1, replica_groups=mesh['band_0'=4,'band_1'=16,'band_2'=2,'pair'=4] {'band_0','band_1'}, dimensions={0} | all-to-all | bytes 262144 | tf_op jit(solution)/shard_map/all_to_all | solution.py:73
  314.1 21.1 %all_to_all.35 = f32[64,1,512]{2,1,0:T(1,128)S(1)} all-to-all(f32[64,1,512]{2,1,0:T(1,128)S(1)} %broadcast_in_dim.22), channel_id=1, replica_groups=mesh['band_0'=4,'band_1'=16,'band_2'=2,'pair'=4] {'band_0','band_1'}, dimensions={0} | all-to-all | bytes 262144 | tf_op jit(solution)/shard_map/all_to_all | solution.py:54
  335.4 20.7 %all_to_all.36 = f32[8,64,1,512]{3,1,2,0:T(8,128)S(1)} all-to-all(f32[8,64,1,512]{3,1,2,0:T(8,128)S(1)} %broadcast_in_dim.23), channel_id=1, replica_groups=mesh['band_0'=4,'band_1'=16,'band_2'=2,'pair'=4] {'band_2','pair'}, dimensions={0} | all-to-all | bytes 2097152 | tf_op jit(solution)/shard_map/all_to_all | solution.py:54
  (83 shorter events, 75.2 us)
Async XLA Ops:
  0.0 41.8 %copy-start.1 = (bf16[1,262144]{1,0:T(2,128)(2,1)S(1)}, bf16[1,262144]{1,0:T(2,128)(2,1)}, u32[]{:S(2)}) copy-start(bf16[1,262144]{1,0:T(2,128)(2,1)} %param.8) | copy-start | bytes 1572868
  0.0 59.6 %collective-permute-start.1 = (bf16[1,262144]{1,0:T(2,128)(2,1)}, bf16[1,262144]{1,0:T(2,128)(2,1)}, u32[]{:S(2)}, u32[]{:S(2)}) collective-permute-start(bf16[1,262144]{1,0:T(2,128)(2,1)} %param.8), channel_id=1, source_target_pairs={{0,8},{4,12},{8,0},{12,4},{16,24},{20,28},{24,16},{28,20},{32,40},... | collective-permute-start | bytes 1572872 | tf_op jit(solution)/shard_map/ppermute | solution.py:22
  4.5 74.0 %collective-permute-start.2 = (bf16[1,262144]{1,0:T(2,128)(2,1)}, bf16[1,262144]{1,0:T(2,128)(2,1)}, u32[]{:S(2)}, u32[]{:S(2)}) collective-permute-start(bf16[1,262144]{1,0:T(2,128)(2,1)} %param.8), channel_id=1, source_target_pairs={{0,16},{4,20},{8,24},{12,28},{16,0},{20,4},{24,8},{28,12},{32,48},... | collective-permute-start | bytes 1572872 | tf_op jit(solution)/shard_map/ppermute | solution.py:22
  9.4 119.1 %collective-permute-start = (bf16[1,262144]{1,0:T(2,128)(2,1)}, bf16[1,262144]{1,0:T(2,128)(2,1)}, u32[]{:S(2)}, u32[]{:S(2)}) collective-permute-start(bf16[1,262144]{1,0:T(2,128)(2,1)} %param.8), channel_id=1, source_target_pairs={{0,4},{4,0},{8,12},{12,8},{16,20},{20,16},{24,28},{28,24},{32,36},... | collective-permute-start | bytes 1572872 | tf_op jit(solution)/shard_map/ppermute | solution.py:22
  19.0 164.3 %all-to-all-start.1 = ((bf16[512,2,256]{2,1,0:T(2,128)(2,1)}), bf16[512,2,256]{2,1,0:T(2,128)(2,1)}, u32[]{:S(2)}, u32[]{:S(2)}) async-start(bf16[512,2,256]{2,1,0:T(2,128)(2,1)} %reshape.245), calls=%async_computation.1 | async-start | bytes 1048576 | tf_op jit(solution)/shard_map/all_to_all | solution.py:42
  52.7 3.3 copy-start.5
  54.4 4.1 %copy-start = (f32[64,4096]{1,0:T(8,128)S(1)}, f32[64,4096]{1,0:T(8,128)}, u32[]{:S(2)}) copy-start(f32[64,4096]{1,0:T(8,128)} %add.208) | copy-start | bytes 3145732
  154.1 2.2 copy-start.4
  174.3 1.0 copy-start.2
  174.3 1.2 copy-start.3
  183.3 88.9 %all-to-all-start = ((bf16[512,2,256]{2,1,0:T(2,128)(2,1)}), bf16[512,2,256]{2,1,0:T(2,128)(2,1)S(1)}, u32[]{:S(2)}, u32[]{:S(2)}) async-start(bf16[512,2,256]{2,1,0:T(2,128)(2,1)} %reshape.247), calls=%async_computation | async-start | bytes 1048576 | tf_op jit(solution)/shard_map/all_to_all | solution.py:42
where the time goes:
time: 364 us; the launch traced here: 359 us
  starting transfers between devices  88.3 us (24%)
  blocking collectives  78.4 us (22%)
  other arithmetic  59.5 us (16%)
  local copies, waits for them, and re-layouts  48.5 us (13%)
  matrix products  43.8 us (12%)
  waiting for transfers between devices  29 us (8%)
  loops' own time  8.77 us (2%)
    all_to_all x2, starting transfers between devices, exchange_both(): tiles = lax.all_to_all(tiles, axis, split_axis=0, concat_axis=0, tiled=True)  75.6 us
    all_to_all x2, blocking collectives, copy_for_each(): return lax.all_to_all(copies, axis, split_axis=0, concat_axis=0, tiled=True)  41.8 us
    convert_element_type x3, other arithmetic, on_device(): other = arrived.reshape(NG, NG * NG).astype(jnp.float32)  29.2 us
    all_to_all x2, waiting for transfers between devices, exchange_both(): tiles = lax.all_to_all(tiles, axis, split_axis=0, concat_axis=0, tiled=True)  29 us
    dot_general x4, matrix products, sine_transform(): jnp.einsum('ky,xyz->xkz', table, field.reshape(size, size, size), precisi...  25.5 us
    all_to_all x1, blocking collectives, sum_in_two_steps(): return jnp.sum(lax.all_to_all(own, far, 0, 0, tiled=True), axis=0)  18.7 us
    all_to_all x1, blocking collectives, sum_at_owner(): lax.all_to_all(tiles, axis, split_axis=0, concat_axis=0, tiled=True)  17.9 us
    ppermute x3, starting transfers between devices, partner(): return lax.ppermute(value, axis, pairs)  12.7 us
  transfers between devices with their start and end apart: 5, of which 1 were waited for; matrix products, arithmetic and copies ran while one was open for 40% of the time, Pallas kernels for 0%

commit v1 on v0

v1 whole, which is shorter than its diff:
```python
import math

import jax
import jax.numpy as jnp
import numpy as np
from jax import lax
from jax.experimental import pallas as pl
from jax.experimental.pallas import tpu as pltpu
from jax.sharding import Mesh
from jax.sharding import PartitionSpec as P

NG = 64
PARTNERS = 3
NG3 = 262144
LANES = 128
ROWS = NG3 // LANES
BAND = ("band_0", "band_1", "band_2")
BAND_PAIR = ("band_0", "band_1", "band_2", "pair")
PLANE = ("band_0", "band_2", "pair")
LINE = "band_1"
F32, BF16 = jnp.float32, jnp.bfloat16
LIMIT = pltpu.CompilerParams(vmem_limit_bytes=16 * 2**20)


screening = 0.05


def partner(value, axis, distance):
    mask = 2**distance
    pairs = [(source, source ^ mask) for source in range(lax.axis_size(axis))]
    return lax.ppermute(value, axis, pairs)


def two_parts(value):
    high = value.astype(BF16)
    return high, (value - high.astype(F32)).astype(BF16)


def tables():
    steps = np.arange(NG) + 1
    table = np.sqrt(2.0 / (NG + 1)) * np.sin(np.pi * (np.outer(steps, steps) % (2 * NG + 2)) / (NG + 1))
    order = np.concatenate([np.arange(0, NG, 2), np.arange(1, NG, 2)])
    high = table.astype(BF16).astype(np.float64)
    low = table - high
    z_high, z_low = (np.kron(np.eye(2), part) for part in (high, low))
    high_y, low_y = (part[order][:, order] for part in (high, low))
    parts = (
        np.concatenate([z_high, z_high], axis=0),
        z_low,
        np.concatenate([high_y, high_y, low_y], axis=1),
        np.concatenate([high, high, low], axis=1),
    )
    return [jnp.asarray(part.astype(BF16)) for part in parts]


def compact_kernel(raw, out):
    def step(n, carry):
        rows = pl.ds(pl.multiple_of(n * 128, 128), 128)
        out[rows] = raw[rows, 0, :]
        return carry

    lax.fori_loop(0, ROWS // 128, step, 0)


def compact(raw):
    return pl.pallas_call(
        compact_kernel, out_shape=jax.ShapeDtypeStruct((ROWS, LANES), BF16), name="compact",
        compiler_params=LIMIT
    )(raw.reshape(ROWS, 1, LANES))


def inverse_kernel(out):
    def lam(index):
        return 2.0 - 2.0 * jnp.cos(math.pi * (index.astype(F32) + 1.0) / (NG + 1))

    shape = (NG, LANES)
    lane = lax.broadcasted_iota(jnp.int32, shape, 1)
    base = lam(lax.broadcasted_iota(jnp.int32, shape, 0)) + lam(lane % NG) + screening

    def step(pair, carry):
        y = lax.broadcasted_iota(jnp.int32, (8, LANES), 1) // NG + 2 * pair
        out[pair] = 1.0 / (base + jnp.broadcast_to(lam(y)[0:1], shape))
        return carry

    lax.fori_loop(0, NG // 2, step, 0)


def inverse_eigen():
    return pl.pallas_call(
        inverse_kernel, out_shape=jax.ShapeDtypeStruct((NG // 2, NG, LANES), F32), name="inverse",
        compiler_params=LIMIT
    )()


def dot(a, b):
    return jnp.dot(a, b, preferred_element_type=F32)


def side(table, value):
    high, low = two_parts(value)
    return dot(table, jnp.concatenate([high, low, high], axis=0))


def along_z(value, z_main, z_low):
    high, low = two_parts(value)
    return dot(jnp.concatenate([high, low], axis=1), z_main) + dot(high, z_low)


def swap_halves(rows, mask):
    first, second = rows[:32], rows[32:]
    top = jnp.where(mask, first, pltpu.roll(second, NG, 1))
    bottom = jnp.where(mask, pltpu.roll(first, NG, 1), second)
    return jnp.concatenate([top, bottom], axis=0)


def along_y(slabs, y_side, mask):
    moved = side(y_side, jnp.concatenate([swap_halves(s, mask) for s in slabs], axis=1))
    return [swap_halves(moved[:, LANES * n : LANES * (n + 1)], mask) for n in range(len(slabs))]


def pair_slabs(block, pair):
    start = 128 * pair
    return [block[start : start + 64], block[start + 64 : start + 128]]


def forward_part(own, other, z_main, z_low, y_side, field, mask):
    def step(n, carry):
        rows = pl.ds(pl.multiple_of(n * 256, 256), 256)
        density = own[rows].astype(F32) * other[rows].astype(F32)
        moved = along_z(density, z_main[...], z_low[...])
        for pair in range(2):
            for m, slab in enumerate(along_y(pair_slabs(moved, pair), y_side[...], mask)):
                field[pl.ds(n * 8 + 4 * pair + 2 * m, 2)] = slab.reshape(2, 32, LANES)
        return carry

    lax.fori_loop(0, ROWS // 256, step, 0)


def middle_part(x_side, inverse, field):
    def step(n, carry):
        group = pl.ds(pl.multiple_of(n * 8, 8), 8)
        block = jnp.transpose(field[:, group, :], (1, 0, 2))
        outs = []
        for pair in range(4):
            lines = [2 * pair, 2 * pair + 1]
            value = jnp.concatenate([block[m] for m in lines], axis=1)
            scale = jnp.concatenate([inverse[n * 8 + m] for m in lines], axis=1)
            value = side(x_side[...], side(x_side[...], value) * scale)
            outs += [value[:, :LANES], value[:, LANES:]]
        field[:, group, :] = jnp.transpose(jnp.stack(outs, axis=0), (1, 0, 2))
        return carry

    lax.fori_loop(0, 4, step, 0)


def backward_block(n, other, z_main, z_low, y_side, field, mask):
    rows = pl.ds(pl.multiple_of(n * 256, 256), 256)
    block = field[pl.ds(n * 8, 8)].reshape(256, LANES)
    slabs = []
    for pair in range(2):
        slabs += along_y(pair_slabs(block, pair), y_side[...], mask)
    moved = along_z(jnp.concatenate(slabs, axis=0), z_main[...], z_low[...])
    return rows, (moved * other[rows].astype(F32)).astype(BF16)


def solve_kernel(own, other, z_main, z_low, y_side, x_side, inverse, term, field):
    mask = lax.broadcasted_iota(jnp.int32, (32, LANES), 1) < NG
    forward_part(own, other, z_main, z_low, y_side, field, mask)
    middle_part(x_side, inverse, field)

    def step(n, carry):
        rows, value = backward_block(n, other, z_main, z_low, y_side, field, mask)
        term[rows] = value
        return carry

    lax.fori_loop(0, ROWS // 256, step, 0)


def last_kernel(
    partners, own, other, z_main, z_low, y_side, x_side, inverse, first, second, out, field
):
    mask = lax.broadcasted_iota(jnp.int32, (32, LANES), 1) < NG
    forward_part(own, other, z_main, z_low, y_side, field, mask)
    middle_part(x_side, inverse, field)

    def step(n, carry):
        rows, third = backward_block(n, other, z_main, z_low, y_side, field, mask)
        total = jnp.zeros((256, LANES), F32)
        for slot, value in enumerate((first[rows], second[rows], third)):
            total = total + jnp.where(partners[0, slot] >= 0, value.astype(F32), 0.0)
        out[pl.ds(n % 2 * 8, 8), n // 2] = total.astype(BF16).reshape(8, 32, LANES)
        return carry

    lax.fori_loop(0, ROWS // 256, step, 0)


FIELD = pltpu.VMEM((NG, NG // 2, LANES), F32)
VMEM = pl.BlockSpec(memory_space=pltpu.VMEM)
SMEM = pl.BlockSpec(memory_space=pltpu.SMEM)


def solve(own, other, parts, inverse):
    return pl.pallas_call(
        solve_kernel,
        out_shape=jax.ShapeDtypeStruct((ROWS, LANES), BF16),
        scratch_shapes=[FIELD],
        name="solve",
        compiler_params=LIMIT,
    )(own, other, *parts, inverse)


def solve_last(partners, own, other, parts, inverse, first, second):
    return pl.pallas_call(
        last_kernel,
        out_shape=jax.ShapeDtypeStruct((16, 4, 32, LANES), BF16),
        in_specs=[SMEM] + [VMEM] * 9,
        scratch_shapes=[FIELD],
        name="last",
        compiler_params=LIMIT,
    )(partners, own, other, *parts, inverse, first, second)


def turn_kernel(value, out):
    for n in range(8):
        block = jnp.transpose(value[:, 16 * n : 16 * n + 16, :], (1, 0, 2))
        out[4 * n : 4 * n + 4] = block.reshape(4, 64, LANES)


def turned(value):
    return pl.pallas_call(
        turn_kernel, out_shape=jax.ShapeDtypeStruct((32, 64, LANES), BF16), name="turn",
        compiler_params=LIMIT
    )(value)


def exchange(value, axes):
    return lax.all_to_all(value, axes, split_axis=0, concat_axis=0, tiled=True)


def regroup(value):
    return exchange(turned(exchange(value.reshape(16, 128, LANES), LINE)), PLANE)


def quarter(slab, q):
    return slab[:, 16 * q : 16 * q + 16, :].reshape(512, LANES)


def whole(slab):
    return jnp.concatenate([quarter(slab, q) for q in range(4)], axis=1)


def overlap_kernel(phi, applied, out):
    value = lax.dot_general(
        whole(applied), whole(phi), (((1,), (1,)), ((), ())), preferred_element_type=F32
    )
    out[...] = value * (1.0 / NG3)


def overlap(phi, applied):
    return pl.pallas_call(
        overlap_kernel, out_shape=jax.ShapeDtypeStruct((512, 512), F32), name="overlap",
        compiler_params=LIMIT
    )(phi, applied)


def project_kernel(overlaps, phi, applied, out):
    high, low = two_parts(overlaps[...])
    cells = whole(phi)
    value = whole(applied).astype(F32) - (dot(high, cells) + dot(low, cells))
    for y in range(4):
        block = value[128 * y : 128 * y + 128].reshape(8, 16, 512)
        out[128 * y : 128 * y + 128] = jnp.transpose(block, (1, 0, 2)).reshape(128, 512)


def project(overlaps, phi, applied):
    return pl.pallas_call(
        project_kernel, out_shape=jax.ShapeDtypeStruct((512, 512), F32), name="project",
        compiler_params=LIMIT
    )(overlaps, phi, applied)


def total_of(value):
    arrived = exchange(value.reshape(32, 16, 512), PLANE).sum(axis=0)
    owned = exchange(arrived.reshape(16, 4, LANES), LINE).sum(axis=0)
    line = exchange(jnp.broadcast_to(owned, (16, 4, LANES)), LINE).reshape(16, 512)
    return exchange(jnp.broadcast_to(line, (32, 16, 512)), PLANE).reshape(512, 512)


def on_device(orbitals, partners):
    mine = compact(orbitals)
    others = [partner(mine, BAND, slot) for slot in range(PARTNERS)]
    parts = tables()
    inverse = inverse_eigen()
    first = solve(mine, others[0], parts, inverse)
    second = solve(mine, others[1], parts, inverse)
    early, first = lax.optimization_barrier((mine, first))
    phi = regroup(early.reshape(4, 16, 32, LANES).transpose(1, 0, 2, 3))
    applied = regroup(solve_last(partners, mine, others[2], parts, inverse, first, second))
    return project(total_of(overlap(phi, applied)), phi, applied)


def solution(mesh):
    torus = Mesh(
        mesh.devices.reshape(4, 16, 2, mesh.shape["pair"]), ("band_0", "band_1", "band_2", "pair")
    )
    in_specs = (P(BAND_PAIR, None), P(BAND_PAIR, None))
    out_specs = P(None, BAND_PAIR)
    return jax.shard_map(
        on_device, mesh=torus, in_specs=in_specs, out_specs=out_specs, check_vma=False
    )
```

time: 364 us -> 244 us (0.67); the launches traced: 359 us -> 243 us
  other arithmetic: 59.5 us -> 0.1 us
  local copies, waits for them, and re-layouts: 48.5 us -> 2.25 us
  matrix products: 43.8 us -> 0 us
  Pallas kernels: 0 us -> 38 us
  starting transfers between devices: 88.3 us -> 51.1 us
  waiting for transfers between devices: 29 us -> 61.1 us
  blocking collectives: 78.4 us -> 90.5 us
  loops' own time: 8.77 us -> 0 us
    dot_general x14 -> x0, matrix products: 43.8 us -> none  [the longest x4 25.5 us: sine_transform(): jnp.einsum('ky,xyz->xkz', table, field.reshape(size, size, size), precisi...]
    convert_element_type x9 -> x0, other arithmetic: 42.9 us -> none  [the longest x3 29.2 us: on_device(): other = arrived.reshape(NG, NG * NG).astype(jnp.float32)]
    pallas_call x0 -> x9, Pallas kernels: none -> 38 us  [the longest x2 19.6 us: solve(): pl.pallas_call(solve_kernel, out_shape=jax.ShapeDtypeStruct((ROWS, LANES)...]
    all_to_all x2 -> x3, starting transfers between devices: 75.6 us -> 38.4 us  [exchange(): return lax.all_to_all(value, axes, split_axis=0, concat_axis=0, tiled=True)]
    all_to_all x2 -> x3, waiting for transfers between devices: 29 us -> 55.7 us  [exchange(): return lax.all_to_all(value, axes, split_axis=0, concat_axis=0, tiled=True)]
    reshape x14 -> x2, local copies, waits for them, and re-layouts: 21.5 us -> 0.87 us  [the longest x1 0.85 us: on_device(): phi = regroup(early.reshape(4, 16, 32, LANES).transpose(1, 0, 2, 3))]
    all_to_all x4 -> x5, blocking collectives: 78.4 us -> 90.5 us  [exchange(): return lax.all_to_all(value, axes, split_axis=0, concat_axis=0, tiled=True)]
    transpose x4 -> x0, local copies, waits for them, and re-layouts: 12.1 us -> none  [sine_transform(): jnp.einsum('ky,xyz->xkz', table, field.reshape(size, size, size), precisi...]
  transfers between devices with their start and end apart: 5 -> 6, of which waited for: 1 -> 4; matrix products, arithmetic and copies ran while one was open for 40% -> 0% of each run, Pallas kernels for 0% -> 9%
where the time goes in v1:
time: 244 us; the launch traced here: 243 us
  blocking collectives  90.5 us (37%)
  waiting for transfers between devices  61.1 us (25%)
  starting transfers between devices  51.1 us (21%)
  Pallas kernels  38 us (16%)
    all_to_all x5, blocking collectives, exchange(): return lax.all_to_all(value, axes, split_axis=0, concat_axis=0, tiled=True)  90.5 us
    all_to_all x3, waiting for transfers between devices, exchange(): return lax.all_to_all(value, axes, split_axis=0, concat_axis=0, tiled=True)  55.7 us
    all_to_all x3, starting transfers between devices, exchange(): return lax.all_to_all(value, axes, split_axis=0, concat_axis=0, tiled=True)  38.4 us
    pallas_call x2, Pallas kernels, solve(): pl.pallas_call(solve_kernel, out_shape=jax.ShapeDtypeStruct((ROWS, LANES)...  19.6 us
    ppermute x3, starting transfers between devices, partner(): return lax.ppermute(value, axis, pairs)  12.7 us
    pallas_call x1, Pallas kernels, solve_last(): pl.pallas_call(last_kernel, out_shape=jax.ShapeDtypeStruct((16, 4, 32, LA...  11.2 us
    ppermute x3, waiting for transfers between devices, partner(): return lax.ppermute(value, axis, pairs)  5.47 us
  transfers between devices with their start and end apart: 6, of which 4 were waited for; matrix products, arithmetic and copies ran while one was open for 0% of the time, Pallas kernels for 9%

profile of v1, /device:TPU:1, one launch (start us, length us, event | category | flops | bytes accessed | tf_op | source)
XLA Modules:
  0.0 243.3 jit_solution(5846487573896974381)
XLA Ops:
  0.0 1.2 copy-done
  1.2 1.6 compact.1.own
  2.9 8.9 %collective-permute-start = (bf16[2048,128]{1,0:T(8,128)(2,1)S(1)}, bf16[2048,128]{1,0:T(8,128)(2,1)S(1)}, u32[]{:S(2)}, u32[]{:S(2)}) collective-permute-start(bf16[2048,128]{1,0:T(8,128)(2,1)S(1)} %compact.1.own), channel_id=1, source_target_pairs={{0,4},{4,0},{8,12},{12,8},{16,20},{20,16},{24,28},{28,24},{32,36},... | collective-permute-start | bytes 1572872 | tf_op jit(solution)/shard_map/ppermute | solution.py:31
  11.8 1.9 collective-permute-start.2
  13.7 1.9 collective-permute-start.1
  15.6 2.2 inverse.1
  17.9 9.8 %solve.2.first = bf16[2048,128]{1,0:T(8,128)(2,1)S(1)} custom-call(bf16[2048,128]{1,0:T(8,128)(2,1)S(1)} %compact.1.own, bf16[2048,128]{1,0:T(8,128)(2,1)S(1)} %collective-permute-done.other, bf16[256,128]{1,0:T(8,128)(2,1)S(1)} %copy-done.1, bf16[128,128]{1,0:T(8,128)(2,1)S(1)} %copy-done.4, bf16[64,192]{1,0:T(8,128)(2,1)S(1)} %copy-done.3, ...), custom_call_target="tpu_custom_call" | custom-call | tf_op jit(solution)/shard_map/solve/pallas_call | solution.py:203
  27.7 5.5 %collective-permute-done.2.other = bf16[2048,128]{1,0:T(8,128)(2,1)S(1)} collective-permute-done((bf16[2048,128]{1,0:T(8,128)(2,1)S(1)}, bf16[2048,128]{1,0:T(8,128)(2,1)S(1)}, u32[]{:S(2)}, u32[]{:S(2)}) %collective-permute-start.2) | collective-permute-done | bytes 524320 | tf_op jit(solution)/shard_map/ppermute | solution.py:31
  33.1 9.8 %solve.3.second = bf16[2048,128]{1,0:T(8,128)(2,1)S(1)} custom-call(bf16[2048,128]{1,0:T(8,128)(2,1)S(1)} %compact.1.own, bf16[2048,128]{1,0:T(8,128)(2,1)S(1)} %collective-permute-done.2.other, bf16[256,128]{1,0:T(8,128)(2,1)S(1)} %copy-done.1, bf16[128,128]{1,0:T(8,128)(2,1)S(1)} %copy-done.4, bf16[64,192]{1,0:T(8,128)(2,1)S(1)} %copy-done.3, ...), custom_call_target="tpu_custom_call" | custom-call | tf_op jit(solution)/shard_map/solve/pallas_call | solution.py:203
  43.0 11.2 %last.1 = bf16[16,4,32,128]{3,2,1,0:T(8,128)(2,1)} custom-call(s32[1,3]{1,0:T(1,128)S(1)} %copy-done.5, bf16[2048,128]{1,0:T(8,128)(2,1)S(1)} %compact.1.own, bf16[2048,128]{1,0:T(8,128)(2,1)S(1)} %collective-permute-done.1.other, bf16[256,128]{1,0:T(8,128)(2,1)S(1)} %copy-done.1, bf16[128,128]{1,0:T(8,128)(2,1)S(1)} %copy-done.4, ...), custom_call_target="tpu_custom_call" | custom-call | tf_op jit(solution)/shard_map/last/pallas_call | solution.py:213
  54.1 12.2 %all-to-all-start.2 = ((bf16[16,128,128]{2,1,0:T(8,128)(2,1)}), bf16[16,128,128]{2,1,0:T(8,128)(2,1)S(1)}, u32[]{:S(2)}, u32[]{:S(2)}) async-start(bf16[16,128,128]{2,1,0:T(8,128)(2,1)} %bitcast.4), calls=%async_computation.2 | async-start | bytes 1048576 | tf_op jit(solution)/shard_map/all_to_all | solution.py:237
  66.4 0.9 copy.9
  67.2 22.3 %all-to-all-done.2.value = bf16[16,128,128]{2,1,0:T(8,128)(2,1)S(1)} async-done(((bf16[16,128,128]{2,1,0:T(8,128)(2,1)}), bf16[16,128,128]{2,1,0:T(8,128)(2,1)S(1)}, u32[]{:S(2)}, u32[]{:S(2)}) %all-to-all-start.2) | async-done | bytes 524320 | tf_op jit(solution)/shard_map/all_to_all | solution.py:237
  89.5 12.1 %all-to-all-start = ((bf16[16,128,128]{2,1,0:T(8,128)(2,1)}), bf16[16,128,128]{2,1,0:T(8,128)(2,1)S(1)}, u32[]{:S(2)}, u32[]{:S(2)}) async-start(bf16[16,128,128]{2,1,0:T(8,128)(2,1)} %bitcast.3), calls=%async_computation | async-start | bytes 1048576 | tf_op jit(solution)/shard_map/all_to_all | solution.py:237
  101.6 1.0 turn.3
  102.5 22.1 %all-to-all-done.value = bf16[16,128,128]{2,1,0:T(8,128)(2,1)S(1)} async-done(((bf16[16,128,128]{2,1,0:T(8,128)(2,1)}), bf16[16,128,128]{2,1,0:T(8,128)(2,1)S(1)}, u32[]{:S(2)}, u32[]{:S(2)}) %all-to-all-start) | async-done | bytes 524320 | tf_op jit(solution)/shard_map/all_to_all | solution.py:237
  124.7 14.1 %all-to-all-start.3 = ((bf16[32,64,128]{2,1,0:T(8,128)(2,1)}), bf16[32,64,128]{2,1,0:T(8,128)(2,1)S(1)}, u32[]{:S(2)}, u32[]{:S(2)}) async-start(bf16[32,64,128]{2,1,0:T(8,128)(2,1)} %turn.3), calls=%async_computation.3 | async-start | bytes 1048576 | tf_op jit(solution)/shard_map/all_to_all | solution.py:237
  138.9 11.3 %all-to-all-done.3.applied = bf16[32,64,128]{2,1,0:T(8,128)(2,1)S(1)} async-done(((bf16[32,64,128]{2,1,0:T(8,128)(2,1)}), bf16[32,64,128]{2,1,0:T(8,128)(2,1)S(1)}, u32[]{:S(2)}, u32[]{:S(2)}) %all-to-all-start.3) | async-done | bytes 524320 | tf_op jit(solution)/shard_map/all_to_all | solution.py:237
  150.2 15.5 %all_to_all.40.phi = bf16[32,64,128]{2,1,0:T(8,128)(2,1)S(1)} all-to-all(bf16[32,64,128]{2,1,0:T(8,128)(2,1)S(1)} %turn.2), channel_id=1, replica_groups=mesh['band_0'=4,'band_1'=16,'band_2'=2,'pair'=4] {'band_0','band_2','pair'}, dimensions={0} | all-to-all | bytes 1048576 | tf_op jit(solution)/shard_map/all_to_all | solution.py:237
  166.2 20.1 %all_to_all.41 = f32[32,16,512]{2,1,0:T(8,128)S(1)} all-to-all(f32[32,16,512]{2,1,0:T(8,128)S(1)} %bitcast.14), channel_id=1, replica_groups=mesh['band_0'=4,'band_1'=16,'band_2'=2,'pair'=4] {'band_0','band_2','pair'}, dimensions={0} | all-to-all | bytes 2097152 | tf_op jit(solution)/shard_map/all_to_all | solution.py:237
  186.4 17.3 %all_to_all.42 = f32[16,4,128]{2,1,0:T(4,128)S(1)} all-to-all(f32[16,4,128]{2,1,0:T(4,128)S(1)} %reshape.29), channel_id=1, replica_groups=mesh['band_0'=4,'band_1'=16,'band_2'=2,'pair'=4] {'band_1'}, dimensions={0} | all-to-all | bytes 65536 | tf_op jit(solution)/shard_map/all_to_all | solution.py:237
  203.7 14.0 %all_to_all.43 = f32[16,4,128]{2,1,0:T(4,128)S(1)} all-to-all(f32[16,4,128]{2,1,0:T(4,128)S(1)} %broadcast_in_dim.6), channel_id=1, replica_groups=mesh['band_0'=4,'band_1'=16,'band_2'=2,'pair'=4] {'band_1'}, dimensions={0} | all-to-all | bytes 65536 | tf_op jit(solution)/shard_map/all_to_all | solution.py:237
  217.8 23.7 %all_to_all.44 = f32[32,16,512]{2,1,0:T(8,128)S(1)} all-to-all(f32[32,16,512]{2,1,0:T(8,128)S(1)} %broadcast_in_dim.7), channel_id=1, replica_groups=mesh['band_0'=4,'band_1'=16,'band_2'=2,'pair'=4] {'band_0','band_2','pair'}, dimensions={0} | all-to-all | bytes 2097152 | tf_op jit(solution)/shard_map/all_to_all | solution.py:237
  241.4 1.8 project.1
  (21 shorter events, 0.9 us)
Async XLA Ops:
  0.0 1.2 copy-start
  2.8 15.0 %copy-start.1 = (bf16[256,128]{1,0:T(8,128)(2,1)S(1)}, bf16[256,128]{1,0:T(8,128)(2,1)}, u32[]{:S(2)}) copy-start(bf16[256,128]{1,0:T(8,128)(2,1)} %constant.10.clone.z_main) | copy-start | bytes 196612
  2.9 15.0 %copy-start.2 = (bf16[64,192]{1,0:T(8,128)(2,1)S(1)}, bf16[64,192]{1,0:T(8,128)(2,1)}, u32[]{:S(2)}) copy-start(bf16[64,192]{1,0:T(8,128)(2,1)} %constant.13.clone.x_side) | copy-start | bytes 73732
  2.9 15.0 %copy-start.3 = (bf16[64,192]{1,0:T(8,128)(2,1)S(1)}, bf16[64,192]{1,0:T(8,128)(2,1)}, u32[]{:S(2)}) copy-start(bf16[64,192]{1,0:T(8,128)(2,1)} %constant.12.clone.y_side) | copy-start | bytes 73732
  2.9 15.0 %copy-start.4 = (bf16[128,128]{1,0:T(8,128)(2,1)S(1)}, bf16[128,128]{1,0:T(8,128)(2,1)}, u32[]{:S(2)}) copy-start(bf16[128,128]{1,0:T(8,128)(2,1)} %constant.11.clone.z_low) | copy-start | bytes 98308
  2.9 14.9 %collective-permute-start = (bf16[2048,128]{1,0:T(8,128)(2,1)S(1)}, bf16[2048,128]{1,0:T(8,128)(2,1)S(1)}, u32[]{:S(2)}, u32[]{:S(2)}) collective-permute-start(bf16[2048,128]{1,0:T(8,128)(2,1)S(1)} %compact.1.own), channel_id=1, source_target_pairs={{0,4},{4,0},{8,12},{12,8},{16,20},{20,16},{24,28},{28,24},{32,36},... | collective-permute-start | bytes 1572872 | tf_op jit(solution)/shard_map/ppermute | solution.py:31
  11.8 21.4 %collective-permute-start.2 = (bf16[2048,128]{1,0:T(8,128)(2,1)S(1)}, bf16[2048,128]{1,0:T(8,128)(2,1)S(1)}, u32[]{:S(2)}, u32[]{:S(2)}) collective-permute-start(bf16[2048,128]{1,0:T(8,128)(2,1)S(1)} %compact.1.own), channel_id=1, source_target_pairs={{0,8},{4,12},{8,0},{12,4},{16,24},{20,28},{24,16},{28,20},{32,40},... | collective-permute-start | bytes 1572872 | tf_op jit(solution)/shard_map/ppermute | solution.py:31
  13.7 29.2 %collective-permute-start.1 = (bf16[2048,128]{1,0:T(8,128)(2,1)S(1)}, bf16[2048,128]{1,0:T(8,128)(2,1)S(1)}, u32[]{:S(2)}, u32[]{:S(2)}) collective-permute-start(bf16[2048,128]{1,0:T(8,128)(2,1)S(1)} %compact.1.own), channel_id=1, source_target_pairs={{0,16},{4,20},{8,24},{12,28},{16,0},{20,4},{24,8},{28,12},{32,48},... | collective-permute-start | bytes 1572872 | tf_op jit(solution)/shard_map/ppermute | solution.py:31
  27.7 15.3 %copy-start.5 = (s32[1,3]{1,0:T(1,128)S(1)}, s32[1,3]{1,0:T(1,128)}, u32[]{:S(2)}) copy-start(s32[1,3]{1,0:T(1,128)} %partners.1) | copy-start | bytes 40
  54.1 35.3 %all-to-all-start.2 = ((bf16[16,128,128]{2,1,0:T(8,128)(2,1)}), bf16[16,128,128]{2,1,0:T(8,128)(2,1)S(1)}, u32[]{:S(2)}, u32[]{:S(2)}) async-start(bf16[16,128,128]{2,1,0:T(8,128)(2,1)} %bitcast.4), calls=%async_computation.2 | async-start | bytes 1048576 | tf_op jit(solution)/shard_map/all_to_all | solution.py:237
  89.5 35.2 %all-to-all-start = ((bf16[16,128,128]{2,1,0:T(8,128)(2,1)}), bf16[16,128,128]{2,1,0:T(8,128)(2,1)S(1)}, u32[]{:S(2)}, u32[]{:S(2)}) async-start(bf16[16,128,128]{2,1,0:T(8,128)(2,1)} %bitcast.3), calls=%async_computation | async-start | bytes 1048576 | tf_op jit(solution)/shard_map/all_to_all | solution.py:237
  124.7 25.5 %all-to-all-start.3 = ((bf16[32,64,128]{2,1,0:T(8,128)(2,1)}), bf16[32,64,128]{2,1,0:T(8,128)(2,1)S(1)}, u32[]{:S(2)}, u32[]{:S(2)}) async-start(bf16[32,64,128]{2,1,0:T(8,128)(2,1)} %turn.3), calls=%async_computation.3 | async-start | bytes 1048576 | tf_op jit(solution)/shard_map/all_to_all | solution.py:237

commit v2 on v1

--- a/solution.py
+++ b/solution.py
@@ -9,6 +9,7 @@
 from jax.sharding import Mesh
 from jax.sharding import PartitionSpec as P
 
+
 NG = 64
 PARTNERS = 3
 NG3 = 262144
@@ -16,8 +17,8 @@
 ROWS = NG3 // LANES
 BAND = ("band_0", "band_1", "band_2")
 BAND_PAIR = ("band_0", "band_1", "band_2", "pair")
-PLANE = ("band_0", "band_2", "pair")
-LINE = "band_1"
+ACROSS = ("band_1", "pair")
+HELD = ("band_0", "band_2")
 F32, BF16 = jnp.float32, jnp.bfloat16
 LIMIT = pltpu.CompilerParams(vmem_limit_bytes=16 * 2**20)
 
@@ -176,6 +177,40 @@
     lax.fori_loop(0, ROWS // 256, step, 0)
 
 
+def woven(first, second):
+    mask = lax.broadcasted_iota(jnp.int32, first.shape, 1) < 4
+    top = jnp.where(mask, first, pltpu.roll(second, 4, 1))
+    bottom = jnp.where(mask, pltpu.roll(first, 4, 1), second)
+    return jnp.stack([top, bottom], axis=1).reshape(-1, 8, LANES)
+
+
+def by_owner(rows):
+    tiles = rows.reshape(8, 2, 2, 8, LANES)
+    return woven(tiles[:, 0].reshape(16, 8, LANES), tiles[:, 1].reshape(16, 8, LANES))
+
+
+def place(out, n, rows):
+    start = pl.multiple_of(n // 2 * 8, 8)
+    out[pl.ds(n % 2 * 32, 32), pl.ds(start, 8), :] = by_owner(rows).astype(BF16)
+
+
+def spread_kernel(mine, out):
+    def step(n, carry):
+        place(out, n, mine[pl.ds(pl.multiple_of(n * 256, 256), 256)].astype(F32))
+        return carry
+
+    lax.fori_loop(0, ROWS // 256, step, 0)
+
+
+def spread(mine):
+    return pl.pallas_call(
+        spread_kernel,
+        out_shape=jax.ShapeDtypeStruct((64, 32, LANES), BF16),
+        name="spread",
+        compiler_params=LIMIT,
+    )(mine)
+
+
 def last_kernel(
     partners, own, other, z_main, z_low, y_side, x_side, inverse, first, second, out, field
 ):
@@ -188,7 +223,7 @@
         total = jnp.zeros((256, LANES), F32)
         for slot, value in enumerate((first[rows], second[rows], third)):
             total = total + jnp.where(partners[0, slot] >= 0, value.astype(F32), 0.0)
-        out[pl.ds(n % 2 * 8, 8), n // 2] = total.astype(BF16).reshape(8, 32, LANES)
+        place(out, n, total)
         return carry
 
     lax.fori_loop(0, ROWS // 256, step, 0)
@@ -212,7 +247,7 @@
 def solve_last(partners, own, other, parts, inverse, first, second):
     return pl.pallas_call(
         last_kernel,
-        out_shape=jax.ShapeDtypeStruct((16, 4, 32, LANES), BF16),
+        out_shape=jax.ShapeDtypeStruct((64, 32, LANES), BF16),
         in_specs=[SMEM] + [VMEM] * 9,
         scratch_shapes=[FIELD],
         name="last",
@@ -220,16 +255,17 @@
     )(partners, own, other, *parts, inverse, first, second)
 
 
-def turn_kernel(value, out):
-    for n in range(8):
-        block = jnp.transpose(value[:, 16 * n : 16 * n + 16, :], (1, 0, 2))
-        out[4 * n : 4 * n + 4] = block.reshape(4, 64, LANES)
+def turn_to(value, out):
+    for n in range(2):
+        out[16 * n : 16 * n + 16] = jnp.transpose(value[:, 16 * n : 16 * n + 16, :], (1, 0, 2))
 
 
 def turned(value):
     return pl.pallas_call(
-        turn_kernel, out_shape=jax.ShapeDtypeStruct((32, 64, LANES), BF16), name="turn",
-        compiler_params=LIMIT
+        turn_to,
+        out_shape=jax.ShapeDtypeStruct((32, 64, LANES), BF16),
+        name="turn",
+        compiler_params=LIMIT,
     )(value)
 
 
@@ -237,66 +273,116 @@
     return lax.all_to_all(value, axes, split_axis=0, concat_axis=0, tiled=True)
 
 
-def regroup(value):
-    return exchange(turned(exchange(value.reshape(16, 128, LANES), LINE)), PLANE)
-
-
-def quarter(slab, q):
-    return slab[:, 16 * q : 16 * q + 16, :].reshape(512, LANES)
-
-
-def whole(slab):
-    return jnp.concatenate([quarter(slab, q) for q in range(4)], axis=1)
-
-
-def overlap_kernel(phi, applied, out):
-    value = lax.dot_general(
-        whole(applied), whole(phi), (((1,), (1,)), ((), ())), preferred_element_type=F32
-    )
-    out[...] = value * (1.0 / NG3)
-
-
-def overlap(phi, applied):
-    return pl.pallas_call(
-        overlap_kernel, out_shape=jax.ShapeDtypeStruct((512, 512), F32), name="overlap",
-        compiler_params=LIMIT
-    )(phi, applied)
-
-
-def project_kernel(overlaps, phi, applied, out):
-    high, low = two_parts(overlaps[...])
-    cells = whole(phi)
-    value = whole(applied).astype(F32) - (dot(high, cells) + dot(low, cells))
+def two_rows(slab, n):
+    return jnp.concatenate([slab[2 * n], slab[2 * n + 1]], axis=1)
+
+
+def all_two_rows(slabs, n):
+    return jnp.concatenate([two_rows(slab, n) for slab in slabs], axis=0)
+
+
+def overlap_kernel(applied, *refs):
+    phis, (out, slab) = refs[:8], refs[8:]
+    turn_to(applied, slab)
+
+    def step(n, total):
+        return total + lax.dot_general(
+            two_rows(slab, n),
+            all_two_rows(phis, n),
+            (((1,), (1,)), ((), ())),
+            preferred_element_type=F32,
+        )
+
+    total = lax.fori_loop(0, 16, step, jnp.zeros((64, 512), F32)) * (1.0 / NG3)
+    for n in range(4):
+        out[:, n, :] = total[:, LANES * n : LANES * (n + 1)]
+
+
+def overlap(applied, phis):
+    return pl.pallas_call(
+        overlap_kernel,
+        out_shape=(
+            jax.ShapeDtypeStruct((64, 4, LANES), F32),
+            jax.ShapeDtypeStruct((32, 64, LANES), BF16),
+        ),
+        name="overlap",
+        compiler_params=LIMIT,
+    )(applied, *phis)
+
+
+def project_kernel(overlaps, slab, *refs):
+    phis, out = refs[:8], refs[8]
+    high, low = two_parts(jnp.concatenate([overlaps[:, n, :] for n in range(4)], axis=1))
+
+    def step(n, carry):
+        cells = all_two_rows(phis, n)
+        value = two_rows(slab, n).astype(F32) - (dot(high, cells) + dot(low, cells))
+        out[2 * n] = value[:, :LANES]
+        out[2 * n + 1] = value[:, LANES:]
+        return carry
+
+    lax.fori_loop(0, 16, step, 0)
+
+
+def project(overlaps, slab, phis):
+    return pl.pallas_call(
+        project_kernel,
+        out_shape=jax.ShapeDtypeStruct((32, 64, LANES), F32),
+        name="project",
+        compiler_params=LIMIT,
+    )(overlaps, slab, *phis)
+
+
+def settle_kernel(arrived, out):
     for y in range(4):
-        block = value[128 * y : 128 * y + 128].reshape(8, 16, 512)
-        out[128 * y : 128 * y + 128] = jnp.transpose(block, (1, 0, 2)).reshape(128, 512)
-
-
-def project(overlaps, phi, applied):
-    return pl.pallas_call(
-        project_kernel, out_shape=jax.ShapeDtypeStruct((512, 512), F32), name="project",
-        compiler_params=LIMIT
-    )(overlaps, phi, applied)
+        for q in range(4):
+            both = [arrived[2 * y + core, 64 * q : 64 * q + 64, :].reshape(8, 8, LANES) for core in range(2)]
+            out[128 * y : 128 * y + 128, LANES * q : LANES * (q + 1)] = woven(*both).reshape(128, LANES)
+
+
+def settle(arrived):
+    return pl.pallas_call(
+        settle_kernel,
+        out_shape=jax.ShapeDtypeStruct((512, 512), F32),
+        name="settle",
+        compiler_params=LIMIT,
+    )(arrived)
+
+
+def shifted(value, axis, distance):
+    size = lax.axis_size(axis)
+    return lax.ppermute(value, axis, [(n, (n + distance) % size) for n in range(size)])
+
+
+def gathered(slab):
+    slabs = [slab]
+    for distance in (1, 3, 2):
+        slabs.append(shifted(slab, "band_0", distance))
+    return slabs + [shifted(value, "band_2", 1) for value in slabs]
 
 
 def total_of(value):
-    arrived = exchange(value.reshape(32, 16, 512), PLANE).sum(axis=0)
-    owned = exchange(arrived.reshape(16, 4, LANES), LINE).sum(axis=0)
-    line = exchange(jnp.broadcast_to(owned, (16, 4, LANES)), LINE).reshape(16, 512)
-    return exchange(jnp.broadcast_to(line, (32, 16, 512)), PLANE).reshape(512, 512)
+    owned = exchange(value, ACROSS).sum(axis=0)
+    return exchange(jnp.broadcast_to(owned, value.shape), ACROSS)
 
 
 def on_device(orbitals, partners):
     mine = compact(orbitals)
-    others = [partner(mine, BAND, slot) for slot in range(PARTNERS)]
+    others = []
+    for slot in range(PARTNERS):
+        others.append(partner(mine, BAND, slot))
     parts = tables()
     inverse = inverse_eigen()
     first = solve(mine, others[0], parts, inverse)
+    first, others[1] = lax.optimization_barrier((first, others[1]))
     second = solve(mine, others[1], parts, inverse)
-    early, first = lax.optimization_barrier((mine, first))
-    phi = regroup(early.reshape(4, 16, 32, LANES).transpose(1, 0, 2, 3))
-    applied = regroup(solve_last(partners, mine, others[2], parts, inverse, first, second))
-    return project(total_of(overlap(phi, applied)), phi, applied)
+    applied = solve_last(partners, mine, others[2], parts, inverse, first, second)
+    phi = exchange(spread(mine), ACROSS)
+    phis = gathered(turned(phi))
+    applied = exchange(applied, ACROSS)
+    partial, slab = overlap(applied, phis)
+    gradient = project(total_of(partial), slab, phis)
+    return settle(exchange(gradient.reshape(8, 256, LANES), HELD))
 
 
 def solution(mesh):

time: 244 us -> 228 us (0.934)
  waiting for transfers between devices: 61.1 us -> 31.2 us
  starting transfers between devices: 51.1 us -> 69.7 us
  blocking collectives: 90.5 us -> 76 us
  Pallas kernels: 38 us -> 46.4 us
    all_to_all x3 -> x2, waiting for transfers between devices: 55.7 us -> 0.01 us  [exchange(): return lax.all_to_all(value, axes, split_axis=0, concat_axis=0, tiled=True)]
    ppermute x0 -> x7, starting transfers between devices: none -> 25.9 us  [shifted(): lax.ppermute(value, axis, [(n, (n + distance) % size) for n in range(size)])]
    ppermute x3, waiting for transfers between devices: 5.47 us -> 23.7 us  [partner(): return lax.ppermute(value, axis, pairs)]
    all_to_all x5 -> x3, blocking collectives: 90.5 us -> 76 us  [exchange(): return lax.all_to_all(value, axes, split_axis=0, concat_axis=0, tiled=True)]
    pallas_call x5 -> x6, Pallas kernels: 14.6 us -> 23 us  [the longest x1 11.2 us: solve_last(): pl.pallas_call(last_kernel, out_shape=jax.ShapeDtypeStruct((64, 32, LANES...]
    ppermute x0 -> x7, waiting for transfers between devices: none -> 7.48 us  [shifted(): lax.ppermute(value, axis, [(n, (n + distance) % size) for n in range(size)])]
    all_to_all x3 -> x2, starting transfers between devices: 38.4 us -> 33.6 us  [exchange(): return lax.all_to_all(value, axes, split_axis=0, concat_axis=0, tiled=True)]
    ppermute x3, starting transfers between devices: 12.7 us -> 10.2 us  [partner(): return lax.ppermute(value, axis, pairs)]
  transfers between devices with their start and end apart: 6 -> 12, of which waited for: 4 -> 4; matrix products, arithmetic and copies ran while one was open for 0% -> 0% of each run, Pallas kernels for 9% -> 15%
where the time goes in v2:
time: 228 us; the launch traced here: 227 us
  blocking collectives  76 us (33%)
  starting transfers between devices  69.7 us (31%)
  Pallas kernels  46.4 us (20%)
  waiting for transfers between devices  31.2 us (14%)
  local copies, waits for them, and re-layouts  3.11 us (1%)
    all_to_all x3, blocking collectives, exchange(): return lax.all_to_all(value, axes, split_axis=0, concat_axis=0, tiled=True)  76 us
    all_to_all x2, starting transfers between devices, exchange(): return lax.all_to_all(value, axes, split_axis=0, concat_axis=0, tiled=True)  33.6 us
    ppermute x7, starting transfers between devices, shifted(): lax.ppermute(value, axis, [(n, (n + distance) % size) for n in range(size)])  25.9 us
    ppermute x3, waiting for transfers between devices, partner(): return lax.ppermute(value, axis, pairs)  23.7 us
    pallas_call x2, Pallas kernels, solve(): pl.pallas_call(solve_kernel, out_shape=jax.ShapeDtypeStruct((ROWS, LANES)...  19.6 us
    pallas_call x1, Pallas kernels, solve_last(): pl.pallas_call(last_kernel, out_shape=jax.ShapeDtypeStruct((64, 32, LANES...  11.2 us
    ppermute x3, starting transfers between devices, partner(): return lax.ppermute(value, axis, pairs)  10.2 us
    ppermute x7, waiting for transfers between devices, shifted(): lax.ppermute(value, axis, [(n, (n + distance) % size) for n in range(size)])  7.48 us
  transfers between devices with their start and end apart: 12, of which 4 were waited for; matrix products, arithmetic and copies ran while one was open for 0% of the time, Pallas kernels for 15%

profile of v2, /device:TPU:1, one launch (start us, length us, event | category | flops | bytes accessed | tf_op | source)
XLA Modules:
  0.0 226.7 jit_solution(3245524846692782131)
XLA Ops:
  1.2 1.6 compact.1.own.mine
  3.8 19.1 %all-to-all-start.1 = ((bf16[64,32,128]{2,1,0:T(8,128)(2,1)}), bf16[64,32,128]{2,1,0:T(8,128)(2,1)S(1)}, u32[]{:S(2)}, u32[]{:S(2)}) async-start(bf16[64,32,128]{2,1,0:T(8,128)(2,1)} %spread.1), calls=%async_computation.1 | async-start | bytes 1048576 | tf_op jit(solution)/shard_map/all_to_all | solution.py:273
  23.0 3.0 %collective-permute-start.1 = (bf16[2048,128]{1,0:T(8,128)(2,1)S(1)}, bf16[2048,128]{1,0:T(8,128)(2,1)S(1)}, u32[]{:S(2)}, u32[]{:S(2)}) collective-permute-start(bf16[2048,128]{1,0:T(8,128)(2,1)S(1)} %compact.1.own.mine), channel_id=1, source_target_pairs={{0,4},{4,0},{8,12},{12,8},{16,20},{20,16},{24,28},{28,24},{32,36},... | collective-permute-start | bytes 1572872 | tf_op jit(solution)/shard_map/ppermute | solution.py:32
  26.0 3.2 %collective-permute-start.2 = (bf16[2048,128]{1,0:T(8,128)(2,1)S(1)}, bf16[2048,128]{1,0:T(8,128)(2,1)S(1)}, u32[]{:S(2)}, u32[]{:S(2)}) collective-permute-start(bf16[2048,128]{1,0:T(8,128)(2,1)S(1)} %compact.1.own.mine), channel_id=1, source_target_pairs={{0,8},{4,12},{8,0},{12,4},{16,24},{20,28},{24,16},{28,20},{32,40},... | collective-permute-start | bytes 1572872 | tf_op jit(solution)/shard_map/ppermute | solution.py:32
  29.2 4.0 %collective-permute-start = (bf16[2048,128]{1,0:T(8,128)(2,1)S(1)}, bf16[2048,128]{1,0:T(8,128)(2,1)S(1)}, u32[]{:S(2)}, u32[]{:S(2)}) collective-permute-start(bf16[2048,128]{1,0:T(8,128)(2,1)S(1)} %compact.1.own.mine), channel_id=1, source_target_pairs={{0,16},{4,20},{8,24},{12,28},{16,0},{20,4},{24,8},{28,12},{32,48},... | collective-permute-start | bytes 1572872 | tf_op jit(solution)/shard_map/ppermute | solution.py:32
  33.2 2.2 inverse.1
  35.4 9.8 %solve.2.first = bf16[2048,128]{1,0:T(8,128)(2,1)S(1)} custom-call(bf16[2048,128]{1,0:T(8,128)(2,1)S(1)} %compact.1.own.mine, bf16[2048,128]{1,0:T(8,128)(2,1)S(1)} %collective-permute-done.1.other, bf16[256,128]{1,0:T(8,128)(2,1)S(1)} %copy-done.1, bf16[128,128]{1,0:T(8,128)(2,1)S(1)} %copy-done.4, bf16[64,192]{1,0:T(8,128)(2,1)S(1)} %copy-done.5, ...), custom_call_target="tpu_custom_call" | custom-call | tf_op jit(solution)/shard_map/solve/pallas_call | solution.py:238
  45.2 23.7 %collective-permute-done.2.other = bf16[2048,128]{1,0:T(8,128)(2,1)S(1)} collective-permute-done((bf16[2048,128]{1,0:T(8,128)(2,1)S(1)}, bf16[2048,128]{1,0:T(8,128)(2,1)S(1)}, u32[]{:S(2)}, u32[]{:S(2)}) %collective-permute-start.2) | collective-permute-done | bytes 524320 | tf_op jit(solution)/shard_map/ppermute | solution.py:32
  69.0 9.8 %solve.3.second = bf16[2048,128]{1,0:T(8,128)(2,1)S(1)} custom-call(bf16[2048,128]{1,0:T(8,128)(2,1)S(1)} %compact.1.own.mine, bf16[2048,128]{1,0:T(8,128)(2,1)S(1)} %collective-permute-done.2.other, bf16[256,128]{1,0:T(8,128)(2,1)S(1)} %copy-done.1, bf16[128,128]{1,0:T(8,128)(2,1)S(1)} %copy-done.4, bf16[64,192]{1,0:T(8,128)(2,1)S(1)} %copy-done.5, ...), custom_call_target="tpu_custom_call" | custom-call | tf_op jit(solution)/shard_map/solve/pallas_call | solution.py:238
  78.8 11.2 %last.1 = bf16[64,32,128]{2,1,0:T(8,128)(2,1)} custom-call(s32[1,3]{1,0:T(1,128)S(1)} %copy-done.7, bf16[2048,128]{1,0:T(8,128)(2,1)S(1)} %compact.1.own.mine, bf16[2048,128]{1,0:T(8,128)(2,1)S(1)} %collective-permute-done.other, bf16[256,128]{1,0:T(8,128)(2,1)S(1)} %copy-done.1, bf16[128,128]{1,0:T(8,128)(2,1)S(1)} %copy-done.4, ...), custom_call_target="tpu_custom_call" | custom-call | tf_op jit(solution)/shard_map/last/pallas_call | solution.py:248
  90.0 14.5 %all-to-all-start = ((bf16[64,32,128]{2,1,0:T(8,128)(2,1)}), bf16[64,32,128]{2,1,0:T(8,128)(2,1)}, u32[]{:S(2)}, u32[]{:S(2)}) async-start(bf16[64,32,128]{2,1,0:T(8,128)(2,1)} %last.1), calls=%async_computation | async-start | bytes 1048576 | tf_op jit(solution)/shard_map/all_to_all | solution.py:273
  104.6 3.2 %collective-permute-start.3 = (bf16[32,64,128]{2,1,0:T(8,128)(2,1)S(1)}, bf16[32,64,128]{2,1,0:T(8,128)(2,1)S(1)}, u32[]{:S(2)}, u32[]{:S(2)}) collective-permute-start(bf16[32,64,128]{2,1,0:T(8,128)(2,1)S(1)} %turn.1.refs_0_), channel_id=1, source_target_pairs={{0,128},{128,256},{256,384},{384,0},{1,129},{129,257},{257,385},{3... | collective-permute-start | bytes 1572872 | tf_op jit(solution)/shard_map/ppermute | solution.py:354
  107.9 3.4 %collective-permute-start.4 = (bf16[32,64,128]{2,1,0:T(8,128)(2,1)S(1)}, bf16[32,64,128]{2,1,0:T(8,128)(2,1)S(1)}, u32[]{:S(2)}, u32[]{:S(2)}) collective-permute-start(bf16[32,64,128]{2,1,0:T(8,128)(2,1)S(1)} %turn.1.refs_0_), channel_id=1, source_target_pairs={{0,384},{128,0},{256,128},{384,256},{1,385},{129,1},{257,129},{385... | collective-permute-start | bytes 1572872 | tf_op jit(solution)/shard_map/ppermute | solution.py:354
  111.2 3.5 %collective-permute-start.5 = (bf16[32,64,128]{2,1,0:T(8,128)(2,1)S(1)}, bf16[32,64,128]{2,1,0:T(8,128)(2,1)S(1)}, u32[]{:S(2)}, u32[]{:S(2)}) collective-permute-start(bf16[32,64,128]{2,1,0:T(8,128)(2,1)S(1)} %turn.1.refs_0_), channel_id=1, source_target_pairs={{0,256},{128,384},{256,0},{384,128},{1,257},{129,385},{257,1},{385... | collective-permute-start | bytes 1572872 | tf_op jit(solution)/shard_map/ppermute | solution.py:354
  114.8 4.0 %collective-permute-start.6 = (bf16[32,64,128]{2,1,0:T(8,128)(2,1)S(1)}, bf16[32,64,128]{2,1,0:T(8,128)(2,1)S(1)}, u32[]{:S(2)}, u32[]{:S(2)}) collective-permute-start(bf16[32,64,128]{2,1,0:T(8,128)(2,1)S(1)} %turn.1.refs_0_), channel_id=1, source_target_pairs={{0,4},{4,0},{1,5},{5,1},{2,6},{6,2},{3,7},{7,3},{8,12},{12,8},{9,1... | collective-permute-start | bytes 1572872 | tf_op jit(solution)/shard_map/ppermute | solution.py:354
  120.2 4.4 %collective-permute-start.7 = (bf16[32,64,128]{2,1,0:T(8,128)(2,1)S(1)}, bf16[32,64,128]{2,1,0:T(8,128)(2,1)S(1)}, u32[]{:S(2)}, u32[]{:S(2)}) collective-permute-start(bf16[32,64,128]{2,1,0:T(8,128)(2,1)S(1)} %collective-permute-done.3.refs_1_), channel_id=1, source_target_pairs={{0,4},{4,0},{1,5},{5,1},{2,6},{6,2},{3,7},{7,3},{8,12},{12,8},{9,1... | collective-permute-start | bytes 1572872 | tf_op jit(solution)/shard_map/ppermute | solution.py:354
  124.6 3.4 %collective-permute-start.8 = (bf16[32,64,128]{2,1,0:T(8,128)(2,1)S(1)}, bf16[32,64,128]{2,1,0:T(8,128)(2,1)}, u32[]{:S(2)}, u32[]{:S(2)}) collective-permute-start(bf16[32,64,128]{2,1,0:T(8,128)(2,1)S(1)} %collective-permute-done.4.refs_2_), channel_id=1, source_target_pairs={{0,4},{4,0},{1,5},{5,1},{2,6},{6,2},{3,7},{7,3},{8,12},{12,8},{9,1... | collective-permute-start | bytes 1572872 | tf_op jit(solution)/shard_map/ppermute | solution.py:354
  128.0 4.5 %collective-permute-done.5.refs_3_ = bf16[32,64,128]{2,1,0:T(8,128)(2,1)S(1)} collective-permute-done((bf16[32,64,128]{2,1,0:T(8,128)(2,1)S(1)}, bf16[32,64,128]{2,1,0:T(8,128)(2,1)S(1)}, u32[]{:S(2)}, u32[]{:S(2)}) %collective-permute-start.5) | collective-permute-done | bytes 524320 | tf_op jit(solution)/shard_map/ppermute | solution.py:354
  132.5 3.9 %collective-permute-start.9 = (bf16[32,64,128]{2,1,0:T(8,128)(2,1)S(1)}, bf16[32,64,128]{2,1,0:T(8,128)(2,1)}, u32[]{:S(2)}, u32[]{:S(2)}) collective-permute-start(bf16[32,64,128]{2,1,0:T(8,128)(2,1)S(1)} %collective-permute-done.5.refs_3_), channel_id=1, source_target_pairs={{0,4},{4,0},{1,5},{5,1},{2,6},{6,2},{3,7},{7,3},{8,12},{12,8},{9,1... | collective-permute-start | bytes 1572872 | tf_op jit(solution)/shard_map/ppermute | solution.py:354
  138.1 5.0 %overlap.1 = (f32[64,4,128]{2,1,0:T(4,128)S(1)}, bf16[32,64,128]{2,1,0:T(8,128)(2,1)S(1)}) custom-call(bf16[64,32,128]{2,1,0:T(8,128)(2,1)} %all-to-all-done.applied, bf16[32,64,128]{2,1,0:T(8,128)(2,1)S(1)} %turn.1.refs_0_, bf16[32,64,128]{2,1,0:T(8,128)(2,1)S(1)} %collective-permute-done.3.refs_1_, ...), custom_call_target="tpu_custom_call" | custom-call | tf_op jit(solution)/shard_map/overlap/pallas_call | solution.py:302
  143.9 29.4 %all_to_all.25 = f32[64,4,128]{2,1,0:T(4,128)S(1)} all-to-all(f32[64,4,128]{2,1,0:T(4,128)S(1)} %get-tuple-element.11), channel_id=1, replica_groups=mesh['band_0'=4,'band_1'=16,'band_2'=2,'pair'=4] {'band_1','pair'}, dimensions={0} | all-to-all | bytes 262144 | tf_op jit(solution)/shard_map/all_to_all | solution.py:273
  173.4 21.3 %all_to_all.26.overlaps = f32[64,4,128]{2,1,0:T(4,128)S(1)} all-to-all(f32[64,4,128]{2,1,0:T(4,128)S(1)} %broadcast_in_dim.3), channel_id=1, replica_groups=mesh['band_0'=4,'band_1'=16,'band_2'=2,'pair'=4] {'band_1','pair'}, dimensions={0} | all-to-all | bytes 262144 | tf_op jit(solution)/shard_map/all_to_all | solution.py:273
  195.7 4.6 %project.1 = f32[32,64,128]{2,1,0:T(8,128)S(1)} custom-call(f32[64,4,128]{2,1,0:T(4,128)S(1)} %all_to_all.26.overlaps, bf16[32,64,128]{2,1,0:T(8,128)(2,1)S(1)} %copy-done.3, bf16[32,64,128]{2,1,0:T(8,128)(2,1)S(1)} %turn.1.refs_0_, bf16[32,64,128]{2,1,0:T(8,128)(2,1)S(1)} %collective-permute-done.3.refs_1_, ...), custom_call_target="tpu_custom_call" | custom-call | tf_op jit(solution)/shard_map/project/pallas_call | solution.py:328
  200.4 25.3 %all_to_all.27.arrived = f32[8,256,128]{2,1,0:T(8,128)S(1)} all-to-all(f32[8,256,128]{2,1,0:T(8,128)S(1)} %bitcast.2), channel_id=1, replica_groups=mesh['band_0'=4,'band_1'=16,'band_2'=2,'pair'=4] {'band_0','band_2'}, dimensions={0} | all-to-all | bytes 2097152 | tf_op jit(solution)/shard_map/all_to_all | solution.py:273
  (31 shorter events, 8.4 us)
Async XLA Ops:
  0.0 1.2 copy-start
  3.8 86.2 %all-to-all-start.1 = ((bf16[64,32,128]{2,1,0:T(8,128)(2,1)}), bf16[64,32,128]{2,1,0:T(8,128)(2,1)S(1)}, u32[]{:S(2)}, u32[]{:S(2)}) async-start(bf16[64,32,128]{2,1,0:T(8,128)(2,1)} %spread.1), calls=%async_computation.1 | async-start | bytes 1048576 | tf_op jit(solution)/shard_map/all_to_all | solution.py:273
  22.9 12.5 %copy-start.1 = (bf16[256,128]{1,0:T(8,128)(2,1)S(1)}, bf16[256,128]{1,0:T(8,128)(2,1)}, u32[]{:S(2)}) copy-start(bf16[256,128]{1,0:T(8,128)(2,1)} %constant.10.clone.z_main) | copy-start | bytes 196612
  22.9 12.5 %copy-start.4 = (bf16[128,128]{1,0:T(8,128)(2,1)S(1)}, bf16[128,128]{1,0:T(8,128)(2,1)}, u32[]{:S(2)}) copy-start(bf16[128,128]{1,0:T(8,128)(2,1)} %constant.11.clone.z_low) | copy-start | bytes 98308
  22.9 12.5 %copy-start.5 = (bf16[64,192]{1,0:T(8,128)(2,1)S(1)}, bf16[64,192]{1,0:T(8,128)(2,1)}, u32[]{:S(2)}) copy-start(bf16[64,192]{1,0:T(8,128)(2,1)} %constant.12.clone.y_side) | copy-start | bytes 73732
  23.0 12.4 %copy-start.6 = (bf16[64,192]{1,0:T(8,128)(2,1)S(1)}, bf16[64,192]{1,0:T(8,128)(2,1)}, u32[]{:S(2)}) copy-start(bf16[64,192]{1,0:T(8,128)(2,1)} %constant.13.clone.x_side) | copy-start | bytes 73732
  23.0 12.4 %collective-permute-start.1 = (bf16[2048,128]{1,0:T(8,128)(2,1)S(1)}, bf16[2048,128]{1,0:T(8,128)(2,1)S(1)}, u32[]{:S(2)}, u32[]{:S(2)}) collective-permute-start(bf16[2048,128]{1,0:T(8,128)(2,1)S(1)} %compact.1.own.mine), channel_id=1, source_target_pairs={{0,4},{4,0},{8,12},{12,8},{16,20},{20,16},{24,28},{28,24},{32,36},... | collective-permute-start | bytes 1572872 | tf_op jit(solution)/shard_map/ppermute | solution.py:32
  26.0 43.0 %collective-permute-start.2 = (bf16[2048,128]{1,0:T(8,128)(2,1)S(1)}, bf16[2048,128]{1,0:T(8,128)(2,1)S(1)}, u32[]{:S(2)}, u32[]{:S(2)}) collective-permute-start(bf16[2048,128]{1,0:T(8,128)(2,1)S(1)} %compact.1.own.mine), channel_id=1, source_target_pairs={{0,8},{4,12},{8,0},{12,4},{16,24},{20,28},{24,16},{28,20},{32,40},... | collective-permute-start | bytes 1572872 | tf_op jit(solution)/shard_map/ppermute | solution.py:32
  29.2 49.6 %collective-permute-start = (bf16[2048,128]{1,0:T(8,128)(2,1)S(1)}, bf16[2048,128]{1,0:T(8,128)(2,1)S(1)}, u32[]{:S(2)}, u32[]{:S(2)}) collective-permute-start(bf16[2048,128]{1,0:T(8,128)(2,1)S(1)} %compact.1.own.mine), channel_id=1, source_target_pairs={{0,16},{4,20},{8,24},{12,28},{16,0},{20,4},{24,8},{28,12},{32,48},... | collective-permute-start | bytes 1572872 | tf_op jit(solution)/shard_map/ppermute | solution.py:32
  45.2 33.6 %copy-start.7 = (s32[1,3]{1,0:T(1,128)S(1)}, s32[1,3]{1,0:T(1,128)}, u32[]{:S(2)}) copy-start(s32[1,3]{1,0:T(1,128)} %partners.1) | copy-start | bytes 40
  90.0 46.5 %all-to-all-start = ((bf16[64,32,128]{2,1,0:T(8,128)(2,1)}), bf16[64,32,128]{2,1,0:T(8,128)(2,1)}, u32[]{:S(2)}, u32[]{:S(2)}) async-start(bf16[64,32,128]{2,1,0:T(8,128)(2,1)} %last.1), calls=%async_computation | async-start | bytes 1048576 | tf_op jit(solution)/shard_map/all_to_all | solution.py:273
  104.6 15.5 %collective-permute-start.3 = (bf16[32,64,128]{2,1,0:T(8,128)(2,1)S(1)}, bf16[32,64,128]{2,1,0:T(8,128)(2,1)S(1)}, u32[]{:S(2)}, u32[]{:S(2)}) collective-permute-start(bf16[32,64,128]{2,1,0:T(8,128)(2,1)S(1)} %turn.1.refs_0_), channel_id=1, source_target_pairs={{0,128},{128,256},{256,384},{384,0},{1,129},{129,257},{257,385},{3... | collective-permute-start | bytes 1572872 | tf_op jit(solution)/shard_map/ppermute | solution.py:354
  107.9 16.8 %collective-permute-start.4 = (bf16[32,64,128]{2,1,0:T(8,128)(2,1)S(1)}, bf16[32,64,128]{2,1,0:T(8,128)(2,1)S(1)}, u32[]{:S(2)}, u32[]{:S(2)}) collective-permute-start(bf16[32,64,128]{2,1,0:T(8,128)(2,1)S(1)} %turn.1.refs_0_), channel_id=1, source_target_pairs={{0,384},{128,0},{256,128},{384,256},{1,385},{129,1},{257,129},{385... | collective-permute-start | bytes 1572872 | tf_op jit(solution)/shard_map/ppermute | solution.py:354
  111.2 21.3 %collective-permute-start.5 = (bf16[32,64,128]{2,1,0:T(8,128)(2,1)S(1)}, bf16[32,64,128]{2,1,0:T(8,128)(2,1)S(1)}, u32[]{:S(2)}, u32[]{:S(2)}) collective-permute-start(bf16[32,64,128]{2,1,0:T(8,128)(2,1)S(1)} %turn.1.refs_0_), channel_id=1, source_target_pairs={{0,256},{128,384},{256,0},{384,128},{1,257},{129,385},{257,1},{385... | collective-permute-start | bytes 1572872 | tf_op jit(solution)/shard_map/ppermute | solution.py:354
  114.8 21.7 %collective-permute-start.6 = (bf16[32,64,128]{2,1,0:T(8,128)(2,1)S(1)}, bf16[32,64,128]{2,1,0:T(8,128)(2,1)S(1)}, u32[]{:S(2)}, u32[]{:S(2)}) collective-permute-start(bf16[32,64,128]{2,1,0:T(8,128)(2,1)S(1)} %turn.1.refs_0_), channel_id=1, source_target_pairs={{0,4},{4,0},{1,5},{5,1},{2,6},{6,2},{3,7},{7,3},{8,12},{12,8},{9,1... | collective-permute-start | bytes 1572872 | tf_op jit(solution)/shard_map/ppermute | solution.py:354
  120.2 16.3 %collective-permute-start.7 = (bf16[32,64,128]{2,1,0:T(8,128)(2,1)S(1)}, bf16[32,64,128]{2,1,0:T(8,128)(2,1)S(1)}, u32[]{:S(2)}, u32[]{:S(2)}) collective-permute-start(bf16[32,64,128]{2,1,0:T(8,128)(2,1)S(1)} %collective-permute-done.3.refs_1_), channel_id=1, source_target_pairs={{0,4},{4,0},{1,5},{5,1},{2,6},{6,2},{3,7},{7,3},{8,12},{12,8},{9,1... | collective-permute-start | bytes 1572872 | tf_op jit(solution)/shard_map/ppermute | solution.py:354
  124.6 11.9 %collective-permute-start.8 = (bf16[32,64,128]{2,1,0:T(8,128)(2,1)S(1)}, bf16[32,64,128]{2,1,0:T(8,128)(2,1)}, u32[]{:S(2)}, u32[]{:S(2)}) collective-permute-start(bf16[32,64,128]{2,1,0:T(8,128)(2,1)S(1)} %collective-permute-done.4.refs_2_), channel_id=1, source_target_pairs={{0,4},{4,0},{1,5},{5,1},{2,6},{6,2},{3,7},{7,3},{8,12},{12,8},{9,1... | collective-permute-start | bytes 1572872 | tf_op jit(solution)/shard_map/ppermute | solution.py:354
  132.5 5.6 %collective-permute-start.9 = (bf16[32,64,128]{2,1,0:T(8,128)(2,1)S(1)}, bf16[32,64,128]{2,1,0:T(8,128)(2,1)}, u32[]{:S(2)}, u32[]{:S(2)}) collective-permute-start(bf16[32,64,128]{2,1,0:T(8,128)(2,1)S(1)} %collective-permute-done.5.refs_3_), channel_id=1, source_target_pairs={{0,4},{4,0},{1,5},{5,1},{2,6},{6,2},{3,7},{7,3},{8,12},{12,8},{9,1... | collective-permute-start | bytes 1572872 | tf_op jit(solution)/shard_map/ppermute | solution.py:354
  143.1 0.8 copy-start.2
  194.7 1.0 copy-start.3

commit v3 on v2

--- a/solution.py
+++ b/solution.py
@@ -15,10 +15,10 @@
 NG3 = 262144
 LANES = 128
 ROWS = NG3 // LANES
-BAND = ("band_0", "band_1", "band_2")
-BAND_PAIR = ("band_0", "band_1", "band_2", "pair")
-ACROSS = ("band_1", "pair")
-HELD = ("band_0", "band_2")
+BAND = ("y_high", "y_low", "z", "core")
+BAND_PAIR = BAND + ("x_high", "x_low")
+ACROSS = ("y_high", "x_high", "z")
+HELD = ("y_low", "core", "x_low")
 F32, BF16 = jnp.float32, jnp.bfloat16
 LIMIT = pltpu.CompilerParams(vmem_limit_bytes=16 * 2**20)
 
@@ -134,7 +134,7 @@
                 field[pl.ds(n * 8 + 4 * pair + 2 * m, 2)] = slab.reshape(2, 32, LANES)
         return carry
 
-    lax.fori_loop(0, ROWS // 256, step, 0)
+    lax.fori_loop(0, ROWS // 256, step, 0, unroll=2)
 
 
 def middle_part(x_side, inverse, field):
@@ -151,7 +151,7 @@
         field[:, group, :] = jnp.transpose(jnp.stack(outs, axis=0), (1, 0, 2))
         return carry
 
-    lax.fori_loop(0, 4, step, 0)
+    lax.fori_loop(0, 4, step, 0, unroll=2)
 
 
 def backward_block(n, other, z_main, z_low, y_side, field, mask):
@@ -174,32 +174,24 @@
         term[rows] = value
         return carry
 
-    lax.fori_loop(0, ROWS // 256, step, 0)
-
-
-def woven(first, second):
-    mask = lax.broadcasted_iota(jnp.int32, first.shape, 1) < 4
-    top = jnp.where(mask, first, pltpu.roll(second, 4, 1))
-    bottom = jnp.where(mask, pltpu.roll(first, 4, 1), second)
-    return jnp.stack([top, bottom], axis=1).reshape(-1, 8, LANES)
-
-
-def by_owner(rows):
-    tiles = rows.reshape(8, 2, 2, 8, LANES)
-    return woven(tiles[:, 0].reshape(16, 8, LANES), tiles[:, 1].reshape(16, 8, LANES))
+    lax.fori_loop(0, ROWS // 256, step, 0, unroll=2)
 
 
 def place(out, n, rows):
-    start = pl.multiple_of(n // 2 * 8, 8)
-    out[pl.ds(n % 2 * 32, 32), pl.ds(start, 8), :] = by_owner(rows).astype(BF16)
+    tiles = rows.astype(BF16).reshape(8, 2, 2, 8, LANES)
+    for core in range(2):
+        start = pl.multiple_of((n // 2 % 2 * 2 + core) * 8, 8)
+        for x_high in range(2):
+            owner = (n // 4 * 2 + x_high) * 16 + n % 2 * 8
+            out[pl.ds(owner, 8), pl.ds(start, 8), :] = tiles[:, core, x_high]
 
 
 def spread_kernel(mine, out):
     def step(n, carry):
-        place(out, n, mine[pl.ds(pl.multiple_of(n * 256, 256), 256)].astype(F32))
-        return carry
-
-    lax.fori_loop(0, ROWS // 256, step, 0)
+        place(out, n, mine[pl.ds(pl.multiple_of(n * 256, 256), 256)])
+        return carry
+
+    lax.fori_loop(0, ROWS // 256, step, 0, unroll=2)
 
 
 def spread(mine):
@@ -226,7 +218,7 @@
         place(out, n, total)
         return carry
 
-    lax.fori_loop(0, ROWS // 256, step, 0)
+    lax.fori_loop(0, ROWS // 256, step, 0, unroll=2)
 
 
 FIELD = pltpu.VMEM((NG, NG // 2, LANES), F32)
@@ -293,7 +285,7 @@
             preferred_element_type=F32,
         )
 
-    total = lax.fori_loop(0, 16, step, jnp.zeros((64, 512), F32)) * (1.0 / NG3)
+    total = lax.fori_loop(0, 16, step, jnp.zeros((64, 512), F32), unroll=4) * (1.0 / NG3)
     for n in range(4):
         out[:, n, :] = total[:, LANES * n : LANES * (n + 1)]
 
@@ -312,16 +304,18 @@
 
 def project_kernel(overlaps, slab, *refs):
     phis, out = refs[:8], refs[8]
-    high, low = two_parts(jnp.concatenate([overlaps[:, n, :] for n in range(4)], axis=1))
-
-    def step(n, carry):
-        cells = all_two_rows(phis, n)
-        value = two_rows(slab, n).astype(F32) - (dot(high, cells) + dot(low, cells))
+    parts = jnp.concatenate(
+        two_parts(jnp.concatenate([overlaps[:, n, :] for n in range(4)], axis=1)), axis=0
+    )
+
+    def step(n, carry):
+        both = dot(parts, all_two_rows(phis, n))
+        value = two_rows(slab, n).astype(F32) - (both[:64] + both[64:])
         out[2 * n] = value[:, :LANES]
         out[2 * n + 1] = value[:, LANES:]
         return carry
 
-    lax.fori_loop(0, 16, step, 0)
+    lax.fori_loop(0, 16, step, 0, unroll=4)
 
 
 def project(overlaps, slab, phis):
@@ -336,8 +330,13 @@
 def settle_kernel(arrived, out):
     for y in range(4):
         for q in range(4):
-            both = [arrived[2 * y + core, 64 * q : 64 * q + 64, :].reshape(8, 8, LANES) for core in range(2)]
-            out[128 * y : 128 * y + 128, LANES * q : LANES * (q + 1)] = woven(*both).reshape(128, LANES)
+            lines = []
+            for core in range(2):
+                for x in range(4):
+                    start = 64 * q + 32 * (y // 2) + 16 * (x // 2)
+                    lines.append(arrived[4 * (y % 2) + 2 * core + x % 2, start : start + 16, :])
+            rows = jnp.transpose(jnp.stack(lines, axis=0), (1, 0, 2)).reshape(128, LANES)
+            out[128 * y : 128 * y + 128, LANES * q : LANES * (q + 1)] = rows
 
 
 def settle(arrived):
@@ -349,16 +348,16 @@
     )(arrived)
 
 
-def shifted(value, axis, distance):
-    size = lax.axis_size(axis)
-    return lax.ppermute(value, axis, [(n, (n + distance) % size) for n in range(size)])
+def flipped(value, axes, mask):
+    size = lax.axis_size(axes)
+    return lax.ppermute(value, axes, [(n, n ^ mask) for n in range(size)])
 
 
 def gathered(slab):
     slabs = [slab]
-    for distance in (1, 3, 2):
-        slabs.append(shifted(slab, "band_0", distance))
-    return slabs + [shifted(value, "band_2", 1) for value in slabs]
+    for mask in (1, 2, 3):
+        slabs.append(flipped(slab, ("y_low", "x_low"), mask))
+    return slabs + [flipped(value, "core", 1) for value in slabs]
 
 
 def total_of(value):
@@ -386,9 +385,7 @@
 
 
 def solution(mesh):
-    torus = Mesh(
-        mesh.devices.reshape(4, 16, 2, mesh.shape["pair"]), ("band_0", "band_1", "band_2", "pair")
-    )
+    torus = Mesh(mesh.devices.reshape(2, 2, 16, 2, 2, 2), BAND_PAIR)
     in_specs = (P(BAND_PAIR, None), P(BAND_PAIR, None))
     out_specs = P(None, BAND_PAIR)
     return jax.shard_map(

time: 228 us -> 231 us (1.013)
  waiting for transfers between devices: 31.2 us -> 42.9 us
  Pallas kernels: 46.4 us -> 35.9 us
  starting transfers between devices: 69.7 us -> 72.8 us
    ppermute x7, waiting for transfers between devices: 7.48 us -> 16.9 us  [flipped(): return lax.ppermute(value, axes, [(n, n ^ mask) for n in range(size)])]
    all_to_all x2, starting transfers between devices: 33.6 us -> 38.9 us  [exchange(): return lax.all_to_all(value, axes, split_axis=0, concat_axis=0, tiled=True)]
    pallas_call x2, Pallas kernels: 19.6 us -> 15.1 us  [solve(): pl.pallas_call(solve_kernel, out_shape=jax.ShapeDtypeStruct((ROWS, LANES)...]
    pallas_call x1, Pallas kernels: 11.2 us -> 8.88 us  [solve_last(): pl.pallas_call(last_kernel, out_shape=jax.ShapeDtypeStruct((64, 32, LANES...]
  transfers between devices with their start and end apart: 12 -> 12, of which waited for: 4 -> 4; matrix products, arithmetic and copies ran while one was open for 0% -> 0% of each run, Pallas kernels for 15% -> 11%
where the time goes in v3:
time: 231 us; the launch traced here: 230 us
  blocking collectives  75.2 us (33%)
  starting transfers between devices  72.8 us (32%)
  waiting for transfers between devices  42.9 us (19%)
  Pallas kernels  35.9 us (16%)
  local copies, waits for them, and re-layouts  3.11 us (1%)
    all_to_all x3, blocking collectives, exchange(): return lax.all_to_all(value, axes, split_axis=0, concat_axis=0, tiled=True)  75.2 us
    all_to_all x2, starting transfers between devices, exchange(): return lax.all_to_all(value, axes, split_axis=0, concat_axis=0, tiled=True)  38.9 us
    ppermute x3, waiting for transfers between devices, partner(): return lax.ppermute(value, axis, pairs)  26 us
    ppermute x7, starting transfers between devices, flipped(): return lax.ppermute(value, axes, [(n, n ^ mask) for n in range(size)])  23.7 us
    ppermute x7, waiting for transfers between devices, flipped(): return lax.ppermute(value, axes, [(n, n ^ mask) for n in range(size)])  16.9 us
    pallas_call x2, Pallas kernels, solve(): pl.pallas_call(solve_kernel, out_shape=jax.ShapeDtypeStruct((ROWS, LANES)...  15.1 us
    ppermute x3, starting transfers between devices, partner(): return lax.ppermute(value, axis, pairs)  10.2 us
    pallas_call x1, Pallas kernels, solve_last(): pl.pallas_call(last_kernel, out_shape=jax.ShapeDtypeStruct((64, 32, LANES...  8.88 us
  transfers between devices with their start and end apart: 12, of which 4 were waited for; matrix products, arithmetic and copies ran while one was open for 0% of the time, Pallas kernels for 11%

profile of v3, /device:TPU:1, one launch (start us, length us, event | category | flops | bytes accessed | tf_op | source)
XLA Modules:
  0.0 230.3 jit_solution(10353796914401500437)
XLA Ops:
  3.8 21.7 %all-to-all-start.1 = ((bf16[64,32,128]{2,1,0:T(8,128)(2,1)}), bf16[64,32,128]{2,1,0:T(8,128)(2,1)S(1)}, u32[]{:S(2)}, u32[]{:S(2)}) async-start(bf16[64,32,128]{2,1,0:T(8,128)(2,1)} %spread.1), calls=%async_computation.1 | async-start | bytes 1048576 | tf_op jit(solution)/shard_map/all_to_all | solution.py:265
  25.6 3.0 %collective-permute-start.1 = (bf16[2048,128]{1,0:T(8,128)(2,1)S(1)}, bf16[2048,128]{1,0:T(8,128)(2,1)S(1)}, u32[]{:S(2)}, u32[]{:S(2)}) collective-permute-start(bf16[2048,128]{1,0:T(8,128)(2,1)S(1)} %compact.1.own.mine), channel_id=1, source_target_pairs={{0,4},{4,0},{8,12},{12,8},{16,20},{20,16},{24,28},{28,24},{32,36},... | collective-permute-start | bytes 1572872 | tf_op jit(solution)/shard_map/ppermute | solution.py:32
  28.6 3.2 %collective-permute-start.2 = (bf16[2048,128]{1,0:T(8,128)(2,1)S(1)}, bf16[2048,128]{1,0:T(8,128)(2,1)S(1)}, u32[]{:S(2)}, u32[]{:S(2)}) collective-permute-start(bf16[2048,128]{1,0:T(8,128)(2,1)S(1)} %compact.1.own.mine), channel_id=1, source_target_pairs={{0,8},{4,12},{8,0},{12,4},{16,24},{20,28},{24,16},{28,20},{32,40},... | collective-permute-start | bytes 1572872 | tf_op jit(solution)/shard_map/ppermute | solution.py:32
  31.8 4.0 %collective-permute-start = (bf16[2048,128]{1,0:T(8,128)(2,1)S(1)}, bf16[2048,128]{1,0:T(8,128)(2,1)S(1)}, u32[]{:S(2)}, u32[]{:S(2)}) collective-permute-start(bf16[2048,128]{1,0:T(8,128)(2,1)S(1)} %compact.1.own.mine), channel_id=1, source_target_pairs={{0,16},{4,20},{8,24},{12,28},{16,0},{20,4},{24,8},{28,12},{32,48},... | collective-permute-start | bytes 1572872 | tf_op jit(solution)/shard_map/ppermute | solution.py:32
  35.8 2.2 inverse.1
  38.0 7.5 %solve.2.first = bf16[2048,128]{1,0:T(8,128)(2,1)S(1)} custom-call(bf16[2048,128]{1,0:T(8,128)(2,1)S(1)} %compact.1.own.mine, bf16[2048,128]{1,0:T(8,128)(2,1)S(1)} %collective-permute-done.1.other, bf16[256,128]{1,0:T(8,128)(2,1)S(1)} %copy-done.1, bf16[128,128]{1,0:T(8,128)(2,1)S(1)} %copy-done.4, bf16[64,192]{1,0:T(8,128)(2,1)S(1)} %copy-done.5, ...), custom_call_target="tpu_custom_call" | custom-call | tf_op jit(solution)/shard_map/solve/pallas_call | solution.py:230
  45.6 26.0 %collective-permute-done.2.other = bf16[2048,128]{1,0:T(8,128)(2,1)S(1)} collective-permute-done((bf16[2048,128]{1,0:T(8,128)(2,1)S(1)}, bf16[2048,128]{1,0:T(8,128)(2,1)S(1)}, u32[]{:S(2)}, u32[]{:S(2)}) %collective-permute-start.2) | collective-permute-done | bytes 524320 | tf_op jit(solution)/shard_map/ppermute | solution.py:32
  71.6 7.5 %solve.3.second = bf16[2048,128]{1,0:T(8,128)(2,1)S(1)} custom-call(bf16[2048,128]{1,0:T(8,128)(2,1)S(1)} %compact.1.own.mine, bf16[2048,128]{1,0:T(8,128)(2,1)S(1)} %collective-permute-done.2.other, bf16[256,128]{1,0:T(8,128)(2,1)S(1)} %copy-done.1, bf16[128,128]{1,0:T(8,128)(2,1)S(1)} %copy-done.4, bf16[64,192]{1,0:T(8,128)(2,1)S(1)} %copy-done.5, ...), custom_call_target="tpu_custom_call" | custom-call | tf_op jit(solution)/shard_map/solve/pallas_call | solution.py:230
  79.1 8.9 %last.1 = bf16[64,32,128]{2,1,0:T(8,128)(2,1)} custom-call(s32[1,3]{1,0:T(1,128)S(1)} %copy-done.7, bf16[2048,128]{1,0:T(8,128)(2,1)S(1)} %compact.1.own.mine, bf16[2048,128]{1,0:T(8,128)(2,1)S(1)} %collective-permute-done.other, bf16[256,128]{1,0:T(8,128)(2,1)S(1)} %copy-done.1, bf16[128,128]{1,0:T(8,128)(2,1)S(1)} %copy-done.4, ...), custom_call_target="tpu_custom_call" | custom-call | tf_op jit(solution)/shard_map/last/pallas_call | solution.py:240
  88.0 17.2 %all-to-all-start = ((bf16[64,32,128]{2,1,0:T(8,128)(2,1)}), bf16[64,32,128]{2,1,0:T(8,128)(2,1)}, u32[]{:S(2)}, u32[]{:S(2)}) async-start(bf16[64,32,128]{2,1,0:T(8,128)(2,1)} %last.1), calls=%async_computation | async-start | bytes 1048576 | tf_op jit(solution)/shard_map/all_to_all | solution.py:265
  105.4 2.2 collective-permute-start.3
  107.6 2.3 %collective-permute-start.4 = (bf16[32,64,128]{2,1,0:T(8,128)(2,1)S(1)}, bf16[32,64,128]{2,1,0:T(8,128)(2,1)S(1)}, u32[]{:S(2)}, u32[]{:S(2)}) collective-permute-start(bf16[32,64,128]{2,1,0:T(8,128)(2,1)S(1)} %turn.1.refs_0_), channel_id=1, source_target_pairs={{0,128},{1,129},{128,0},{129,1},{2,130},{3,131},{130,2},{131,3},{4... | collective-permute-start | bytes 1572872 | tf_op jit(solution)/shard_map/ppermute | solution.py:353
  109.9 3.9 %collective-permute-start.5 = (bf16[32,64,128]{2,1,0:T(8,128)(2,1)S(1)}, bf16[32,64,128]{2,1,0:T(8,128)(2,1)S(1)}, u32[]{:S(2)}, u32[]{:S(2)}) collective-permute-start(bf16[32,64,128]{2,1,0:T(8,128)(2,1)S(1)} %turn.1.refs_0_), channel_id=1, source_target_pairs={{0,129},{1,128},{128,1},{129,0},{2,131},{3,130},{130,3},{131,2},{4... | collective-permute-start | bytes 1572872 | tf_op jit(solution)/shard_map/ppermute | solution.py:353
  113.8 3.9 %collective-permute-start.6 = (bf16[32,64,128]{2,1,0:T(8,128)(2,1)S(1)}, bf16[32,64,128]{2,1,0:T(8,128)(2,1)S(1)}, u32[]{:S(2)}, u32[]{:S(2)}) collective-permute-start(bf16[32,64,128]{2,1,0:T(8,128)(2,1)S(1)} %turn.1.refs_0_), channel_id=1, source_target_pairs={{0,4},{4,0},{1,5},{5,1},{2,6},{6,2},{3,7},{7,3},{8,12},{12,8},{9,1... | collective-permute-start | bytes 1572872 | tf_op jit(solution)/shard_map/ppermute | solution.py:353
  117.7 5.3 %collective-permute-done.3.refs_1_ = bf16[32,64,128]{2,1,0:T(8,128)(2,1)S(1)} collective-permute-done((bf16[32,64,128]{2,1,0:T(8,128)(2,1)S(1)}, bf16[32,64,128]{2,1,0:T(8,128)(2,1)S(1)}, u32[]{:S(2)}, u32[]{:S(2)}) %collective-permute-start.3) | collective-permute-done | bytes 524320 | tf_op jit(solution)/shard_map/ppermute | solution.py:353
  122.9 5.7 %collective-permute-start.7 = (bf16[32,64,128]{2,1,0:T(8,128)(2,1)S(1)}, bf16[32,64,128]{2,1,0:T(8,128)(2,1)S(1)}, u32[]{:S(2)}, u32[]{:S(2)}) collective-permute-start(bf16[32,64,128]{2,1,0:T(8,128)(2,1)S(1)} %collective-permute-done.3.refs_1_), channel_id=1, source_target_pairs={{0,4},{4,0},{1,5},{5,1},{2,6},{6,2},{3,7},{7,3},{8,12},{12,8},{9,1... | collective-permute-start | bytes 1572872 | tf_op jit(solution)/shard_map/ppermute | solution.py:353
  128.7 9.7 %collective-permute-done.4.refs_2_ = bf16[32,64,128]{2,1,0:T(8,128)(2,1)S(1)} collective-permute-done((bf16[32,64,128]{2,1,0:T(8,128)(2,1)S(1)}, bf16[32,64,128]{2,1,0:T(8,128)(2,1)S(1)}, u32[]{:S(2)}, u32[]{:S(2)}) %collective-permute-start.4) | collective-permute-done | bytes 524320 | tf_op jit(solution)/shard_map/ppermute | solution.py:353
  138.4 3.8 %collective-permute-start.8 = (bf16[32,64,128]{2,1,0:T(8,128)(2,1)S(1)}, bf16[32,64,128]{2,1,0:T(8,128)(2,1)}, u32[]{:S(2)}, u32[]{:S(2)}) collective-permute-start(bf16[32,64,128]{2,1,0:T(8,128)(2,1)S(1)} %collective-permute-done.4.refs_2_), channel_id=1, source_target_pairs={{0,4},{4,0},{1,5},{5,1},{2,6},{6,2},{3,7},{7,3},{8,12},{12,8},{9,1... | collective-permute-start | bytes 1572872 | tf_op jit(solution)/shard_map/ppermute | solution.py:353
  144.1 2.0 collective-permute-done.9.refs_7_
  146.1 3.4 %overlap.1 = (f32[64,4,128]{2,1,0:T(4,128)S(1)}, bf16[32,64,128]{2,1,0:T(8,128)(2,1)S(1)}) custom-call(bf16[64,32,128]{2,1,0:T(8,128)(2,1)} %all-to-all-done.applied, bf16[32,64,128]{2,1,0:T(8,128)(2,1)S(1)} %turn.1.refs_0_, bf16[32,64,128]{2,1,0:T(8,128)(2,1)S(1)} %collective-permute-done.3.refs_1_, ...), custom_call_target="tpu_custom_call" | custom-call | tf_op jit(solution)/shard_map/overlap/pallas_call | solution.py:294
  150.3 32.2 %all_to_all.25 = f32[64,4,128]{2,1,0:T(4,128)S(1)} all-to-all(f32[64,4,128]{2,1,0:T(4,128)S(1)} %get-tuple-element.11), channel_id=1, replica_groups=mesh['y_high'=2,'y_low'=2,'z'=16,'core'=2,'x_high'=2,'x_low'=2] {'y_high..., dimensions={0} | all-to-all | bytes 262144 | tf_op jit(solution)/shard_map/all_to_all | solution.py:265
  182.6 23.5 %all_to_all.26.overlaps = f32[64,4,128]{2,1,0:T(4,128)S(1)} all-to-all(f32[64,4,128]{2,1,0:T(4,128)S(1)} %broadcast_in_dim.3), channel_id=1, replica_groups=mesh['y_high'=2,'y_low'=2,'z'=16,'core'=2,'x_high'=2,'x_low'=2] {'y_high..., dimensions={0} | all-to-all | bytes 262144 | tf_op jit(solution)/shard_map/all_to_all | solution.py:265
  207.1 2.5 %project.1 = f32[32,64,128]{2,1,0:T(8,128)S(1)} custom-call(f32[64,4,128]{2,1,0:T(4,128)S(1)} %all_to_all.26.overlaps, bf16[32,64,128]{2,1,0:T(8,128)(2,1)S(1)} %copy-done.3, bf16[32,64,128]{2,1,0:T(8,128)(2,1)S(1)} %turn.1.refs_0_, bf16[32,64,128]{2,1,0:T(8,128)(2,1)S(1)} %collective-permute-done.3.refs_1_, ...), custom_call_target="tpu_custom_call" | custom-call | tf_op jit(solution)/shard_map/project/pallas_call | solution.py:322
  209.6 19.5 %all_to_all.27.arrived = f32[8,256,128]{2,1,0:T(8,128)S(1)} all-to-all(f32[8,256,128]{2,1,0:T(8,128)S(1)} %bitcast.2), channel_id=1, replica_groups=mesh['y_high'=2,'y_low'=2,'z'=16,'core'=2,'x_high'=2,'x_low'=2] {'y_low'..., dimensions={0} | all-to-all | bytes 2097152 | tf_op jit(solution)/shard_map/all_to_all | solution.py:265
  (31 shorter events, 9.0 us)
Async XLA Ops:
  0.0 1.2 copy-start
  3.8 84.2 %all-to-all-start.1 = ((bf16[64,32,128]{2,1,0:T(8,128)(2,1)}), bf16[64,32,128]{2,1,0:T(8,128)(2,1)S(1)}, u32[]{:S(2)}, u32[]{:S(2)}) async-start(bf16[64,32,128]{2,1,0:T(8,128)(2,1)} %spread.1), calls=%async_computation.1 | async-start | bytes 1048576 | tf_op jit(solution)/shard_map/all_to_all | solution.py:265
  25.5 12.5 %copy-start.1 = (bf16[256,128]{1,0:T(8,128)(2,1)S(1)}, bf16[256,128]{1,0:T(8,128)(2,1)}, u32[]{:S(2)}) copy-start(bf16[256,128]{1,0:T(8,128)(2,1)} %constant.10.clone.z_main) | copy-start | bytes 196612
  25.5 12.5 %copy-start.4 = (bf16[128,128]{1,0:T(8,128)(2,1)S(1)}, bf16[128,128]{1,0:T(8,128)(2,1)}, u32[]{:S(2)}) copy-start(bf16[128,128]{1,0:T(8,128)(2,1)} %constant.11.clone.z_low) | copy-start | bytes 98308
  25.6 12.4 %copy-start.5 = (bf16[64,192]{1,0:T(8,128)(2,1)S(1)}, bf16[64,192]{1,0:T(8,128)(2,1)}, u32[]{:S(2)}) copy-start(bf16[64,192]{1,0:T(8,128)(2,1)} %constant.12.clone.y_side) | copy-start | bytes 73732
  25.6 12.4 %copy-start.6 = (bf16[64,192]{1,0:T(8,128)(2,1)S(1)}, bf16[64,192]{1,0:T(8,128)(2,1)}, u32[]{:S(2)}) copy-start(bf16[64,192]{1,0:T(8,128)(2,1)} %constant.13.clone.x_side) | copy-start | bytes 73732
  25.6 12.4 %collective-permute-start.1 = (bf16[2048,128]{1,0:T(8,128)(2,1)S(1)}, bf16[2048,128]{1,0:T(8,128)(2,1)S(1)}, u32[]{:S(2)}, u32[]{:S(2)}) collective-permute-start(bf16[2048,128]{1,0:T(8,128)(2,1)S(1)} %compact.1.own.mine), channel_id=1, source_target_pairs={{0,4},{4,0},{8,12},{12,8},{16,20},{20,16},{24,28},{28,24},{32,36},... | collective-permute-start | bytes 1572872 | tf_op jit(solution)/shard_map/ppermute | solution.py:32
  28.6 43.0 %collective-permute-start.2 = (bf16[2048,128]{1,0:T(8,128)(2,1)S(1)}, bf16[2048,128]{1,0:T(8,128)(2,1)S(1)}, u32[]{:S(2)}, u32[]{:S(2)}) collective-permute-start(bf16[2048,128]{1,0:T(8,128)(2,1)S(1)} %compact.1.own.mine), channel_id=1, source_target_pairs={{0,8},{4,12},{8,0},{12,4},{16,24},{20,28},{24,16},{28,20},{32,40},... | collective-permute-start | bytes 1572872 | tf_op jit(solution)/shard_map/ppermute | solution.py:32
  31.8 47.3 %collective-permute-start = (bf16[2048,128]{1,0:T(8,128)(2,1)S(1)}, bf16[2048,128]{1,0:T(8,128)(2,1)S(1)}, u32[]{:S(2)}, u32[]{:S(2)}) collective-permute-start(bf16[2048,128]{1,0:T(8,128)(2,1)S(1)} %compact.1.own.mine), channel_id=1, source_target_pairs={{0,16},{4,20},{8,24},{12,28},{16,0},{20,4},{24,8},{28,12},{32,48},... | collective-permute-start | bytes 1572872 | tf_op jit(solution)/shard_map/ppermute | solution.py:32
  45.6 33.6 %copy-start.7 = (s32[1,3]{1,0:T(1,128)S(1)}, s32[1,3]{1,0:T(1,128)}, u32[]{:S(2)}) copy-start(s32[1,3]{1,0:T(1,128)} %partners.1) | copy-start | bytes 40
  88.0 56.1 %all-to-all-start = ((bf16[64,32,128]{2,1,0:T(8,128)(2,1)}), bf16[64,32,128]{2,1,0:T(8,128)(2,1)}, u32[]{:S(2)}, u32[]{:S(2)}) async-start(bf16[64,32,128]{2,1,0:T(8,128)(2,1)} %last.1), calls=%async_computation | async-start | bytes 1048576 | tf_op jit(solution)/shard_map/all_to_all | solution.py:265
  105.4 17.6 %collective-permute-start.3 = (bf16[32,64,128]{2,1,0:T(8,128)(2,1)S(1)}, bf16[32,64,128]{2,1,0:T(8,128)(2,1)S(1)}, u32[]{:S(2)}, u32[]{:S(2)}) collective-permute-start(bf16[32,64,128]{2,1,0:T(8,128)(2,1)S(1)} %turn.1.refs_0_), channel_id=1, source_target_pairs={{0,1},{1,0},{128,129},{129,128},{2,3},{3,2},{130,131},{131,130},{4... | collective-permute-start | bytes 1572872 | tf_op jit(solution)/shard_map/ppermute | solution.py:353
  107.6 30.8 %collective-permute-start.4 = (bf16[32,64,128]{2,1,0:T(8,128)(2,1)S(1)}, bf16[32,64,128]{2,1,0:T(8,128)(2,1)S(1)}, u32[]{:S(2)}, u32[]{:S(2)}) collective-permute-start(bf16[32,64,128]{2,1,0:T(8,128)(2,1)S(1)} %turn.1.refs_0_), channel_id=1, source_target_pairs={{0,128},{1,129},{128,0},{129,1},{2,130},{3,131},{130,2},{131,3},{4... | collective-permute-start | bytes 1572872 | tf_op jit(solution)/shard_map/ppermute | solution.py:353
  109.9 32.2 %collective-permute-start.5 = (bf16[32,64,128]{2,1,0:T(8,128)(2,1)S(1)}, bf16[32,64,128]{2,1,0:T(8,128)(2,1)S(1)}, u32[]{:S(2)}, u32[]{:S(2)}) collective-permute-start(bf16[32,64,128]{2,1,0:T(8,128)(2,1)S(1)} %turn.1.refs_0_), channel_id=1, source_target_pairs={{0,129},{1,128},{128,1},{129,0},{2,131},{3,130},{130,3},{131,2},{4... | collective-permute-start | bytes 1572872 | tf_op jit(solution)/shard_map/ppermute | solution.py:353
  113.8 30.3 %collective-permute-start.6 = (bf16[32,64,128]{2,1,0:T(8,128)(2,1)S(1)}, bf16[32,64,128]{2,1,0:T(8,128)(2,1)S(1)}, u32[]{:S(2)}, u32[]{:S(2)}) collective-permute-start(bf16[32,64,128]{2,1,0:T(8,128)(2,1)S(1)} %turn.1.refs_0_), channel_id=1, source_target_pairs={{0,4},{4,0},{1,5},{5,1},{2,6},{6,2},{3,7},{7,3},{8,12},{12,8},{9,1... | collective-permute-start | bytes 1572872 | tf_op jit(solution)/shard_map/ppermute | solution.py:353
  122.9 21.2 %collective-permute-start.7 = (bf16[32,64,128]{2,1,0:T(8,128)(2,1)S(1)}, bf16[32,64,128]{2,1,0:T(8,128)(2,1)S(1)}, u32[]{:S(2)}, u32[]{:S(2)}) collective-permute-start(bf16[32,64,128]{2,1,0:T(8,128)(2,1)S(1)} %collective-permute-done.3.refs_1_), channel_id=1, source_target_pairs={{0,4},{4,0},{1,5},{5,1},{2,6},{6,2},{3,7},{7,3},{8,12},{12,8},{9,1... | collective-permute-start | bytes 1572872 | tf_op jit(solution)/shard_map/ppermute | solution.py:353
  138.4 5.8 %collective-permute-start.8 = (bf16[32,64,128]{2,1,0:T(8,128)(2,1)S(1)}, bf16[32,64,128]{2,1,0:T(8,128)(2,1)}, u32[]{:S(2)}, u32[]{:S(2)}) collective-permute-start(bf16[32,64,128]{2,1,0:T(8,128)(2,1)S(1)} %collective-permute-done.4.refs_2_), channel_id=1, source_target_pairs={{0,4},{4,0},{1,5},{5,1},{2,6},{6,2},{3,7},{7,3},{8,12},{12,8},{9,1... | collective-permute-start | bytes 1572872 | tf_op jit(solution)/shard_map/ppermute | solution.py:353
  142.2 3.9 %collective-permute-start.9 = (bf16[32,64,128]{2,1,0:T(8,128)(2,1)S(1)}, bf16[32,64,128]{2,1,0:T(8,128)(2,1)}, u32[]{:S(2)}, u32[]{:S(2)}) collective-permute-start(bf16[32,64,128]{2,1,0:T(8,128)(2,1)S(1)} %collective-permute-done.5.refs_3_), channel_id=1, source_target_pairs={{0,4},{4,0},{1,5},{5,1},{2,6},{6,2},{3,7},{7,3},{8,12},{12,8},{9,1... | collective-permute-start | bytes 1572872 | tf_op jit(solution)/shard_map/ppermute | solution.py:353
  149.5 0.8 copy-start.2
  206.1 1.0 copy-start.3

commit v4 on v2

--- a/solution.py
+++ b/solution.py
@@ -134,7 +134,7 @@
                 field[pl.ds(n * 8 + 4 * pair + 2 * m, 2)] = slab.reshape(2, 32, LANES)
         return carry
 
-    lax.fori_loop(0, ROWS // 256, step, 0)
+    lax.fori_loop(0, ROWS // 256, step, 0, unroll=2)
 
 
 def middle_part(x_side, inverse, field):
@@ -151,7 +151,7 @@
         field[:, group, :] = jnp.transpose(jnp.stack(outs, axis=0), (1, 0, 2))
         return carry
 
-    lax.fori_loop(0, 4, step, 0)
+    lax.fori_loop(0, 4, step, 0, unroll=2)
 
 
 def backward_block(n, other, z_main, z_low, y_side, field, mask):
@@ -174,7 +174,7 @@
         term[rows] = value
         return carry
 
-    lax.fori_loop(0, ROWS // 256, step, 0)
+    lax.fori_loop(0, ROWS // 256, step, 0, unroll=2)
 
 
 def woven(first, second):
@@ -199,7 +199,7 @@
         place(out, n, mine[pl.ds(pl.multiple_of(n * 256, 256), 256)].astype(F32))
         return carry
 
-    lax.fori_loop(0, ROWS // 256, step, 0)
+    lax.fori_loop(0, ROWS // 256, step, 0, unroll=2)
 
 
 def spread(mine):
@@ -226,7 +226,7 @@
         place(out, n, total)
         return carry
 
-    lax.fori_loop(0, ROWS // 256, step, 0)
+    lax.fori_loop(0, ROWS // 256, step, 0, unroll=2)
 
 
 FIELD = pltpu.VMEM((NG, NG // 2, LANES), F32)
@@ -293,7 +293,7 @@
             preferred_element_type=F32,
         )
 
-    total = lax.fori_loop(0, 16, step, jnp.zeros((64, 512), F32)) * (1.0 / NG3)
+    total = lax.fori_loop(0, 16, step, jnp.zeros((64, 512), F32), unroll=4) * (1.0 / NG3)
     for n in range(4):
         out[:, n, :] = total[:, LANES * n : LANES * (n + 1)]
 
@@ -312,16 +312,18 @@
 
 def project_kernel(overlaps, slab, *refs):
     phis, out = refs[:8], refs[8]
-    high, low = two_parts(jnp.concatenate([overlaps[:, n, :] for n in range(4)], axis=1))
-
-    def step(n, carry):
-        cells = all_two_rows(phis, n)
-        value = two_rows(slab, n).astype(F32) - (dot(high, cells) + dot(low, cells))
+    parts = jnp.concatenate(
+        two_parts(jnp.concatenate([overlaps[:, n, :] for n in range(4)], axis=1)), axis=0
+    )
+
+    def step(n, carry):
+        both = dot(parts, all_two_rows(phis, n))
+        value = two_rows(slab, n).astype(F32) - (both[:64] + both[64:])
         out[2 * n] = value[:, :LANES]
         out[2 * n + 1] = value[:, LANES:]
         return carry
 
-    lax.fori_loop(0, 16, step, 0)
+    lax.fori_loop(0, 16, step, 0, unroll=4)
 
 
 def project(overlaps, slab, phis):

time: 228 us -> 219 us (0.961)
  Pallas kernels: 46.4 us -> 35.9 us
  waiting for transfers between devices: 31.2 us -> 33.5 us
    pallas_call x2, Pallas kernels: 19.6 us -> 15.1 us  [solve(): pl.pallas_call(solve_kernel, out_shape=jax.ShapeDtypeStruct((ROWS, LANES)...]
    pallas_call x1, Pallas kernels: 11.2 us -> 8.9 us  [solve_last(): pl.pallas_call(last_kernel, out_shape=jax.ShapeDtypeStruct((64, 32, LANES...]
  transfers between devices with their start and end apart: 12 -> 12, of which waited for: 4 -> 4; matrix products, arithmetic and copies ran while one was open for 0% -> 0% of each run, Pallas kernels for 15% -> 12%
where the time goes in v4:
time: 219 us
  blocking collectives  76 us (35%)
  starting transfers between devices  69.7 us (32%)
  Pallas kernels  35.9 us (16%)
  waiting for transfers between devices  33.5 us (15%)
  local copies, waits for them, and re-layouts  3.11 us (1%)
    all_to_all x3, blocking collectives, exchange(): return lax.all_to_all(value, axes, split_axis=0, concat_axis=0, tiled=True)  76 us
    all_to_all x2, starting transfers between devices, exchange(): return lax.all_to_all(value, axes, split_axis=0, concat_axis=0, tiled=True)  33.6 us
    ppermute x3, waiting for transfers between devices, partner(): return lax.ppermute(value, axis, pairs)  26 us
    ppermute x7, starting transfers between devices, shifted(): lax.ppermute(value, axis, [(n, (n + distance) % size) for n in range(size)])  25.9 us
    pallas_call x2, Pallas kernels, solve(): pl.pallas_call(solve_kernel, out_shape=jax.ShapeDtypeStruct((ROWS, LANES)...  15.1 us
    ppermute x3, starting transfers between devices, partner(): return lax.ppermute(value, axis, pairs)  10.2 us
    pallas_call x1, Pallas kernels, solve_last(): pl.pallas_call(last_kernel, out_shape=jax.ShapeDtypeStruct((64, 32, LANES...  8.9 us
    ppermute x7, waiting for transfers between devices, shifted(): lax.ppermute(value, axis, [(n, (n + distance) % size) for n in range(size)])  7.48 us
  transfers between devices with their start and end apart: 12, of which 4 were waited for; matrix products, arithmetic and copies ran while one was open for 0% of the time, Pallas kernels for 12%

profile of v4, /device:TPU:1, one launch (start us, length us, event | category | flops | bytes accessed | tf_op | source)
XLA Modules:
  0.0 218.5 jit_solution(3716953114789266644)
XLA Ops:
  1.2 1.6 compact.1.own.mine
  3.8 19.1 %all-to-all-start.1 = ((bf16[64,32,128]{2,1,0:T(8,128)(2,1)}), bf16[64,32,128]{2,1,0:T(8,128)(2,1)S(1)}, u32[]{:S(2)}, u32[]{:S(2)}) async-start(bf16[64,32,128]{2,1,0:T(8,128)(2,1)} %spread.1), calls=%async_computation.1 | async-start | bytes 1048576 | tf_op jit(solution)/shard_map/all_to_all | solution.py:273
  23.0 3.0 %collective-permute-start.1 = (bf16[2048,128]{1,0:T(8,128)(2,1)S(1)}, bf16[2048,128]{1,0:T(8,128)(2,1)S(1)}, u32[]{:S(2)}, u32[]{:S(2)}) collective-permute-start(bf16[2048,128]{1,0:T(8,128)(2,1)S(1)} %compact.1.own.mine), channel_id=1, source_target_pairs={{0,4},{4,0},{8,12},{12,8},{16,20},{20,16},{24,28},{28,24},{32,36},... | collective-permute-start | bytes 1572872 | tf_op jit(solution)/shard_map/ppermute | solution.py:32
  26.0 3.2 %collective-permute-start.2 = (bf16[2048,128]{1,0:T(8,128)(2,1)S(1)}, bf16[2048,128]{1,0:T(8,128)(2,1)S(1)}, u32[]{:S(2)}, u32[]{:S(2)}) collective-permute-start(bf16[2048,128]{1,0:T(8,128)(2,1)S(1)} %compact.1.own.mine), channel_id=1, source_target_pairs={{0,8},{4,12},{8,0},{12,4},{16,24},{20,28},{24,16},{28,20},{32,40},... | collective-permute-start | bytes 1572872 | tf_op jit(solution)/shard_map/ppermute | solution.py:32
  29.2 4.0 %collective-permute-start = (bf16[2048,128]{1,0:T(8,128)(2,1)S(1)}, bf16[2048,128]{1,0:T(8,128)(2,1)S(1)}, u32[]{:S(2)}, u32[]{:S(2)}) collective-permute-start(bf16[2048,128]{1,0:T(8,128)(2,1)S(1)} %compact.1.own.mine), channel_id=1, source_target_pairs={{0,16},{4,20},{8,24},{12,28},{16,0},{20,4},{24,8},{28,12},{32,48},... | collective-permute-start | bytes 1572872 | tf_op jit(solution)/shard_map/ppermute | solution.py:32
  33.2 2.2 inverse.1
  35.4 7.5 %solve.2.first = bf16[2048,128]{1,0:T(8,128)(2,1)S(1)} custom-call(bf16[2048,128]{1,0:T(8,128)(2,1)S(1)} %compact.1.own.mine, bf16[2048,128]{1,0:T(8,128)(2,1)S(1)} %collective-permute-done.1.other, bf16[256,128]{1,0:T(8,128)(2,1)S(1)} %copy-done.1, bf16[128,128]{1,0:T(8,128)(2,1)S(1)} %copy-done.4, bf16[64,192]{1,0:T(8,128)(2,1)S(1)} %copy-done.5, ...), custom_call_target="tpu_custom_call" | custom-call | tf_op jit(solution)/shard_map/solve/pallas_call | solution.py:238
  43.0 26.0 %collective-permute-done.2.other = bf16[2048,128]{1,0:T(8,128)(2,1)S(1)} collective-permute-done((bf16[2048,128]{1,0:T(8,128)(2,1)S(1)}, bf16[2048,128]{1,0:T(8,128)(2,1)S(1)}, u32[]{:S(2)}, u32[]{:S(2)}) %collective-permute-start.2) | collective-permute-done | bytes 524320 | tf_op jit(solution)/shard_map/ppermute | solution.py:32
  69.0 7.5 %solve.3.second = bf16[2048,128]{1,0:T(8,128)(2,1)S(1)} custom-call(bf16[2048,128]{1,0:T(8,128)(2,1)S(1)} %compact.1.own.mine, bf16[2048,128]{1,0:T(8,128)(2,1)S(1)} %collective-permute-done.2.other, bf16[256,128]{1,0:T(8,128)(2,1)S(1)} %copy-done.1, bf16[128,128]{1,0:T(8,128)(2,1)S(1)} %copy-done.4, bf16[64,192]{1,0:T(8,128)(2,1)S(1)} %copy-done.5, ...), custom_call_target="tpu_custom_call" | custom-call | tf_op jit(solution)/shard_map/solve/pallas_call | solution.py:238
  76.5 8.9 %last.1 = bf16[64,32,128]{2,1,0:T(8,128)(2,1)} custom-call(s32[1,3]{1,0:T(1,128)S(1)} %copy-done.7, bf16[2048,128]{1,0:T(8,128)(2,1)S(1)} %compact.1.own.mine, bf16[2048,128]{1,0:T(8,128)(2,1)S(1)} %collective-permute-done.other, bf16[256,128]{1,0:T(8,128)(2,1)S(1)} %copy-done.1, bf16[128,128]{1,0:T(8,128)(2,1)S(1)} %copy-done.4, ...), custom_call_target="tpu_custom_call" | custom-call | tf_op jit(solution)/shard_map/last/pallas_call | solution.py:248
  85.4 14.5 %all-to-all-start = ((bf16[64,32,128]{2,1,0:T(8,128)(2,1)}), bf16[64,32,128]{2,1,0:T(8,128)(2,1)}, u32[]{:S(2)}, u32[]{:S(2)}) async-start(bf16[64,32,128]{2,1,0:T(8,128)(2,1)} %last.1), calls=%async_computation | async-start | bytes 1048576 | tf_op jit(solution)/shard_map/all_to_all | solution.py:273
  100.1 3.2 %collective-permute-start.3 = (bf16[32,64,128]{2,1,0:T(8,128)(2,1)S(1)}, bf16[32,64,128]{2,1,0:T(8,128)(2,1)S(1)}, u32[]{:S(2)}, u32[]{:S(2)}) collective-permute-start(bf16[32,64,128]{2,1,0:T(8,128)(2,1)S(1)} %turn.1.refs_0_), channel_id=1, source_target_pairs={{0,128},{128,256},{256,384},{384,0},{1,129},{129,257},{257,385},{3... | collective-permute-start | bytes 1572872 | tf_op jit(solution)/shard_map/ppermute | solution.py:356
  103.3 3.4 %collective-permute-start.4 = (bf16[32,64,128]{2,1,0:T(8,128)(2,1)S(1)}, bf16[32,64,128]{2,1,0:T(8,128)(2,1)S(1)}, u32[]{:S(2)}, u32[]{:S(2)}) collective-permute-start(bf16[32,64,128]{2,1,0:T(8,128)(2,1)S(1)} %turn.1.refs_0_), channel_id=1, source_target_pairs={{0,384},{128,0},{256,128},{384,256},{1,385},{129,1},{257,129},{385... | collective-permute-start | bytes 1572872 | tf_op jit(solution)/shard_map/ppermute | solution.py:356
  106.7 3.5 %collective-permute-start.5 = (bf16[32,64,128]{2,1,0:T(8,128)(2,1)S(1)}, bf16[32,64,128]{2,1,0:T(8,128)(2,1)S(1)}, u32[]{:S(2)}, u32[]{:S(2)}) collective-permute-start(bf16[32,64,128]{2,1,0:T(8,128)(2,1)S(1)} %turn.1.refs_0_), channel_id=1, source_target_pairs={{0,256},{128,384},{256,0},{384,128},{1,257},{129,385},{257,1},{385... | collective-permute-start | bytes 1572872 | tf_op jit(solution)/shard_map/ppermute | solution.py:356
  110.2 4.0 %collective-permute-start.6 = (bf16[32,64,128]{2,1,0:T(8,128)(2,1)S(1)}, bf16[32,64,128]{2,1,0:T(8,128)(2,1)S(1)}, u32[]{:S(2)}, u32[]{:S(2)}) collective-permute-start(bf16[32,64,128]{2,1,0:T(8,128)(2,1)S(1)} %turn.1.refs_0_), channel_id=1, source_target_pairs={{0,4},{4,0},{1,5},{5,1},{2,6},{6,2},{3,7},{7,3},{8,12},{12,8},{9,1... | collective-permute-start | bytes 1572872 | tf_op jit(solution)/shard_map/ppermute | solution.py:356
  115.7 4.4 %collective-permute-start.7 = (bf16[32,64,128]{2,1,0:T(8,128)(2,1)S(1)}, bf16[32,64,128]{2,1,0:T(8,128)(2,1)S(1)}, u32[]{:S(2)}, u32[]{:S(2)}) collective-permute-start(bf16[32,64,128]{2,1,0:T(8,128)(2,1)S(1)} %collective-permute-done.3.refs_1_), channel_id=1, source_target_pairs={{0,4},{4,0},{1,5},{5,1},{2,6},{6,2},{3,7},{7,3},{8,12},{12,8},{9,1... | collective-permute-start | bytes 1572872 | tf_op jit(solution)/shard_map/ppermute | solution.py:356
  120.1 3.4 %collective-permute-start.8 = (bf16[32,64,128]{2,1,0:T(8,128)(2,1)S(1)}, bf16[32,64,128]{2,1,0:T(8,128)(2,1)}, u32[]{:S(2)}, u32[]{:S(2)}) collective-permute-start(bf16[32,64,128]{2,1,0:T(8,128)(2,1)S(1)} %collective-permute-done.4.refs_2_), channel_id=1, source_target_pairs={{0,4},{4,0},{1,5},{5,1},{2,6},{6,2},{3,7},{7,3},{8,12},{12,8},{9,1... | collective-permute-start | bytes 1572872 | tf_op jit(solution)/shard_map/ppermute | solution.py:356
  123.5 4.5 %collective-permute-done.5.refs_3_ = bf16[32,64,128]{2,1,0:T(8,128)(2,1)S(1)} collective-permute-done((bf16[32,64,128]{2,1,0:T(8,128)(2,1)S(1)}, bf16[32,64,128]{2,1,0:T(8,128)(2,1)S(1)}, u32[]{:S(2)}, u32[]{:S(2)}) %collective-permute-start.5) | collective-permute-done | bytes 524320 | tf_op jit(solution)/shard_map/ppermute | solution.py:356
  128.0 3.9 %collective-permute-start.9 = (bf16[32,64,128]{2,1,0:T(8,128)(2,1)S(1)}, bf16[32,64,128]{2,1,0:T(8,128)(2,1)}, u32[]{:S(2)}, u32[]{:S(2)}) collective-permute-start(bf16[32,64,128]{2,1,0:T(8,128)(2,1)S(1)} %collective-permute-done.5.refs_3_), channel_id=1, source_target_pairs={{0,4},{4,0},{1,5},{5,1},{2,6},{6,2},{3,7},{7,3},{8,12},{12,8},{9,1... | collective-permute-start | bytes 1572872 | tf_op jit(solution)/shard_map/ppermute | solution.py:356
  133.6 3.4 %overlap.1 = (f32[64,4,128]{2,1,0:T(4,128)S(1)}, bf16[32,64,128]{2,1,0:T(8,128)(2,1)S(1)}) custom-call(bf16[64,32,128]{2,1,0:T(8,128)(2,1)} %all-to-all-done.applied, bf16[32,64,128]{2,1,0:T(8,128)(2,1)S(1)} %turn.1.refs_0_, bf16[32,64,128]{2,1,0:T(8,128)(2,1)S(1)} %collective-permute-done.3.refs_1_, ...), custom_call_target="tpu_custom_call" | custom-call | tf_op jit(solution)/shard_map/overlap/pallas_call | solution.py:302
  137.7 29.4 %all_to_all.25 = f32[64,4,128]{2,1,0:T(4,128)S(1)} all-to-all(f32[64,4,128]{2,1,0:T(4,128)S(1)} %get-tuple-element.11), channel_id=1, replica_groups=mesh['band_0'=4,'band_1'=16,'band_2'=2,'pair'=4] {'band_1','pair'}, dimensions={0} | all-to-all | bytes 262144 | tf_op jit(solution)/shard_map/all_to_all | solution.py:273
  167.3 21.3 %all_to_all.26.overlaps = f32[64,4,128]{2,1,0:T(4,128)S(1)} all-to-all(f32[64,4,128]{2,1,0:T(4,128)S(1)} %broadcast_in_dim.3), channel_id=1, replica_groups=mesh['band_0'=4,'band_1'=16,'band_2'=2,'pair'=4] {'band_1','pair'}, dimensions={0} | all-to-all | bytes 262144 | tf_op jit(solution)/shard_map/all_to_all | solution.py:273
  189.6 2.5 %project.1 = f32[32,64,128]{2,1,0:T(8,128)S(1)} custom-call(f32[64,4,128]{2,1,0:T(4,128)S(1)} %all_to_all.26.overlaps, bf16[32,64,128]{2,1,0:T(8,128)(2,1)S(1)} %copy-done.3, bf16[32,64,128]{2,1,0:T(8,128)(2,1)S(1)} %turn.1.refs_0_, bf16[32,64,128]{2,1,0:T(8,128)(2,1)S(1)} %collective-permute-done.3.refs_1_, ...), custom_call_target="tpu_custom_call" | custom-call | tf_op jit(solution)/shard_map/project/pallas_call | solution.py:330
  192.1 25.3 %all_to_all.27.arrived = f32[8,256,128]{2,1,0:T(8,128)S(1)} all-to-all(f32[8,256,128]{2,1,0:T(8,128)S(1)} %bitcast.2), channel_id=1, replica_groups=mesh['band_0'=4,'band_1'=16,'band_2'=2,'pair'=4] {'band_0','band_2'}, dimensions={0} | all-to-all | bytes 2097152 | tf_op jit(solution)/shard_map/all_to_all | solution.py:273
  (31 shorter events, 8.4 us)
Async XLA Ops:
  0.0 1.2 copy-start
  3.8 81.6 %all-to-all-start.1 = ((bf16[64,32,128]{2,1,0:T(8,128)(2,1)}), bf16[64,32,128]{2,1,0:T(8,128)(2,1)S(1)}, u32[]{:S(2)}, u32[]{:S(2)}) async-start(bf16[64,32,128]{2,1,0:T(8,128)(2,1)} %spread.1), calls=%async_computation.1 | async-start | bytes 1048576 | tf_op jit(solution)/shard_map/all_to_all | solution.py:273
  22.9 12.5 %copy-start.1 = (bf16[256,128]{1,0:T(8,128)(2,1)S(1)}, bf16[256,128]{1,0:T(8,128)(2,1)}, u32[]{:S(2)}) copy-start(bf16[256,128]{1,0:T(8,128)(2,1)} %constant.10.clone.z_main) | copy-start | bytes 196612
  22.9 12.5 %copy-start.4 = (bf16[128,128]{1,0:T(8,128)(2,1)S(1)}, bf16[128,128]{1,0:T(8,128)(2,1)}, u32[]{:S(2)}) copy-start(bf16[128,128]{1,0:T(8,128)(2,1)} %constant.11.clone.z_low) | copy-start | bytes 98308
  23.0 12.5 %copy-start.5 = (bf16[64,192]{1,0:T(8,128)(2,1)S(1)}, bf16[64,192]{1,0:T(8,128)(2,1)}, u32[]{:S(2)}) copy-start(bf16[64,192]{1,0:T(8,128)(2,1)} %constant.12.clone.y_side) | copy-start | bytes 73732
  23.0 12.4 %copy-start.6 = (bf16[64,192]{1,0:T(8,128)(2,1)S(1)}, bf16[64,192]{1,0:T(8,128)(2,1)}, u32[]{:S(2)}) copy-start(bf16[64,192]{1,0:T(8,128)(2,1)} %constant.13.clone.x_side) | copy-start | bytes 73732
  23.0 12.4 %collective-permute-start.1 = (bf16[2048,128]{1,0:T(8,128)(2,1)S(1)}, bf16[2048,128]{1,0:T(8,128)(2,1)S(1)}, u32[]{:S(2)}, u32[]{:S(2)}) collective-permute-start(bf16[2048,128]{1,0:T(8,128)(2,1)S(1)} %compact.1.own.mine), channel_id=1, source_target_pairs={{0,4},{4,0},{8,12},{12,8},{16,20},{20,16},{24,28},{28,24},{32,36},... | collective-permute-start | bytes 1572872 | tf_op jit(solution)/shard_map/ppermute | solution.py:32
  26.0 43.0 %collective-permute-start.2 = (bf16[2048,128]{1,0:T(8,128)(2,1)S(1)}, bf16[2048,128]{1,0:T(8,128)(2,1)S(1)}, u32[]{:S(2)}, u32[]{:S(2)}) collective-permute-start(bf16[2048,128]{1,0:T(8,128)(2,1)S(1)} %compact.1.own.mine), channel_id=1, source_target_pairs={{0,8},{4,12},{8,0},{12,4},{16,24},{20,28},{24,16},{28,20},{32,40},... | collective-permute-start | bytes 1572872 | tf_op jit(solution)/shard_map/ppermute | solution.py:32
  29.2 47.3 %collective-permute-start = (bf16[2048,128]{1,0:T(8,128)(2,1)S(1)}, bf16[2048,128]{1,0:T(8,128)(2,1)S(1)}, u32[]{:S(2)}, u32[]{:S(2)}) collective-permute-start(bf16[2048,128]{1,0:T(8,128)(2,1)S(1)} %compact.1.own.mine), channel_id=1, source_target_pairs={{0,16},{4,20},{8,24},{12,28},{16,0},{20,4},{24,8},{28,12},{32,48},... | collective-permute-start | bytes 1572872 | tf_op jit(solution)/shard_map/ppermute | solution.py:32
  43.0 33.6 %copy-start.7 = (s32[1,3]{1,0:T(1,128)S(1)}, s32[1,3]{1,0:T(1,128)}, u32[]{:S(2)}) copy-start(s32[1,3]{1,0:T(1,128)} %partners.1) | copy-start | bytes 40
  85.4 46.5 %all-to-all-start = ((bf16[64,32,128]{2,1,0:T(8,128)(2,1)}), bf16[64,32,128]{2,1,0:T(8,128)(2,1)}, u32[]{:S(2)}, u32[]{:S(2)}) async-start(bf16[64,32,128]{2,1,0:T(8,128)(2,1)} %last.1), calls=%async_computation | async-start | bytes 1048576 | tf_op jit(solution)/shard_map/all_to_all | solution.py:273
  100.1 15.5 %collective-permute-start.3 = (bf16[32,64,128]{2,1,0:T(8,128)(2,1)S(1)}, bf16[32,64,128]{2,1,0:T(8,128)(2,1)S(1)}, u32[]{:S(2)}, u32[]{:S(2)}) collective-permute-start(bf16[32,64,128]{2,1,0:T(8,128)(2,1)S(1)} %turn.1.refs_0_), channel_id=1, source_target_pairs={{0,128},{128,256},{256,384},{384,0},{1,129},{129,257},{257,385},{3... | collective-permute-start | bytes 1572872 | tf_op jit(solution)/shard_map/ppermute | solution.py:356
  103.3 16.8 %collective-permute-start.4 = (bf16[32,64,128]{2,1,0:T(8,128)(2,1)S(1)}, bf16[32,64,128]{2,1,0:T(8,128)(2,1)S(1)}, u32[]{:S(2)}, u32[]{:S(2)}) collective-permute-start(bf16[32,64,128]{2,1,0:T(8,128)(2,1)S(1)} %turn.1.refs_0_), channel_id=1, source_target_pairs={{0,384},{128,0},{256,128},{384,256},{1,385},{129,1},{257,129},{385... | collective-permute-start | bytes 1572872 | tf_op jit(solution)/shard_map/ppermute | solution.py:356
  106.7 21.3 %collective-permute-start.5 = (bf16[32,64,128]{2,1,0:T(8,128)(2,1)S(1)}, bf16[32,64,128]{2,1,0:T(8,128)(2,1)S(1)}, u32[]{:S(2)}, u32[]{:S(2)}) collective-permute-start(bf16[32,64,128]{2,1,0:T(8,128)(2,1)S(1)} %turn.1.refs_0_), channel_id=1, source_target_pairs={{0,256},{128,384},{256,0},{384,128},{1,257},{129,385},{257,1},{385... | collective-permute-start | bytes 1572872 | tf_op jit(solution)/shard_map/ppermute | solution.py:356
  110.2 21.7 %collective-permute-start.6 = (bf16[32,64,128]{2,1,0:T(8,128)(2,1)S(1)}, bf16[32,64,128]{2,1,0:T(8,128)(2,1)S(1)}, u32[]{:S(2)}, u32[]{:S(2)}) collective-permute-start(bf16[32,64,128]{2,1,0:T(8,128)(2,1)S(1)} %turn.1.refs_0_), channel_id=1, source_target_pairs={{0,4},{4,0},{1,5},{5,1},{2,6},{6,2},{3,7},{7,3},{8,12},{12,8},{9,1... | collective-permute-start | bytes 1572872 | tf_op jit(solution)/shard_map/ppermute | solution.py:356
  115.7 16.3 %collective-permute-start.7 = (bf16[32,64,128]{2,1,0:T(8,128)(2,1)S(1)}, bf16[32,64,128]{2,1,0:T(8,128)(2,1)S(1)}, u32[]{:S(2)}, u32[]{:S(2)}) collective-permute-start(bf16[32,64,128]{2,1,0:T(8,128)(2,1)S(1)} %collective-permute-done.3.refs_1_), channel_id=1, source_target_pairs={{0,4},{4,0},{1,5},{5,1},{2,6},{6,2},{3,7},{7,3},{8,12},{12,8},{9,1... | collective-permute-start | bytes 1572872 | tf_op jit(solution)/shard_map/ppermute | solution.py:356
  120.1 11.9 %collective-permute-start.8 = (bf16[32,64,128]{2,1,0:T(8,128)(2,1)S(1)}, bf16[32,64,128]{2,1,0:T(8,128)(2,1)}, u32[]{:S(2)}, u32[]{:S(2)}) collective-permute-start(bf16[32,64,128]{2,1,0:T(8,128)(2,1)S(1)} %collective-permute-done.4.refs_2_), channel_id=1, source_target_pairs={{0,4},{4,0},{1,5},{5,1},{2,6},{6,2},{3,7},{7,3},{8,12},{12,8},{9,1... | collective-permute-start | bytes 1572872 | tf_op jit(solution)/shard_map/ppermute | solution.py:356
  128.0 5.6 %collective-permute-start.9 = (bf16[32,64,128]{2,1,0:T(8,128)(2,1)S(1)}, bf16[32,64,128]{2,1,0:T(8,128)(2,1)}, u32[]{:S(2)}, u32[]{:S(2)}) collective-permute-start(bf16[32,64,128]{2,1,0:T(8,128)(2,1)S(1)} %collective-permute-done.5.refs_3_), channel_id=1, source_target_pairs={{0,4},{4,0},{1,5},{5,1},{2,6},{6,2},{3,7},{7,3},{8,12},{12,8},{9,1... | collective-permute-start | bytes 1572872 | tf_op jit(solution)/shard_map/ppermute | solution.py:356
  136.9 0.8 copy-start.2
  188.6 1.0 copy-start.3

commit v5 on v4

--- a/solution.py
+++ b/solution.py
@@ -229,6 +229,7 @@
     lax.fori_loop(0, ROWS // 256, step, 0, unroll=2)
 
 
+SLAB = pltpu.VMEM((32, 64, LANES), BF16)
 FIELD = pltpu.VMEM((NG, NG // 2, LANES), F32)
 VMEM = pl.BlockSpec(memory_space=pltpu.VMEM)
 SMEM = pl.BlockSpec(memory_space=pltpu.SMEM)
@@ -301,17 +302,16 @@
 def overlap(applied, phis):
     return pl.pallas_call(
         overlap_kernel,
-        out_shape=(
-            jax.ShapeDtypeStruct((64, 4, LANES), F32),
-            jax.ShapeDtypeStruct((32, 64, LANES), BF16),
-        ),
+        out_shape=jax.ShapeDtypeStruct((64, 4, LANES), F32),
+        scratch_shapes=[SLAB],
         name="overlap",
         compiler_params=LIMIT,
     )(applied, *phis)
 
 
-def project_kernel(overlaps, slab, *refs):
-    phis, out = refs[:8], refs[8]
+def project_kernel(overlaps, applied, *refs):
+    phis, (out, slab) = refs[:8], refs[8:]
+    turn_to(applied, slab)
     parts = jnp.concatenate(
         two_parts(jnp.concatenate([overlaps[:, n, :] for n in range(4)], axis=1)), axis=0
     )
@@ -326,13 +326,14 @@
     lax.fori_loop(0, 16, step, 0, unroll=4)
 
 
-def project(overlaps, slab, phis):
+def project(overlaps, applied, phis):
     return pl.pallas_call(
         project_kernel,
         out_shape=jax.ShapeDtypeStruct((32, 64, LANES), F32),
+        scratch_shapes=[SLAB],
         name="project",
         compiler_params=LIMIT,
-    )(overlaps, slab, *phis)
+    )(overlaps, applied, *phis)
 
 
 def settle_kernel(arrived, out):
@@ -382,8 +383,7 @@
     phi = exchange(spread(mine), ACROSS)
     phis = gathered(turned(phi))
     applied = exchange(applied, ACROSS)
-    partial, slab = overlap(applied, phis)
-    gradient = project(total_of(partial), slab, phis)
+    gradient = project(total_of(overlap(applied, phis)), applied, phis)
     return settle(exchange(gradient.reshape(8, 256, LANES), HELD))
 
 

time: 219 us -> 218 us (level)
  no operation moved by 1% of the time
where the time goes in v5:
time: 218 us; the launch traced here: 217 us
  blocking collectives  76.1 us (35%)
  starting transfers between devices  69.6 us (32%)
  Pallas kernels  36.2 us (17%)
  waiting for transfers between devices  33.3 us (15%)
    all_to_all x3, blocking collectives, exchange(): return lax.all_to_all(value, axes, split_axis=0, concat_axis=0, tiled=True)  76.1 us
    all_to_all x2, starting transfers between devices, exchange(): return lax.all_to_all(value, axes, split_axis=0, concat_axis=0, tiled=True)  33.3 us
    ppermute x7, starting transfers between devices, shifted(): lax.ppermute(value, axis, [(n, (n + distance) % size) for n in range(size)])  26.1 us
    ppermute x3, waiting for transfers between devices, partner(): return lax.ppermute(value, axis, pairs)  26 us
    pallas_call x2, Pallas kernels, solve(): pl.pallas_call(solve_kernel, out_shape=jax.ShapeDtypeStruct((ROWS, LANES)...  15.1 us
    ppermute x3, starting transfers between devices, partner(): return lax.ppermute(value, axis, pairs)  10.2 us
    pallas_call x1, Pallas kernels, solve_last(): pl.pallas_call(last_kernel, out_shape=jax.ShapeDtypeStruct((64, 32, LANES...  8.9 us
    ppermute x7, waiting for transfers between devices, shifted(): lax.ppermute(value, axis, [(n, (n + distance) % size) for n in range(size)])  7.29 us
  transfers between devices with their start and end apart: 12, of which 4 were waited for; matrix products, arithmetic and copies ran while one was open for 0% of the time, Pallas kernels for 12%

profile of v5, /device:TPU:1, one launch (start us, length us, event | category | flops | bytes accessed | tf_op | source)
XLA Modules:
  0.0 216.8 jit_solution(9915845125127062291)
XLA Ops:
  1.2 1.6 compact.1.own.mine
  3.8 19.1 %all-to-all-start.1 = ((bf16[64,32,128]{2,1,0:T(8,128)(2,1)}), bf16[64,32,128]{2,1,0:T(8,128)(2,1)S(1)}, u32[]{:S(2)}, u32[]{:S(2)}) async-start(bf16[64,32,128]{2,1,0:T(8,128)(2,1)} %spread.1), calls=%async_computation.1 | async-start | bytes 1048576 | tf_op jit(solution)/shard_map/all_to_all | solution.py:274
  23.0 3.0 %collective-permute-start.1 = (bf16[2048,128]{1,0:T(8,128)(2,1)S(1)}, bf16[2048,128]{1,0:T(8,128)(2,1)S(1)}, u32[]{:S(2)}, u32[]{:S(2)}) collective-permute-start(bf16[2048,128]{1,0:T(8,128)(2,1)S(1)} %compact.1.own.mine), channel_id=1, source_target_pairs={{0,4},{4,0},{8,12},{12,8},{16,20},{20,16},{24,28},{28,24},{32,36},... | collective-permute-start | bytes 1572872 | tf_op jit(solution)/shard_map/ppermute | solution.py:32
  26.0 3.2 %collective-permute-start.2 = (bf16[2048,128]{1,0:T(8,128)(2,1)S(1)}, bf16[2048,128]{1,0:T(8,128)(2,1)S(1)}, u32[]{:S(2)}, u32[]{:S(2)}) collective-permute-start(bf16[2048,128]{1,0:T(8,128)(2,1)S(1)} %compact.1.own.mine), channel_id=1, source_target_pairs={{0,8},{4,12},{8,0},{12,4},{16,24},{20,28},{24,16},{28,20},{32,40},... | collective-permute-start | bytes 1572872 | tf_op jit(solution)/shard_map/ppermute | solution.py:32
  29.2 4.0 %collective-permute-start = (bf16[2048,128]{1,0:T(8,128)(2,1)S(1)}, bf16[2048,128]{1,0:T(8,128)(2,1)S(1)}, u32[]{:S(2)}, u32[]{:S(2)}) collective-permute-start(bf16[2048,128]{1,0:T(8,128)(2,1)S(1)} %compact.1.own.mine), channel_id=1, source_target_pairs={{0,16},{4,20},{8,24},{12,28},{16,0},{20,4},{24,8},{28,12},{32,48},... | collective-permute-start | bytes 1572872 | tf_op jit(solution)/shard_map/ppermute | solution.py:32
  33.2 2.2 %inverse.1 = f32[32,64,128]{2,1,0:T(8,128)S(1)} custom-call(), custom_call_target="tpu_custom_call" | custom-call | tf_op jit(solution)/shard_map/inverse/pallas_call | solution.py:90
  35.4 7.5 %solve.2.first = bf16[2048,128]{1,0:T(8,128)(2,1)S(1)} custom-call(bf16[2048,128]{1,0:T(8,128)(2,1)S(1)} %compact.1.own.mine, bf16[2048,128]{1,0:T(8,128)(2,1)S(1)} %collective-permute-done.1.other, bf16[256,128]{1,0:T(8,128)(2,1)S(1)} %copy-done.1, bf16[128,128]{1,0:T(8,128)(2,1)S(1)} %copy-done.2, bf16[64,192]{1,0:T(8,128)(2,1)S(1)} %copy-done.3, ...), custom_call_target="tpu_custom_call" | custom-call | tf_op jit(solution)/shard_map/solve/pallas_call | solution.py:239
  43.0 26.0 %collective-permute-done.2.other = bf16[2048,128]{1,0:T(8,128)(2,1)S(1)} collective-permute-done((bf16[2048,128]{1,0:T(8,128)(2,1)S(1)}, bf16[2048,128]{1,0:T(8,128)(2,1)S(1)}, u32[]{:S(2)}, u32[]{:S(2)}) %collective-permute-start.2) | collective-permute-done | bytes 524320 | tf_op jit(solution)/shard_map/ppermute | solution.py:32
  69.0 7.5 %solve.3.second = bf16[2048,128]{1,0:T(8,128)(2,1)S(1)} custom-call(bf16[2048,128]{1,0:T(8,128)(2,1)S(1)} %compact.1.own.mine, bf16[2048,128]{1,0:T(8,128)(2,1)S(1)} %collective-permute-done.2.other, bf16[256,128]{1,0:T(8,128)(2,1)S(1)} %copy-done.1, bf16[128,128]{1,0:T(8,128)(2,1)S(1)} %copy-done.2, bf16[64,192]{1,0:T(8,128)(2,1)S(1)} %copy-done.3, ...), custom_call_target="tpu_custom_call" | custom-call | tf_op jit(solution)/shard_map/solve/pallas_call | solution.py:239
  76.5 8.9 %last.1 = bf16[64,32,128]{2,1,0:T(8,128)(2,1)} custom-call(s32[1,3]{1,0:T(1,128)S(1)} %copy-done.5, bf16[2048,128]{1,0:T(8,128)(2,1)S(1)} %compact.1.own.mine, bf16[2048,128]{1,0:T(8,128)(2,1)S(1)} %collective-permute-done.other, bf16[256,128]{1,0:T(8,128)(2,1)S(1)} %copy-done.1, bf16[128,128]{1,0:T(8,128)(2,1)S(1)} %copy-done.2, ...), custom_call_target="tpu_custom_call" | custom-call | tf_op jit(solution)/shard_map/last/pallas_call | solution.py:249
  85.4 14.2 %all-to-all-start = ((bf16[64,32,128]{2,1,0:T(8,128)(2,1)}), bf16[64,32,128]{2,1,0:T(8,128)(2,1)S(1)}, u32[]{:S(2)}, u32[]{:S(2)}) async-start(bf16[64,32,128]{2,1,0:T(8,128)(2,1)} %last.1), calls=%async_computation | async-start | bytes 1048576 | tf_op jit(solution)/shard_map/all_to_all | solution.py:274
  99.8 3.2 %collective-permute-start.3 = (bf16[32,64,128]{2,1,0:T(8,128)(2,1)S(1)}, bf16[32,64,128]{2,1,0:T(8,128)(2,1)S(1)}, u32[]{:S(2)}, u32[]{:S(2)}) collective-permute-start(bf16[32,64,128]{2,1,0:T(8,128)(2,1)S(1)} %turn.1.refs_0_), channel_id=1, source_target_pairs={{0,128},{128,256},{256,384},{384,0},{1,129},{129,257},{257,385},{3... | collective-permute-start | bytes 1572872 | tf_op jit(solution)/shard_map/ppermute | solution.py:357
  103.1 3.4 %collective-permute-start.4 = (bf16[32,64,128]{2,1,0:T(8,128)(2,1)S(1)}, bf16[32,64,128]{2,1,0:T(8,128)(2,1)S(1)}, u32[]{:S(2)}, u32[]{:S(2)}) collective-permute-start(bf16[32,64,128]{2,1,0:T(8,128)(2,1)S(1)} %turn.1.refs_0_), channel_id=1, source_target_pairs={{0,384},{128,0},{256,128},{384,256},{1,385},{129,1},{257,129},{385... | collective-permute-start | bytes 1572872 | tf_op jit(solution)/shard_map/ppermute | solution.py:357
  106.4 3.5 %collective-permute-start.5 = (bf16[32,64,128]{2,1,0:T(8,128)(2,1)S(1)}, bf16[32,64,128]{2,1,0:T(8,128)(2,1)S(1)}, u32[]{:S(2)}, u32[]{:S(2)}) collective-permute-start(bf16[32,64,128]{2,1,0:T(8,128)(2,1)S(1)} %turn.1.refs_0_), channel_id=1, source_target_pairs={{0,256},{128,384},{256,0},{384,128},{1,257},{129,385},{257,1},{385... | collective-permute-start | bytes 1572872 | tf_op jit(solution)/shard_map/ppermute | solution.py:357
  110.0 4.0 %collective-permute-start.6 = (bf16[32,64,128]{2,1,0:T(8,128)(2,1)S(1)}, bf16[32,64,128]{2,1,0:T(8,128)(2,1)S(1)}, u32[]{:S(2)}, u32[]{:S(2)}) collective-permute-start(bf16[32,64,128]{2,1,0:T(8,128)(2,1)S(1)} %turn.1.refs_0_), channel_id=1, source_target_pairs={{0,4},{4,0},{1,5},{5,1},{2,6},{6,2},{3,7},{7,3},{8,12},{12,8},{9,1... | collective-permute-start | bytes 1572872 | tf_op jit(solution)/shard_map/ppermute | solution.py:357
  115.3 4.5 %collective-permute-start.7 = (bf16[32,64,128]{2,1,0:T(8,128)(2,1)S(1)}, bf16[32,64,128]{2,1,0:T(8,128)(2,1)}, u32[]{:S(2)}, u32[]{:S(2)}) collective-permute-start(bf16[32,64,128]{2,1,0:T(8,128)(2,1)S(1)} %collective-permute-done.3.refs_1_), channel_id=1, source_target_pairs={{0,4},{4,0},{1,5},{5,1},{2,6},{6,2},{3,7},{7,3},{8,12},{12,8},{9,1... | collective-permute-start | bytes 1572872 | tf_op jit(solution)/shard_map/ppermute | solution.py:357
  119.8 3.4 %collective-permute-start.8 = (bf16[32,64,128]{2,1,0:T(8,128)(2,1)S(1)}, bf16[32,64,128]{2,1,0:T(8,128)(2,1)}, u32[]{:S(2)}, u32[]{:S(2)}) collective-permute-start(bf16[32,64,128]{2,1,0:T(8,128)(2,1)S(1)} %collective-permute-done.4.refs_2_), channel_id=1, source_target_pairs={{0,4},{4,0},{1,5},{5,1},{2,6},{6,2},{3,7},{7,3},{8,12},{12,8},{9,1... | collective-permute-start | bytes 1572872 | tf_op jit(solution)/shard_map/ppermute | solution.py:357
  123.2 4.4 %collective-permute-done.5.refs_3_ = bf16[32,64,128]{2,1,0:T(8,128)(2,1)S(1)} collective-permute-done((bf16[32,64,128]{2,1,0:T(8,128)(2,1)S(1)}, bf16[32,64,128]{2,1,0:T(8,128)(2,1)S(1)}, u32[]{:S(2)}, u32[]{:S(2)}) %collective-permute-start.5) | collective-permute-done | bytes 524320 | tf_op jit(solution)/shard_map/ppermute | solution.py:357
  127.6 4.0 %collective-permute-start.9 = (bf16[32,64,128]{2,1,0:T(8,128)(2,1)S(1)}, bf16[32,64,128]{2,1,0:T(8,128)(2,1)}, u32[]{:S(2)}, u32[]{:S(2)}) collective-permute-start(bf16[32,64,128]{2,1,0:T(8,128)(2,1)S(1)} %collective-permute-done.5.refs_3_), channel_id=1, source_target_pairs={{0,4},{4,0},{1,5},{5,1},{2,6},{6,2},{3,7},{7,3},{8,12},{12,8},{9,1... | collective-permute-start | bytes 1572872 | tf_op jit(solution)/shard_map/ppermute | solution.py:357
  133.3 3.4 %overlap.1 = f32[64,4,128]{2,1,0:T(4,128)S(1)} custom-call(bf16[64,32,128]{2,1,0:T(8,128)(2,1)S(1)} %all-to-all-done.applied, bf16[32,64,128]{2,1,0:T(8,128)(2,1)S(1)} %turn.1.refs_0_, bf16[32,64,128]{2,1,0:T(8,128)(2,1)S(1)} %collective-permute-done.3.refs_1_, bf16[32,64,128]{2,1,0:T(8,128)(2,1)S(1)} %collective-permute-done.4.refs_2_, ...), custom_call_target="tpu_custom_call" | custom-call | tf_op jit(solution)/shard_map/overlap/pallas_call | solution.py:303
  136.7 29.5 %all_to_all.25 = f32[64,4,128]{2,1,0:T(4,128)S(1)} all-to-all(f32[64,4,128]{2,1,0:T(4,128)S(1)} %overlap.1), channel_id=1, replica_groups=mesh['band_0'=4,'band_1'=16,'band_2'=2,'pair'=4] {'band_1','pair'}, dimensions={0} | all-to-all | bytes 262144 | tf_op jit(solution)/shard_map/all_to_all | solution.py:274
  166.3 21.3 %all_to_all.26.overlaps = f32[64,4,128]{2,1,0:T(4,128)S(1)} all-to-all(f32[64,4,128]{2,1,0:T(4,128)S(1)} %broadcast_in_dim.3), channel_id=1, replica_groups=mesh['band_0'=4,'band_1'=16,'band_2'=2,'pair'=4] {'band_1','pair'}, dimensions={0} | all-to-all | bytes 262144 | tf_op jit(solution)/shard_map/all_to_all | solution.py:274
  187.6 2.8 %project.1 = f32[32,64,128]{2,1,0:T(8,128)S(1)} custom-call(f32[64,4,128]{2,1,0:T(4,128)S(1)} %all_to_all.26.overlaps, bf16[64,32,128]{2,1,0:T(8,128)(2,1)S(1)} %all-to-all-done.applied, bf16[32,64,128]{2,1,0:T(8,128)(2,1)S(1)} %turn.1.refs_0_, bf16[32,64,128]{2,1,0:T(8,128)(2,1)S(1)} %collective-permute-done.3.refs_1_, ...), custom_call_target="tpu_custom_call" | custom-call | tf_op jit(solution)/shard_map/project/pallas_call | solution.py:330
  190.4 25.3 %all_to_all.27.arrived = f32[8,256,128]{2,1,0:T(8,128)S(1)} all-to-all(f32[8,256,128]{2,1,0:T(8,128)S(1)} %bitcast.2), channel_id=1, replica_groups=mesh['band_0'=4,'band_1'=16,'band_2'=2,'pair'=4] {'band_0','band_2'}, dimensions={0} | all-to-all | bytes 2097152 | tf_op jit(solution)/shard_map/all_to_all | solution.py:274
  (27 shorter events, 6.5 us)
Async XLA Ops:
  0.0 1.2 copy-start
  3.8 81.6 %all-to-all-start.1 = ((bf16[64,32,128]{2,1,0:T(8,128)(2,1)}), bf16[64,32,128]{2,1,0:T(8,128)(2,1)S(1)}, u32[]{:S(2)}, u32[]{:S(2)}) async-start(bf16[64,32,128]{2,1,0:T(8,128)(2,1)} %spread.1), calls=%async_computation.1 | async-start | bytes 1048576 | tf_op jit(solution)/shard_map/all_to_all | solution.py:274
  22.9 12.5 %copy-start.1 = (bf16[256,128]{1,0:T(8,128)(2,1)S(1)}, bf16[256,128]{1,0:T(8,128)(2,1)}, u32[]{:S(2)}) copy-start(bf16[256,128]{1,0:T(8,128)(2,1)} %constant.10.clone.z_main) | copy-start | bytes 196612
  22.9 12.5 %copy-start.2 = (bf16[128,128]{1,0:T(8,128)(2,1)S(1)}, bf16[128,128]{1,0:T(8,128)(2,1)}, u32[]{:S(2)}) copy-start(bf16[128,128]{1,0:T(8,128)(2,1)} %constant.11.clone.z_low) | copy-start | bytes 98308
  23.0 12.5 %copy-start.3 = (bf16[64,192]{1,0:T(8,128)(2,1)S(1)}, bf16[64,192]{1,0:T(8,128)(2,1)}, u32[]{:S(2)}) copy-start(bf16[64,192]{1,0:T(8,128)(2,1)} %constant.12.clone.y_side) | copy-start | bytes 73732
  23.0 12.4 %copy-start.4 = (bf16[64,192]{1,0:T(8,128)(2,1)S(1)}, bf16[64,192]{1,0:T(8,128)(2,1)}, u32[]{:S(2)}) copy-start(bf16[64,192]{1,0:T(8,128)(2,1)} %constant.13.clone.x_side) | copy-start | bytes 73732
  23.0 12.4 %collective-permute-start.1 = (bf16[2048,128]{1,0:T(8,128)(2,1)S(1)}, bf16[2048,128]{1,0:T(8,128)(2,1)S(1)}, u32[]{:S(2)}, u32[]{:S(2)}) collective-permute-start(bf16[2048,128]{1,0:T(8,128)(2,1)S(1)} %compact.1.own.mine), channel_id=1, source_target_pairs={{0,4},{4,0},{8,12},{12,8},{16,20},{20,16},{24,28},{28,24},{32,36},... | collective-permute-start | bytes 1572872 | tf_op jit(solution)/shard_map/ppermute | solution.py:32
  26.0 43.0 %collective-permute-start.2 = (bf16[2048,128]{1,0:T(8,128)(2,1)S(1)}, bf16[2048,128]{1,0:T(8,128)(2,1)S(1)}, u32[]{:S(2)}, u32[]{:S(2)}) collective-permute-start(bf16[2048,128]{1,0:T(8,128)(2,1)S(1)} %compact.1.own.mine), channel_id=1, source_target_pairs={{0,8},{4,12},{8,0},{12,4},{16,24},{20,28},{24,16},{28,20},{32,40},... | collective-permute-start | bytes 1572872 | tf_op jit(solution)/shard_map/ppermute | solution.py:32
  29.2 47.3 %collective-permute-start = (bf16[2048,128]{1,0:T(8,128)(2,1)S(1)}, bf16[2048,128]{1,0:T(8,128)(2,1)S(1)}, u32[]{:S(2)}, u32[]{:S(2)}) collective-permute-start(bf16[2048,128]{1,0:T(8,128)(2,1)S(1)} %compact.1.own.mine), channel_id=1, source_target_pairs={{0,16},{4,20},{8,24},{12,28},{16,0},{20,4},{24,8},{28,12},{32,48},... | collective-permute-start | bytes 1572872 | tf_op jit(solution)/shard_map/ppermute | solution.py:32
  43.0 33.5 %copy-start.5 = (s32[1,3]{1,0:T(1,128)S(1)}, s32[1,3]{1,0:T(1,128)}, u32[]{:S(2)}) copy-start(s32[1,3]{1,0:T(1,128)} %partners.1) | copy-start | bytes 40
  85.4 46.2 %all-to-all-start = ((bf16[64,32,128]{2,1,0:T(8,128)(2,1)}), bf16[64,32,128]{2,1,0:T(8,128)(2,1)S(1)}, u32[]{:S(2)}, u32[]{:S(2)}) async-start(bf16[64,32,128]{2,1,0:T(8,128)(2,1)} %last.1), calls=%async_computation | async-start | bytes 1048576 | tf_op jit(solution)/shard_map/all_to_all | solution.py:274
  99.8 15.4 %collective-permute-start.3 = (bf16[32,64,128]{2,1,0:T(8,128)(2,1)S(1)}, bf16[32,64,128]{2,1,0:T(8,128)(2,1)S(1)}, u32[]{:S(2)}, u32[]{:S(2)}) collective-permute-start(bf16[32,64,128]{2,1,0:T(8,128)(2,1)S(1)} %turn.1.refs_0_), channel_id=1, source_target_pairs={{0,128},{128,256},{256,384},{384,0},{1,129},{129,257},{257,385},{3... | collective-permute-start | bytes 1572872 | tf_op jit(solution)/shard_map/ppermute | solution.py:357
  103.1 16.8 %collective-permute-start.4 = (bf16[32,64,128]{2,1,0:T(8,128)(2,1)S(1)}, bf16[32,64,128]{2,1,0:T(8,128)(2,1)S(1)}, u32[]{:S(2)}, u32[]{:S(2)}) collective-permute-start(bf16[32,64,128]{2,1,0:T(8,128)(2,1)S(1)} %turn.1.refs_0_), channel_id=1, source_target_pairs={{0,384},{128,0},{256,128},{384,256},{1,385},{129,1},{257,129},{385... | collective-permute-start | bytes 1572872 | tf_op jit(solution)/shard_map/ppermute | solution.py:357
  106.4 21.2 %collective-permute-start.5 = (bf16[32,64,128]{2,1,0:T(8,128)(2,1)S(1)}, bf16[32,64,128]{2,1,0:T(8,128)(2,1)S(1)}, u32[]{:S(2)}, u32[]{:S(2)}) collective-permute-start(bf16[32,64,128]{2,1,0:T(8,128)(2,1)S(1)} %turn.1.refs_0_), channel_id=1, source_target_pairs={{0,256},{128,384},{256,0},{384,128},{1,257},{129,385},{257,1},{385... | collective-permute-start | bytes 1572872 | tf_op jit(solution)/shard_map/ppermute | solution.py:357
  110.0 21.7 %collective-permute-start.6 = (bf16[32,64,128]{2,1,0:T(8,128)(2,1)S(1)}, bf16[32,64,128]{2,1,0:T(8,128)(2,1)S(1)}, u32[]{:S(2)}, u32[]{:S(2)}) collective-permute-start(bf16[32,64,128]{2,1,0:T(8,128)(2,1)S(1)} %turn.1.refs_0_), channel_id=1, source_target_pairs={{0,4},{4,0},{1,5},{5,1},{2,6},{6,2},{3,7},{7,3},{8,12},{12,8},{9,1... | collective-permute-start | bytes 1572872 | tf_op jit(solution)/shard_map/ppermute | solution.py:357
  115.3 16.4 %collective-permute-start.7 = (bf16[32,64,128]{2,1,0:T(8,128)(2,1)S(1)}, bf16[32,64,128]{2,1,0:T(8,128)(2,1)}, u32[]{:S(2)}, u32[]{:S(2)}) collective-permute-start(bf16[32,64,128]{2,1,0:T(8,128)(2,1)S(1)} %collective-permute-done.3.refs_1_), channel_id=1, source_target_pairs={{0,4},{4,0},{1,5},{5,1},{2,6},{6,2},{3,7},{7,3},{8,12},{12,8},{9,1... | collective-permute-start | bytes 1572872 | tf_op jit(solution)/shard_map/ppermute | solution.py:357
  119.8 11.9 %collective-permute-start.8 = (bf16[32,64,128]{2,1,0:T(8,128)(2,1)S(1)}, bf16[32,64,128]{2,1,0:T(8,128)(2,1)}, u32[]{:S(2)}, u32[]{:S(2)}) collective-permute-start(bf16[32,64,128]{2,1,0:T(8,128)(2,1)S(1)} %collective-permute-done.4.refs_2_), channel_id=1, source_target_pairs={{0,4},{4,0},{1,5},{5,1},{2,6},{6,2},{3,7},{7,3},{8,12},{12,8},{9,1... | collective-permute-start | bytes 1572872 | tf_op jit(solution)/shard_map/ppermute | solution.py:357
  127.6 5.7 %collective-permute-start.9 = (bf16[32,64,128]{2,1,0:T(8,128)(2,1)S(1)}, bf16[32,64,128]{2,1,0:T(8,128)(2,1)}, u32[]{:S(2)}, u32[]{:S(2)}) collective-permute-start(bf16[32,64,128]{2,1,0:T(8,128)(2,1)S(1)} %collective-permute-done.5.refs_3_), channel_id=1, source_target_pairs={{0,4},{4,0},{1,5},{5,1},{2,6},{6,2},{3,7},{7,3},{8,12},{12,8},{9,1... | collective-permute-start | bytes 1572872 | tf_op jit(solution)/shard_map/ppermute | solution.py:357

commit v6 on v5

--- a/solution.py
+++ b/solution.py
@@ -283,7 +283,7 @@
 
 
 def overlap_kernel(applied, *refs):
-    phis, (out, slab) = refs[:8], refs[8:]
+    phis, before, (out, slab) = refs[:4], refs[4:-2], refs[-2:]
     turn_to(applied, slab)
 
     def step(n, total):
@@ -294,19 +294,21 @@
             preferred_element_type=F32,
         )
 
-    total = lax.fori_loop(0, 16, step, jnp.zeros((64, 512), F32), unroll=4) * (1.0 / NG3)
-    for n in range(4):
-        out[:, n, :] = total[:, LANES * n : LANES * (n + 1)]
-
-
-def overlap(applied, phis):
+    total = lax.fori_loop(0, 16, step, jnp.zeros((64, 256), F32), unroll=4) * (1.0 / NG3)
+    for ref in before:
+        out[:, 0:2, :] = ref[...]
+    for n in range(2):
+        out[:, 2 * len(before) + n, :] = total[:, LANES * n : LANES * (n + 1)]
+
+
+def overlap(applied, phis, *before):
     return pl.pallas_call(
         overlap_kernel,
-        out_shape=jax.ShapeDtypeStruct((64, 4, LANES), F32),
+        out_shape=jax.ShapeDtypeStruct((64, 2 + 2 * len(before), LANES), F32),
         scratch_shapes=[SLAB],
         name="overlap",
         compiler_params=LIMIT,
-    )(applied, *phis)
+    )(applied, *phis, *before)
 
 
 def project_kernel(overlaps, applied, *refs):
@@ -359,7 +361,7 @@
 
 def gathered(slab):
     slabs = [slab]
-    for distance in (1, 3, 2):
+    for distance in (2, 1, 3):
         slabs.append(shifted(slab, "band_0", distance))
     return slabs + [shifted(value, "band_2", 1) for value in slabs]
 
@@ -383,7 +385,8 @@
     phi = exchange(spread(mine), ACROSS)
     phis = gathered(turned(phi))
     applied = exchange(applied, ACROSS)
-    gradient = project(total_of(overlap(applied, phis)), applied, phis)
+    half = overlap(applied, phis[:4])
+    gradient = project(total_of(overlap(applied, phis[4:], half)), applied, phis)
     return settle(exchange(gradient.reshape(8, 256, LANES), HELD))
 
 

time: 218 us -> 215 us (0.986)
  blocking collectives: 76.1 us -> 73.3 us
    all_to_all x3, blocking collectives: 76.1 us -> 73.3 us  [exchange(): return lax.all_to_all(value, axes, split_axis=0, concat_axis=0, tiled=True)]
  transfers between devices with their start and end apart: 12 -> 12, of which waited for: 4 -> 4; matrix products, arithmetic and copies ran while one was open for 0% -> 0% of each run, Pallas kernels for 12% -> 13%
where the time goes in v6:
time: 215 us
  blocking collectives  73.3 us (34%)
  starting transfers between devices  69 us (32%)
  Pallas kernels  36.9 us (17%)
  waiting for transfers between devices  33.9 us (16%)
    all_to_all x3, blocking collectives, exchange(): return lax.all_to_all(value, axes, split_axis=0, concat_axis=0, tiled=True)  73.3 us
    all_to_all x2, starting transfers between devices, exchange(): return lax.all_to_all(value, axes, split_axis=0, concat_axis=0, tiled=True)  33.3 us
    ppermute x3, waiting for transfers between devices, partner(): return lax.ppermute(value, axis, pairs)  26 us
    ppermute x7, starting transfers between devices, shifted(): lax.ppermute(value, axis, [(n, (n + distance) % size) for n in range(size)])  25.5 us
    pallas_call x2, Pallas kernels, solve(): pl.pallas_call(solve_kernel, out_shape=jax.ShapeDtypeStruct((ROWS, LANES)...  15.1 us
    ppermute x3, starting transfers between devices, partner(): return lax.ppermute(value, axis, pairs)  10.2 us
    pallas_call x1, Pallas kernels, solve_last(): pl.pallas_call(last_kernel, out_shape=jax.ShapeDtypeStruct((64, 32, LANES...  8.9 us
    ppermute x7, waiting for transfers between devices, shifted(): lax.ppermute(value, axis, [(n, (n + distance) % size) for n in range(size)])  7.91 us
  transfers between devices with their start and end apart: 12, of which 4 were waited for; matrix products, arithmetic and copies ran while one was open for 0% of the time, Pallas kernels for 13%

profile of v6, /device:TPU:1, one launch (start us, length us, event | category | flops | bytes accessed | tf_op | source)
XLA Modules:
  0.0 214.7 jit_solution(9452070601304399608)
XLA Ops:
  1.2 1.6 compact.1.own.mine
  3.8 19.1 %all-to-all-start.1 = ((bf16[64,32,128]{2,1,0:T(8,128)(2,1)}), bf16[64,32,128]{2,1,0:T(8,128)(2,1)S(1)}, u32[]{:S(2)}, u32[]{:S(2)}) async-start(bf16[64,32,128]{2,1,0:T(8,128)(2,1)} %spread.1), calls=%async_computation.1 | async-start | bytes 1048576 | tf_op jit(solution)/shard_map/all_to_all | solution.py:274
  23.0 3.0 %collective-permute-start.1 = (bf16[2048,128]{1,0:T(8,128)(2,1)S(1)}, bf16[2048,128]{1,0:T(8,128)(2,1)S(1)}, u32[]{:S(2)}, u32[]{:S(2)}) collective-permute-start(bf16[2048,128]{1,0:T(8,128)(2,1)S(1)} %compact.1.own.mine), channel_id=1, source_target_pairs={{0,4},{4,0},{8,12},{12,8},{16,20},{20,16},{24,28},{28,24},{32,36},... | collective-permute-start | bytes 1572872 | tf_op jit(solution)/shard_map/ppermute | solution.py:32
  26.0 3.2 %collective-permute-start.2 = (bf16[2048,128]{1,0:T(8,128)(2,1)S(1)}, bf16[2048,128]{1,0:T(8,128)(2,1)S(1)}, u32[]{:S(2)}, u32[]{:S(2)}) collective-permute-start(bf16[2048,128]{1,0:T(8,128)(2,1)S(1)} %compact.1.own.mine), channel_id=1, source_target_pairs={{0,8},{4,12},{8,0},{12,4},{16,24},{20,28},{24,16},{28,20},{32,40},... | collective-permute-start | bytes 1572872 | tf_op jit(solution)/shard_map/ppermute | solution.py:32
  29.2 4.0 %collective-permute-start = (bf16[2048,128]{1,0:T(8,128)(2,1)S(1)}, bf16[2048,128]{1,0:T(8,128)(2,1)S(1)}, u32[]{:S(2)}, u32[]{:S(2)}) collective-permute-start(bf16[2048,128]{1,0:T(8,128)(2,1)S(1)} %compact.1.own.mine), channel_id=1, source_target_pairs={{0,16},{4,20},{8,24},{12,28},{16,0},{20,4},{24,8},{28,12},{32,48},... | collective-permute-start | bytes 1572872 | tf_op jit(solution)/shard_map/ppermute | solution.py:32
  33.2 2.2 %inverse.1 = f32[32,64,128]{2,1,0:T(8,128)S(1)} custom-call(), custom_call_target="tpu_custom_call" | custom-call | tf_op jit(solution)/shard_map/inverse/pallas_call | solution.py:90
  35.4 7.5 %solve.2.first = bf16[2048,128]{1,0:T(8,128)(2,1)S(1)} custom-call(bf16[2048,128]{1,0:T(8,128)(2,1)S(1)} %compact.1.own.mine, bf16[2048,128]{1,0:T(8,128)(2,1)S(1)} %collective-permute-done.1.other, bf16[256,128]{1,0:T(8,128)(2,1)S(1)} %copy-done.1, bf16[128,128]{1,0:T(8,128)(2,1)S(1)} %copy-done.2, bf16[64,192]{1,0:T(8,128)(2,1)S(1)} %copy-done.3, ...), custom_call_target="tpu_custom_call" | custom-call | tf_op jit(solution)/shard_map/solve/pallas_call | solution.py:239
  43.0 26.0 %collective-permute-done.2.other = bf16[2048,128]{1,0:T(8,128)(2,1)S(1)} collective-permute-done((bf16[2048,128]{1,0:T(8,128)(2,1)S(1)}, bf16[2048,128]{1,0:T(8,128)(2,1)S(1)}, u32[]{:S(2)}, u32[]{:S(2)}) %collective-permute-start.2) | collective-permute-done | bytes 524320 | tf_op jit(solution)/shard_map/ppermute | solution.py:32
  69.0 7.5 %solve.3.second = bf16[2048,128]{1,0:T(8,128)(2,1)S(1)} custom-call(bf16[2048,128]{1,0:T(8,128)(2,1)S(1)} %compact.1.own.mine, bf16[2048,128]{1,0:T(8,128)(2,1)S(1)} %collective-permute-done.2.other, bf16[256,128]{1,0:T(8,128)(2,1)S(1)} %copy-done.1, bf16[128,128]{1,0:T(8,128)(2,1)S(1)} %copy-done.2, bf16[64,192]{1,0:T(8,128)(2,1)S(1)} %copy-done.3, ...), custom_call_target="tpu_custom_call" | custom-call | tf_op jit(solution)/shard_map/solve/pallas_call | solution.py:239
  76.5 8.9 %last.1 = bf16[64,32,128]{2,1,0:T(8,128)(2,1)} custom-call(s32[1,3]{1,0:T(1,128)S(1)} %copy-done.5, bf16[2048,128]{1,0:T(8,128)(2,1)S(1)} %compact.1.own.mine, bf16[2048,128]{1,0:T(8,128)(2,1)S(1)} %collective-permute-done.other, bf16[256,128]{1,0:T(8,128)(2,1)S(1)} %copy-done.1, bf16[128,128]{1,0:T(8,128)(2,1)S(1)} %copy-done.2, ...), custom_call_target="tpu_custom_call" | custom-call | tf_op jit(solution)/shard_map/last/pallas_call | solution.py:249
  85.4 14.2 %all-to-all-start = ((bf16[64,32,128]{2,1,0:T(8,128)(2,1)}), bf16[64,32,128]{2,1,0:T(8,128)(2,1)S(1)}, u32[]{:S(2)}, u32[]{:S(2)}) async-start(bf16[64,32,128]{2,1,0:T(8,128)(2,1)} %last.1), calls=%async_computation | async-start | bytes 1048576 | tf_op jit(solution)/shard_map/all_to_all | solution.py:274
  99.8 4.8 %collective-permute-start.4 = (bf16[32,64,128]{2,1,0:T(8,128)(2,1)S(1)}, bf16[32,64,128]{2,1,0:T(8,128)(2,1)S(1)}, u32[]{:S(2)}, u32[]{:S(2)}) collective-permute-start(bf16[32,64,128]{2,1,0:T(8,128)(2,1)S(1)} %turn.1.refs_0_), channel_id=1, source_target_pairs={{0,256},{128,384},{256,0},{384,128},{1,257},{129,385},{257,1},{385... | collective-permute-start | bytes 1572872 | tf_op jit(solution)/shard_map/ppermute | solution.py:359
  104.7 2.3 %collective-permute-start.6 = (bf16[32,64,128]{2,1,0:T(8,128)(2,1)S(1)}, bf16[32,64,128]{2,1,0:T(8,128)(2,1)S(1)}, u32[]{:S(2)}, u32[]{:S(2)}) collective-permute-start(bf16[32,64,128]{2,1,0:T(8,128)(2,1)S(1)} %turn.1.refs_0_), channel_id=1, source_target_pairs={{0,128},{128,256},{256,384},{384,0},{1,129},{129,257},{257,385},{3... | collective-permute-start | bytes 1572872 | tf_op jit(solution)/shard_map/ppermute | solution.py:359
  107.0 4.2 %collective-permute-start.8 = (bf16[32,64,128]{2,1,0:T(8,128)(2,1)S(1)}, bf16[32,64,128]{2,1,0:T(8,128)(2,1)S(1)}, u32[]{:S(2)}, u32[]{:S(2)}) collective-permute-start(bf16[32,64,128]{2,1,0:T(8,128)(2,1)S(1)} %turn.1.refs_0_), channel_id=1, source_target_pairs={{0,384},{128,0},{256,128},{384,256},{1,385},{129,1},{257,129},{385... | collective-permute-start | bytes 1572872 | tf_op jit(solution)/shard_map/ppermute | solution.py:359
  111.2 4.0 %collective-permute-start.3 = (bf16[32,64,128]{2,1,0:T(8,128)(2,1)S(1)}, bf16[32,64,128]{2,1,0:T(8,128)(2,1)S(1)}, u32[]{:S(2)}, u32[]{:S(2)}) collective-permute-start(bf16[32,64,128]{2,1,0:T(8,128)(2,1)S(1)} %turn.1.refs_0_), channel_id=1, source_target_pairs={{0,4},{4,0},{1,5},{5,1},{2,6},{6,2},{3,7},{7,3},{8,12},{12,8},{9,1... | collective-permute-start | bytes 1572872 | tf_op jit(solution)/shard_map/ppermute | solution.py:359
  115.5 5.8 %collective-permute-start.5 = (bf16[32,64,128]{2,1,0:T(8,128)(2,1)S(1)}, bf16[32,64,128]{2,1,0:T(8,128)(2,1)}, u32[]{:S(2)}, u32[]{:S(2)}) collective-permute-start(bf16[32,64,128]{2,1,0:T(8,128)(2,1)S(1)} %collective-permute-done.4.refs_1_), channel_id=1, source_target_pairs={{0,4},{4,0},{1,5},{5,1},{2,6},{6,2},{3,7},{7,3},{8,12},{12,8},{9,1... | collective-permute-start | bytes 1572872 | tf_op jit(solution)/shard_map/ppermute | solution.py:359
  121.3 7.0 %collective-permute-done.6.refs_2_ = bf16[32,64,128]{2,1,0:T(8,128)(2,1)S(1)} collective-permute-done((bf16[32,64,128]{2,1,0:T(8,128)(2,1)S(1)}, bf16[32,64,128]{2,1,0:T(8,128)(2,1)S(1)}, u32[]{:S(2)}, u32[]{:S(2)}) %collective-permute-start.6) | collective-permute-done | bytes 524320 | tf_op jit(solution)/shard_map/ppermute | solution.py:359
  128.3 2.4 %collective-permute-start.7 = (bf16[32,64,128]{2,1,0:T(8,128)(2,1)S(1)}, bf16[32,64,128]{2,1,0:T(8,128)(2,1)}, u32[]{:S(2)}, u32[]{:S(2)}) collective-permute-start(bf16[32,64,128]{2,1,0:T(8,128)(2,1)S(1)} %collective-permute-done.6.refs_2_), channel_id=1, source_target_pairs={{0,4},{4,0},{1,5},{5,1},{2,6},{6,2},{3,7},{7,3},{8,12},{12,8},{9,1... | collective-permute-start | bytes 1572872 | tf_op jit(solution)/shard_map/ppermute | solution.py:359
  130.7 1.9 collective-permute-start.9
  134.7 2.7 %overlap.3 = f32[64,4,128]{2,1,0:T(4,128)S(1)} custom-call(bf16[64,32,128]{2,1,0:T(8,128)(2,1)S(1)} %all-to-all-done.applied, bf16[32,64,128]{2,1,0:T(8,128)(2,1)S(1)} %collective-permute-done.3.refs_0_.refs_4_, bf16[32,64,128]{2,1,0:T(8,128)(2,1)} %collective-permute-done.5.refs_1_.refs_5_, bf16[32,64,128]{2,1,0:T(8,128)(2,1)} %collective-permute-done.7.refs_2_.refs_6_, ...), custom_call_target="tpu_custom_call" | custom-call | tf_op jit(solution)/shard_map/overlap/pallas_call | solution.py:305
  137.4 29.9 %all_to_all.25 = f32[64,4,128]{2,1,0:T(4,128)S(1)} all-to-all(f32[64,4,128]{2,1,0:T(4,128)S(1)} %overlap.3), channel_id=1, replica_groups=mesh['band_0'=4,'band_1'=16,'band_2'=2,'pair'=4] {'band_1','pair'}, dimensions={0} | all-to-all | bytes 262144 | tf_op jit(solution)/shard_map/all_to_all | solution.py:274
  167.4 21.0 %all_to_all.26.overlaps = f32[64,4,128]{2,1,0:T(4,128)S(1)} all-to-all(f32[64,4,128]{2,1,0:T(4,128)S(1)} %broadcast_in_dim.3), channel_id=1, replica_groups=mesh['band_0'=4,'band_1'=16,'band_2'=2,'pair'=4] {'band_1','pair'}, dimensions={0} | all-to-all | bytes 262144 | tf_op jit(solution)/shard_map/all_to_all | solution.py:274
  188.4 2.8 %project.1 = f32[32,64,128]{2,1,0:T(8,128)S(1)} custom-call(f32[64,4,128]{2,1,0:T(4,128)S(1)} %all_to_all.26.overlaps, bf16[64,32,128]{2,1,0:T(8,128)(2,1)S(1)} %all-to-all-done.applied, bf16[32,64,128]{2,1,0:T(8,128)(2,1)S(1)} %turn.1.refs_0_, bf16[32,64,128]{2,1,0:T(8,128)(2,1)S(1)} %collective-permute-done.4.refs_1_, ...), custom_call_target="tpu_custom_call" | custom-call | tf_op jit(solution)/shard_map/project/pallas_call | solution.py:332
  191.2 22.4 %all_to_all.27.arrived = f32[8,256,128]{2,1,0:T(8,128)S(1)} all-to-all(f32[8,256,128]{2,1,0:T(8,128)S(1)} %bitcast.2), channel_id=1, replica_groups=mesh['band_0'=4,'band_1'=16,'band_2'=2,'pair'=4] {'band_0','band_2'}, dimensions={0} | all-to-all | bytes 2097152 | tf_op jit(solution)/shard_map/all_to_all | solution.py:274
  (28 shorter events, 5.8 us)
Async XLA Ops:
  0.0 1.2 copy-start
  3.8 81.6 %all-to-all-start.1 = ((bf16[64,32,128]{2,1,0:T(8,128)(2,1)}), bf16[64,32,128]{2,1,0:T(8,128)(2,1)S(1)}, u32[]{:S(2)}, u32[]{:S(2)}) async-start(bf16[64,32,128]{2,1,0:T(8,128)(2,1)} %spread.1), calls=%async_computation.1 | async-start | bytes 1048576 | tf_op jit(solution)/shard_map/all_to_all | solution.py:274
  22.9 12.5 %copy-start.1 = (bf16[256,128]{1,0:T(8,128)(2,1)S(1)}, bf16[256,128]{1,0:T(8,128)(2,1)}, u32[]{:S(2)}) copy-start(bf16[256,128]{1,0:T(8,128)(2,1)} %constant.10.clone.z_main) | copy-start | bytes 196612
  22.9 12.5 %copy-start.2 = (bf16[128,128]{1,0:T(8,128)(2,1)S(1)}, bf16[128,128]{1,0:T(8,128)(2,1)}, u32[]{:S(2)}) copy-start(bf16[128,128]{1,0:T(8,128)(2,1)} %constant.11.clone.z_low) | copy-start | bytes 98308
  23.0 12.5 %copy-start.3 = (bf16[64,192]{1,0:T(8,128)(2,1)S(1)}, bf16[64,192]{1,0:T(8,128)(2,1)}, u32[]{:S(2)}) copy-start(bf16[64,192]{1,0:T(8,128)(2,1)} %constant.12.clone.y_side) | copy-start | bytes 73732
  23.0 12.4 %copy-start.4 = (bf16[64,192]{1,0:T(8,128)(2,1)S(1)}, bf16[64,192]{1,0:T(8,128)(2,1)}, u32[]{:S(2)}) copy-start(bf16[64,192]{1,0:T(8,128)(2,1)} %constant.13.clone.x_side) | copy-start | bytes 73732
  23.0 12.4 %collective-permute-start.1 = (bf16[2048,128]{1,0:T(8,128)(2,1)S(1)}, bf16[2048,128]{1,0:T(8,128)(2,1)S(1)}, u32[]{:S(2)}, u32[]{:S(2)}) collective-permute-start(bf16[2048,128]{1,0:T(8,128)(2,1)S(1)} %compact.1.own.mine), channel_id=1, source_target_pairs={{0,4},{4,0},{8,12},{12,8},{16,20},{20,16},{24,28},{28,24},{32,36},... | collective-permute-start | bytes 1572872 | tf_op jit(solution)/shard_map/ppermute | solution.py:32
  26.0 43.0 %collective-permute-start.2 = (bf16[2048,128]{1,0:T(8,128)(2,1)S(1)}, bf16[2048,128]{1,0:T(8,128)(2,1)S(1)}, u32[]{:S(2)}, u32[]{:S(2)}) collective-permute-start(bf16[2048,128]{1,0:T(8,128)(2,1)S(1)} %compact.1.own.mine), channel_id=1, source_target_pairs={{0,8},{4,12},{8,0},{12,4},{16,24},{20,28},{24,16},{28,20},{32,40},... | collective-permute-start | bytes 1572872 | tf_op jit(solution)/shard_map/ppermute | solution.py:32
  29.2 47.3 %collective-permute-start = (bf16[2048,128]{1,0:T(8,128)(2,1)S(1)}, bf16[2048,128]{1,0:T(8,128)(2,1)S(1)}, u32[]{:S(2)}, u32[]{:S(2)}) collective-permute-start(bf16[2048,128]{1,0:T(8,128)(2,1)S(1)} %compact.1.own.mine), channel_id=1, source_target_pairs={{0,16},{4,20},{8,24},{12,28},{16,0},{20,4},{24,8},{28,12},{32,48},... | collective-permute-start | bytes 1572872 | tf_op jit(solution)/shard_map/ppermute | solution.py:32
  43.0 33.5 %copy-start.5 = (s32[1,3]{1,0:T(1,128)S(1)}, s32[1,3]{1,0:T(1,128)}, u32[]{:S(2)}) copy-start(s32[1,3]{1,0:T(1,128)} %partners.1) | copy-start | bytes 40
  85.4 47.2 %all-to-all-start = ((bf16[64,32,128]{2,1,0:T(8,128)(2,1)}), bf16[64,32,128]{2,1,0:T(8,128)(2,1)S(1)}, u32[]{:S(2)}, u32[]{:S(2)}) async-start(bf16[64,32,128]{2,1,0:T(8,128)(2,1)} %last.1), calls=%async_computation | async-start | bytes 1048576 | tf_op jit(solution)/shard_map/all_to_all | solution.py:274
  99.8 15.6 %collective-permute-start.4 = (bf16[32,64,128]{2,1,0:T(8,128)(2,1)S(1)}, bf16[32,64,128]{2,1,0:T(8,128)(2,1)S(1)}, u32[]{:S(2)}, u32[]{:S(2)}) collective-permute-start(bf16[32,64,128]{2,1,0:T(8,128)(2,1)S(1)} %turn.1.refs_0_), channel_id=1, source_target_pairs={{0,256},{128,384},{256,0},{384,128},{1,257},{129,385},{257,1},{385... | collective-permute-start | bytes 1572872 | tf_op jit(solution)/shard_map/ppermute | solution.py:359
  104.7 23.6 %collective-permute-start.6 = (bf16[32,64,128]{2,1,0:T(8,128)(2,1)S(1)}, bf16[32,64,128]{2,1,0:T(8,128)(2,1)S(1)}, u32[]{:S(2)}, u32[]{:S(2)}) collective-permute-start(bf16[32,64,128]{2,1,0:T(8,128)(2,1)S(1)} %turn.1.refs_0_), channel_id=1, source_target_pairs={{0,128},{128,256},{256,384},{384,0},{1,129},{129,257},{257,385},{3... | collective-permute-start | bytes 1572872 | tf_op jit(solution)/shard_map/ppermute | solution.py:359
  107.0 23.7 %collective-permute-start.8 = (bf16[32,64,128]{2,1,0:T(8,128)(2,1)S(1)}, bf16[32,64,128]{2,1,0:T(8,128)(2,1)S(1)}, u32[]{:S(2)}, u32[]{:S(2)}) collective-permute-start(bf16[32,64,128]{2,1,0:T(8,128)(2,1)S(1)} %turn.1.refs_0_), channel_id=1, source_target_pairs={{0,384},{128,0},{256,128},{384,256},{1,385},{129,1},{257,129},{385... | collective-permute-start | bytes 1572872 | tf_op jit(solution)/shard_map/ppermute | solution.py:359
  111.2 22.9 %collective-permute-start.3 = (bf16[32,64,128]{2,1,0:T(8,128)(2,1)S(1)}, bf16[32,64,128]{2,1,0:T(8,128)(2,1)S(1)}, u32[]{:S(2)}, u32[]{:S(2)}) collective-permute-start(bf16[32,64,128]{2,1,0:T(8,128)(2,1)S(1)} %turn.1.refs_0_), channel_id=1, source_target_pairs={{0,4},{4,0},{1,5},{5,1},{2,6},{6,2},{3,7},{7,3},{8,12},{12,8},{9,1... | collective-permute-start | bytes 1572872 | tf_op jit(solution)/shard_map/ppermute | solution.py:359
  115.5 18.6 %collective-permute-start.5 = (bf16[32,64,128]{2,1,0:T(8,128)(2,1)S(1)}, bf16[32,64,128]{2,1,0:T(8,128)(2,1)}, u32[]{:S(2)}, u32[]{:S(2)}) collective-permute-start(bf16[32,64,128]{2,1,0:T(8,128)(2,1)S(1)} %collective-permute-done.4.refs_1_), channel_id=1, source_target_pairs={{0,4},{4,0},{1,5},{5,1},{2,6},{6,2},{3,7},{7,3},{8,12},{12,8},{9,1... | collective-permute-start | bytes 1572872 | tf_op jit(solution)/shard_map/ppermute | solution.py:359
  128.3 5.7 %collective-permute-start.7 = (bf16[32,64,128]{2,1,0:T(8,128)(2,1)S(1)}, bf16[32,64,128]{2,1,0:T(8,128)(2,1)}, u32[]{:S(2)}, u32[]{:S(2)}) collective-permute-start(bf16[32,64,128]{2,1,0:T(8,128)(2,1)S(1)} %collective-permute-done.6.refs_2_), channel_id=1, source_target_pairs={{0,4},{4,0},{1,5},{5,1},{2,6},{6,2},{3,7},{7,3},{8,12},{12,8},{9,1... | collective-permute-start | bytes 1572872 | tf_op jit(solution)/shard_map/ppermute | solution.py:359
  130.7 3.9 %collective-permute-start.9 = (bf16[32,64,128]{2,1,0:T(8,128)(2,1)S(1)}, bf16[32,64,128]{2,1,0:T(8,128)(2,1)}, u32[]{:S(2)}, u32[]{:S(2)}) collective-permute-start(bf16[32,64,128]{2,1,0:T(8,128)(2,1)S(1)} %collective-permute-done.8.refs_3_), channel_id=1, source_target_pairs={{0,4},{4,0},{1,5},{5,1},{2,6},{6,2},{3,7},{7,3},{8,12},{12,8},{9,1... | collective-permute-start | bytes 1572872 | tf_op jit(solution)/shard_map/ppermute | solution.py:359
